TPU v7x, 32 devices: a whole 2x2x4 slice. The times are simulated.
32 devices in a mesh: row: 4 (over y, core), col: 8 (over z, x).
Axes of the slice: x: 2, y: 2, z: 4, core: 2. Of those that a mesh axis runs over, the one named last changes fastest.
Arguments:
- parent_front: float32 [8, 1024, 4, 2048], P(None, 'row', None, 'col'), may hold values from -6 to 6
- generators: bfloat16 [48, 256, 256], P('row'), may hold values from -1.5 to 1.5
- diagonal_blocks: bfloat16 [48, 256, 256], P('row'), may hold values from -6 to 6
- coupling: bfloat16 [2, 256, 256], replicated, may hold values from -0.375 to 0.375
- block_map: int32 [2, 24], replicated, may hold values from 0 to 31, as said below
- valid_rows: int32 [2, 24], replicated, may hold values from 128 to 256
Outputs:
- assembled: float32 [8, 1024, 4, 2048], P(None, 'row', None, 'col')
Inputs may be any that keep to these rules, and one draw needn't show every extreme that they name: `block_map`: for each child c and each s < 2, the child blocks s * 12 to (s + 1) * 12 - 1 map in increasing order to distinct parent blocks of the range s * 16 to (s + 1) * 16 - 1, and the parent blocks s * 16 + m * 4 of that range always receive one.
All inputs are finite; a program needn't handle non-finite values.
Results may differ from a plain program's by a relative error of at most 0.0028.
Values may be sent and summed in bfloat16 or wider, within the bound.
No kernel may reach another device: no remote copies, remote signals or barrier semaphores. Data moves between devices by JAX's collectives and lax.ppermute only.
A program may use at most 128 MiB of HBM per device.

v0:
```python
import jax
import jax.numpy as jnp
from jax import lax
from jax.sharding import PartitionSpec as P


def split_children(stacked, half_rows):
    grouped = stacked.reshape((half_rows, 2, -1) + stacked.shape[2:])
    grouped = jnp.swapaxes(grouped, 0, 1)
    return grouped.reshape((2, -1) + stacked.shape[2:])


def shards(parent_front, generators, diagonal_blocks, coupling, block_map, valid_rows):
    row_count = lax.axis_size("row")
    col_count = lax.axis_size("col")
    half_rows = row_count // 2
    row_index = lax.axis_index("row")
    col_index = lax.axis_index("col")
    own_child = row_index % 2
    own_group = row_index // 2
    group_blocks = generators.shape[0]
    block_size = generators.shape[1]
    rank_width = generators.shape[2]
    rows_local = parent_front.shape[0]
    cols_local = parent_front.shape[2]
    window = 2 * rows_local
    row_cap = window // row_count
    col_cap = window // col_count
    map_child = lax.dynamic_index_in_dim(block_map, own_child, 0, keepdims=False)
    count_child = lax.dynamic_index_in_dim(valid_rows, own_child, 0, keepdims=False)
    coupling_own = lax.dynamic_index_in_dim(coupling, own_child, 0, keepdims=False)
    group_start = own_group * group_blocks
    map_group = lax.dynamic_slice_in_dim(map_child, group_start, group_blocks)
    count_group = lax.dynamic_slice_in_dim(count_child, group_start, group_blocks)
    row_offsets = jnp.arange(block_size, dtype=jnp.int32)
    kept_mask = (row_offsets[None, :] < count_group[:, None]).astype(jnp.bfloat16)
    masked = generators * kept_mask[:, :, None]
    projected = jnp.einsum(
        "ixq,qr->ixr", masked, coupling_own, preferred_element_type=jnp.float32
    ).astype(jnp.bfloat16)
    diag_kept = diagonal_blocks * kept_mask[:, :, None] * kept_mask[:, None, :]
    window_pos = map_group - own_group * window
    slot_ids = jnp.arange(window, dtype=jnp.int32)
    window_place = (window_pos[None, :] == slot_ids[:, None]).astype(jnp.bfloat16)
    row_place = window_place.reshape(row_cap, row_count, group_blocks)
    row_send = jnp.einsum(
        "kri,ixq->rkxq", row_place, masked, preferred_element_type=jnp.float32
    ).astype(jnp.bfloat16)
    row_received = lax.all_to_all(row_send, "row", split_axis=0, concat_axis=0, tiled=True)
    row_received = split_children(row_received, half_rows)
    wanted = jnp.arange(col_cap, dtype=jnp.int32) * col_count + col_index
    column_pick = (window_pos[None, :] == wanted[:, None]).astype(jnp.bfloat16)
    col_send = jnp.einsum(
        "ki,izq->kzq", column_pick, projected, preferred_element_type=jnp.float32
    ).astype(jnp.bfloat16)
    diag_send = jnp.einsum(
        "ki,ixz->kxz", column_pick, diag_kept, preferred_element_type=jnp.float32
    ).astype(jnp.bfloat16)
    col_received, diag_received = (
        lax.all_gather(col_send, "row", axis=0, tiled=True),
        lax.all_gather(diag_send, "row", axis=0, tiled=True),
    )
    col_received = split_children(
        col_received.reshape(row_count, col_cap, block_size, rank_width), half_rows
    )
    diag_received = split_children(
        diag_received.reshape(row_count, col_cap, block_size, block_size), half_rows
    )
    row_parents = jnp.arange(rows_local, dtype=jnp.int32) * row_count + row_index
    col_parents = jnp.arange(cols_local, dtype=jnp.int32) * col_count + col_index
    on_diag = (row_parents[:, None] == col_parents[None, :]).astype(jnp.float32)
    running = parent_front
    for child_index in range(2):
        child_tile = jnp.einsum(
            "axq,bzq->axbz",
            row_received[child_index],
            col_received[child_index],
            preferred_element_type=jnp.float32,
        )
        diag_part = diag_received[child_index].astype(jnp.float32).transpose(1, 0, 2)
        child_tile = child_tile + on_diag[:, None, :, None] * diag_part[None]
        rounded = lax.optimization_barrier(child_tile.astype(jnp.bfloat16))
        running = running + rounded.astype(jnp.float32)
    return running


def solution(mesh):
    in_specs = (
        P(None, "row", None, "col"),
        P("row", None, None),
        P("row", None, None),
        P(),
        P(),
        P(),
    )
    out_specs = P(None, "row", None, "col")
    return jax.shard_map(shards, mesh=mesh, in_specs=in_specs, out_specs=out_specs, check_vma=False)
```

profile of v0, /device:TPU:0, one launch (start us, length us, event | category | flops | bytes accessed | tf_op | source)
XLA Modules:
  0.0 94.6 jit_solution(12335367808657521242)
XLA Ops:
  6.5 0.0 copy-start
  6.5 0.0 all-gather.3.cloned.1.call-start
  6.5 0.8 subtract_bitcast_fusion
  7.4 0.1 fusion.17
  7.4 0.1 copy-done
  7.5 2.0 %fusion.8 = bf16[12,256,256]{2,1,0:T(8,128)(2,1)S(1)} fusion(bf16[12,256,256]{2,1,0:T(8,128)(2,1)} %param.7, bf16[12,256]{1,0:T(8,128)(2,1)S(1)} %fusion.17, bf16[2,256,256]{2,1,0:T(8,128)(2,1)S(1)} %copy-done, s32[]{:T(128)S(6)} %select_n.27), kind=kOutput, calls=%fused_computation.13 | convolution fusion | flops 403439616 | bytes 3284996 | tf_op jit(solution)/shard_map/ixq,qr->ixr/dot_general | solution.py:38
  9.6 0.0 copy-start.1
  9.6 1.0 %fusion.13 = bf16[2,256,256]{2,0,1:T(2,128)(2,1)S(1)} fusion(bf16[12,256,256]{2,1,0:T(8,128)(2,1)S(1)} %fusion.8, s32[12]{0:T(128)S(1)} %get-tuple-element.13, s32[2]{0:T(128)S(1)} %multiply_add_fusion.3), kind=kOutput, calls=%fused_computation.17 | convolution fusion | flops 3276824 | bytes 1835064 | tf_op jit(solution)/shard_map/ki,izq->kzq/dot_general | solution.py:53
  10.6 0.7 copy.20
  11.3 0.0 all-gather.3.cloned.1.call-update
  11.4 0.0 all-gather.5.cloned.1.call-start
  11.4 0.0 copy-done.1
  11.4 1.7 %multiply_bitcast_fusion = (bf16[12,256,256,1]{2,1,0,3:T(8,128)(2,1)S(1)}, bf16[12,256,256]{2,1,0:T(8,128)(2,1)S(1)}) fusion(bf16[12,256,256]{2,1,0:T(8,128)(2,1)S(1)} %copy-done.1, bf16[12,256]{1,0:T(8,128)(2,1)S(1)} %fusion.17, bf16[12,256,256]{2,1,0:T(8,128)(2,1)} %param.8), kind=kLoop, calls=%fused_computation.15 | loop fusion | flops 2359296 | bytes 6297600 | tf_op jit(solution)/shard_map/mul | solution.py:37
  13.2 1.0 %fusion.10 = bf16[2,256,256]{2,0,1:T(2,128)(2,1)S(1)} fusion(bf16[12,256,256]{2,1,0:T(8,128)(2,1)S(1)} %get-tuple-element.12, s32[12]{0:T(128)S(1)} %get-tuple-element.13, s32[2]{0:T(128)S(1)} %multiply_add_fusion.3), kind=kOutput, calls=%fused_computation.16 | convolution fusion | flops 3276824 | bytes 1835064 | tf_op jit(solution)/shard_map/ki,ixz->kxz/dot_general | solution.py:56
  14.2 0.7 copy.23
  14.9 0.0 all-gather.5.cloned.1.call-update
  15.0 1.5 %convert_bitcast_fusion = bf16[4,4,256,256]{3,0,1,2:T(4,128)(2,1)S(1)} fusion(bf16[12,256,256,1]{2,1,0,3:T(8,128)(2,1)S(1)} %get-tuple-element.11, s32[4,4]{1,0:T(4,128)S(1)} %multiply_add_fusion, s32[12]{0:T(128)S(1)} %get-tuple-element.13), kind=kOutput, calls=%fused_computation.11 | convolution fusion | flops 26214592 | bytes 3670128 | tf_op jit(solution)/shard_map/kri,ixq->rkxq/dot_general | solution.py:46
  16.5 2.1 %copy.18 = bf16[4,4,256,256]{3,1,2,0:T(4,128)(2,1)} copy(bf16[4,4,256,256]{3,0,1,2:T(4,128)(2,1)S(1)} %convert_bitcast_fusion) | data formatting | bytes 4194304 | tf_op jit(solution)/shard_map/convert_element_type | solution.py:48
  18.6 4.3 %all-to-all-start = ((bf16[4,4,256,256]{3,1,2,0:T(4,128)(2,1)}), bf16[4,4,256,256]{3,1,2,0:T(4,128)(2,1)S(1)}, u32[]{:S(2)}, u32[]{:S(2)}) async-start(bf16[4,4,256,256]{3,1,2,0:T(4,128)(2,1)} %copy.18), calls=%async_computation | async-start | bytes 4194304 | tf_op jit(solution)/shard_map/all_to_all | solution.py:49
  22.9 0.1 compare_convert_fusion
  23.0 11.1 %all-gather.3.cloned.1.call-done = bf16[8,256,256]{2,1,0:T(8,128)(2,1)} async-done(((bf16[2,256,256]{2,1,0:T(8,128)(2,1)}), bf16[8,256,256]{2,1,0:T(8,128)(2,1)}) %all-gather.3.cloned.1.call-update) | async-done | bytes 1048592 | tf_op jit(solution)/shard_map/all_gather | solution.py:60
  34.1 1.3 %copy.50 = bf16[2,2,2,256,256]{4,3,2,0,1:T(8,128)(2,1)S(1)} copy(bf16[2,2,2,256,256]{4,3,2,1,0:T(8,128)(2,1)} %bitcast.64) | data formatting | bytes 2097152 | tf_op jit(solution)/shard_map/reshape;reshape | solution.py:8
  35.4 1.1 %fusion.32 = (bf16[1,2,2,256,256]{4,3,2,1,0:T(8,128)(2,1)}, bf16[1,2,2,256,256]{4,3,2,1,0:T(8,128)(2,1)}) fusion(bf16[2,2,2,256,256]{4,3,2,1,0:T(8,128)(2,1)S(1)} %bitcast.63), kind=kLoop, calls=%fused_computation.47 | loop fusion | bytes 2097152 | tf_op jit(solution)/shard_map/slice | solution.py:77
  36.4 21.1 %all-gather.5.cloned.1.call-done = bf16[8,256,256]{2,1,0:T(8,128)(2,1)} async-done(((bf16[2,256,256]{2,1,0:T(8,128)(2,1)}), bf16[8,256,256]{2,1,0:T(8,128)(2,1)}) %all-gather.5.cloned.1.call-update) | async-done | bytes 1048592 | tf_op jit(solution)/shard_map/all_gather | solution.py:61
  57.5 1.3 %fusion.33 = (bf16[1,2,2,256,256]{4,3,2,0,1:T(8,128)(2,1)S(1)}, bf16[1,2,2,256,256]{4,3,2,0,1:T(8,128)(2,1)S(1)}) fusion(bf16[2,2,2,256,256]{4,3,2,0,1:T(8,128)(2,1)} %bitcast.65), kind=kLoop, calls=%fused_computation.48 | loop fusion | bytes 2097152 | tf_op jit(solution)/shard_map/slice | solution.py:80
  58.8 0.0 all-to-all-done
  58.8 0.4 copy.49
  59.2 0.1 fusion.31
  59.3 0.0 copy-start.3
  59.3 0.1 convert_bitcast_fusion.2
  59.4 0.1 convert_bitcast_fusion.1
  59.6 0.8 copy-done.3
  60.4 0.0 copy-start.2
  60.4 1.3 %add_convert_fusion = bf16[8,256,4,256]{3,1,2,0:T(8,128)(2,1)S(1)} fusion(f32[256,4,256]{2,0,1:T(8,128)S(1)} %convert_bitcast_fusion.1, f32[8,4]{1,0:T(8,128)S(1)} %compare_convert_fusion, bf16[8,256,256,1]{2,1,3,0:T(8,128)(2,1)S(1)} %bitcast.67, bf16[4,256,256,1]{2,1,0,3:T(8,128)(2,1)S(1)} %bitcast.69), kind=kOutput, calls=%fused_computation.2 | convolution fusion | flops 1080033280 | bytes 6815872 | tf_op jit(solution)/shard_map/axq,bzq->axbz/dot_general | solution.py:74
  61.6 0.0 copy-done.2
  61.7 3.4 %add_convert_fusion.1 = bf16[8,256,4,256]{3,1,2,0:T(8,128)(2,1)} fusion(f32[256,4,256]{2,0,1:T(8,128)S(1)} %convert_bitcast_fusion.2, f32[8,4]{1,0:T(8,128)S(1)} %compare_convert_fusion, bf16[8,256,256,1]{2,1,3,0:T(8,128)(2,1)S(1)} %bitcast.66, bf16[4,256,256,1]{2,1,0,3:T(8,128)(2,1)S(1)} %bitcast.68), kind=kOutput, calls=%fused_computation.3 | convolution fusion | flops 1080033280 | bytes 6815872 | tf_op jit(solution)/shard_map/axq,bzq->axbz/dot_general | solution.py:74
  65.1 10.5 %fusion = f32[8,256,4,256]{3,1,2,0:T(8,128)} fusion(f32[8,256,4,256]{3,2,1,0:T(4,128)} %param.6, bf16[8,256,4,256]{3,1,2,0:T(8,128)(2,1)S(1)} %add_convert_fusion, bf16[8,256,4,256]{3,1,2,0:T(8,128)(2,1)} %add_convert_fusion.1), kind=kLoop, calls=%fused_computation.1 | loop fusion | flops 8388608 | bytes 25165824 | tf_op jit(solution)/shard_map/add | solution.py:83
  75.6 12.2 %copy.25 = f32[8,256,4,256]{3,2,1,0:T(4,128)} copy(f32[8,256,4,256]{3,1,2,0:T(8,128)} %fusion) | data formatting | bytes 16777216 | tf_op jit(solution)/shard_map/add | solution.py:83
  (4 shorter events, 0.0 us)
Async XLA Ops:
  6.5 1.0 %copy-start = (bf16[2,256,256]{2,1,0:T(8,128)(2,1)S(1)}, bf16[2,256,256]{2,1,0:T(8,128)(2,1)}, u32[]{:S(2)}) copy-start(bf16[2,256,256]{2,1,0:T(8,128)(2,1)} %param.9) | copy-start | bytes 786436
  6.5 27.5 %all-gather.3.cloned.1.call-start = ((), (), s32[]{:S(2)}) async-start(), calls=%async_computation.1 | async-start | bytes 1310720 | tf_op jit(solution)/shard_map/all_gather | solution.py:60
  9.6 1.9 %copy-start.1 = (bf16[12,256,256]{2,1,0:T(8,128)(2,1)S(1)}, bf16[12,256,256]{2,1,0:T(8,128)(2,1)}, u32[]{:S(2)}) copy-start(bf16[12,256,256]{2,1,0:T(8,128)(2,1)} %param.7) | copy-start | bytes 4718596
  11.4 46.2 %all-gather.5.cloned.1.call-start = ((), (), s32[]{:S(2)}) async-start(), calls=%async_computation.2 | async-start | bytes 1310720 | tf_op jit(solution)/shard_map/all_gather | solution.py:61
  18.6 40.2 %all-to-all-start = ((bf16[4,4,256,256]{3,1,2,0:T(4,128)(2,1)}), bf16[4,4,256,256]{3,1,2,0:T(4,128)(2,1)S(1)}, u32[]{:S(2)}, u32[]{:S(2)}) async-start(bf16[4,4,256,256]{3,1,2,0:T(4,128)(2,1)} %copy.18), calls=%async_computation | async-start | bytes 4194304 | tf_op jit(solution)/shard_map/all_to_all | solution.py:49
  59.3 1.0 %copy-start.3 = (bf16[1,2,2,256,256]{4,3,2,1,0:T(8,128)(2,1)S(1)}, bf16[1,2,2,256,256]{4,3,2,1,0:T(8,128)(2,1)}, u32[]{:S(2)}) copy-start(bf16[1,2,2,256,256]{4,3,2,1,0:T(8,128)(2,1)} %get-tuple-element.8) | copy-start | bytes 1572868
  60.4 1.3 %copy-start.2 = (bf16[1,2,2,256,256]{4,3,2,1,0:T(8,128)(2,1)S(1)}, bf16[1,2,2,256,256]{4,3,2,1,0:T(8,128)(2,1)}, u32[]{:S(2)}) copy-start(bf16[1,2,2,256,256]{4,3,2,1,0:T(8,128)(2,1)} %get-tuple-element.7) | copy-start | bytes 1572868
Sparse Core Ops, SparseCore 0:
  11.5 22.5 all-gather.2
  35.6 21.8 all-gather.4
where the time goes:
time: 95 us; the launch traced here: 94.6 us
  waiting for transfers between devices  32.2 us (34%)
  local copies, waits for them, and re-layouts  20.8 us (22%)
  between operations  13.5 us (14%)
  other arithmetic  13.4 us (14%)
  matrix products  10.3 us (11%)
  starting transfers between devices  4.3 us (5%)
    all_gather x1, waiting for transfers between devices, shards(): lax.all_gather(diag_send, 'row', axis=0, tiled=True)  21.1 us
    add x1, local copies, waits for them, and re-layouts, shards(): running = running + rounded.astype(jnp.float32)  12.2 us
    all_gather x1, waiting for transfers between devices, shards(): lax.all_gather(col_send, 'row', axis=0, tiled=True)  11.1 us
    add x1, other arithmetic, shards(): running = running + rounded.astype(jnp.float32)  10.5 us
    dot_general x2, matrix products, shards(): jnp.einsum('axq,bzq->axbz', row_received[child_index], col_received[child...  4.72 us
    all_to_all x1, starting transfers between devices, shards(): lax.all_to_all(row_send, 'row', split_axis=0, concat_axis=0, tiled=True)  4.26 us
    convert_element_type x1, local copies, waits for them, and re-layouts, shards(): row_send = jnp.einsum('kri,ixq->rkxq', row_place, masked, preferred_eleme...  2.13 us
    dot_general x1, matrix products, shards(): jnp.einsum('ixq,qr->ixr', masked, coupling_own, preferred_element_type=jn...  2.03 us
  transfers between devices with their start and end apart: 3, of which 2 were waited for; matrix products, arithmetic and copies ran while one was open for 11% of the time, Pallas kernels for 0%

commit v1 on v0

v1 whole, which is shorter than its diff:
```python
import functools

import jax
import jax.numpy as jnp
from jax import lax
from jax.experimental import pallas as pl
from jax.experimental.pallas import tpu as pltpu
from jax.sharding import PartitionSpec as P


ANY = pl.BlockSpec(memory_space=pl.ANY)
SMEM = pl.BlockSpec(memory_space=pltpu.SMEM)
VMEM = pl.BlockSpec(memory_space=pltpu.VMEM)
LANES = 128


def in_hbm(x):
    return pltpu.with_memory_space_constraint(x, pltpu.HBM)


class Plan:
    def __init__(self, rows_n, cols_n, rows_local, cols_local, block, rank, blocks):
        self.rows_n, self.cols_n = rows_n, cols_n
        self.halves = rows_n // 2
        self.window = 2 * rows_local
        self.rows_local, self.cols_local = rows_local, cols_local
        self.row_cap = self.window // rows_n
        self.col_cap = self.window // cols_n
        self.half_cap = self.row_cap // 2
        self.block, self.rank, self.blocks = block, rank, blocks
        self.step = cols_local * (block // LANES)
        assert cols_n == 2 * rows_n and self.half_cap == self.col_cap

    def here(self):
        row, col = lax.axis_index("row"), lax.axis_index("col")
        return row, col, row // 2, row % 2

    def parity(self, group, col):
        return (col // self.rows_n + (col // self.halves) % 2 + 2 * group // self.halves) % 2

    def owns_diag(self, group, col):
        return (col % self.rows_n) // 2 == group


def read_map(plan, block_map, valid_rows, child, group, count, where=None):
    for slot in range(plan.window):
        count[slot] = 0
        if where is not None:
            where[slot] = 0
    for i in range(plan.blocks):
        spot = block_map[child, group * plan.blocks + i] - group * plan.window
        count[spot] = valid_rows[child, group * plan.blocks + i]
        if where is not None:
            where[spot] = i


def keep_rows(plan, x, count):
    pos = lax.broadcasted_iota(jnp.int32, (plan.block, 1), 0)
    return jnp.where(pos < count, x, jnp.zeros_like(x))


def project(x, mixer):
    dims = (((0,), (1,)), ((), ()))
    return lax.dot_general(mixer, x, dims, preferred_element_type=jnp.float32).astype(x.dtype)


def pack_rows_kernel(plan, block_map, valid_rows, generators, *refs):
    outs, (where, count, sems) = refs[:-3], refs[-3:]
    _, col, group, child = plan.here()
    read_map(plan, block_map, valid_rows, child, group, count, where)
    copies = []
    for i, out in enumerate(outs):
        d, k = 1 + i // 2, i % 2
        aim = (group + plan.halves - d) % plan.halves
        target = 2 * aim + (child + k) % 2
        parity = plan.parity(aim, col)
        for j in range(plan.half_cap):
            source = where[(2 * j + parity) * plan.rows_n + target]
            copies.append(pltpu.make_async_copy(
                generators.at[source], out.at[j], sems.at[len(copies)]))
            copies[-1].start()
    for copy in copies:
        copy.wait()


def pack_rest_kernel(plan, block_map, valid_rows, generators, diagonal, coupling, mine, *refs):
    outs, (where, count, picked, mixer, sems) = refs[:-5], refs[-5:]
    _, col, group, child = plan.here()
    read_map(plan, block_map, valid_rows, child, group, count, where)
    copies = []

    def go(source, target):
        copies.append(pltpu.make_async_copy(source, target, sems.at[len(copies)]))
        copies[-1].start()
        return copies[-1]

    first = [go(coupling.at[child], mixer)]
    for s in range(plan.col_cap):
        first.append(go(generators.at[where[s * plan.cols_n + col]], picked.at[s]))
    for s in range(plan.col_cap):
        go(diagonal.at[where[s * plan.cols_n + col]], mine.at[plan.row_cap + plan.col_cap + s])
    partner = 2 * group + (child + 1) % 2
    for q in range(plan.row_cap):
        go(generators.at[where[q * plan.rows_n + partner]], mine.at[q])
    for copy in first:
        copy.wait()
    for s in range(plan.col_cap):
        masked = keep_rows(plan, picked[s], count[s * plan.cols_n + col])
        mine[plan.row_cap + s] = project(masked, mixer[...])
    for copy in copies[len(first):]:
        copy.wait()
    for i, out in enumerate(outs):
        aim = (group + plan.halves - (i + 1)) % plan.halves
        owns = plan.owns_diag(aim, col)

        @pl.when(owns)
        def _():
            for s in range(plan.col_cap):
                out[s] = mine[plan.row_cap + plan.col_cap + s]

        @pl.when(jnp.logical_not(owns))
        def _():
            for s in range(plan.col_cap):
                out[s] = mine[plan.row_cap + s]


def project_kernel(plan, block_map, valid_rows, coupling, *refs):
    halves = plan.halves
    rows_in, (out, count, mixer, sem) = refs[:-4], refs[-4:]
    row, col, group, child = plan.here()
    copy = pltpu.make_async_copy(coupling, mixer, sem)
    copy.start()
    copy.wait()
    for d in range(1, halves):
        aim = (group + d) % halves
        parity = plan.parity(group, col)
        for k in range(2):
            who = (child + k) % 2
            read_map(plan, block_map, valid_rows, who, aim, count)
            for j in range(plan.half_cap):
                rows = count[(2 * j + parity) * plan.rows_n + row]
                masked = keep_rows(plan, rows_in[2 * (d - 1) + k][j], rows)
                out[d - 1, k, j] = project(masked, mixer[who])


def strided(plan, part, b):
    return pl.ds(part * plan.cols_local + b, plan.block, stride=plan.step)


def add_tile(plan, total, a, b, value):
    for part in range(plan.block // LANES):
        rows = strided(plan, part, b)
        total[a, rows, :] += value[:, part * LANES:(part + 1) * LANES]


def diag_tile(plan, pair, counts):
    x_pos = lax.broadcasted_iota(jnp.int32, (plan.block, 1), 0)
    y_pos = lax.broadcasted_iota(jnp.int32, (1, plan.block), 1)
    return sum(
        jnp.where((x_pos < n) & (y_pos < n), x.astype(jnp.float32), 0.0)
        for x, n in zip(pair, counts))


def matmul(x, y):
    return jnp.dot(x, y, preferred_element_type=jnp.float32)


def begin_kernel(plan, block_map, valid_rows, generators, diagonal, mine, theirs, front,
                 total, left, count_a, count_b, where, own_rows, own_diag, sems):
    row, col, group, child = plan.here()
    read_map(plan, block_map, valid_rows, child, group, count_a, where)
    read_map(plan, block_map, valid_rows, (child + 1) % 2, group, count_b)
    counts = (count_a, count_b)
    loads = []
    for q in range(plan.row_cap):
        loads.append(pltpu.make_async_copy(
            generators.at[where[q * plan.rows_n + row]], own_rows.at[q], sems.at[q]))
    for s in range(plan.col_cap):
        loads.append(pltpu.make_async_copy(
            diagonal.at[where[s * plan.cols_n + col]], own_diag.at[s],
            sems.at[plan.row_cap + s]))
    base = plan.row_cap + plan.col_cap
    reads = []
    for i in range(plan.rows_local):
        a = (group * plan.row_cap + i) % plan.rows_local
        reads.append(pltpu.make_async_copy(front.at[a], total.at[a], sems.at[base + i]))
    for copy in loads + reads:
        copy.start()
    for copy in loads:
        copy.wait()
    for q in range(plan.row_cap):
        where_q = q * plan.rows_n + row
        span = pl.ds(q * plan.block, plan.block)
        left[0, span, :] = keep_rows(plan, own_rows[q], count_a[where_q])
        left[1, span, :] = keep_rows(plan, theirs[q], count_b[where_q])
    for copy in reads[: plan.row_cap]:
        copy.wait()
    for s in range(plan.col_cap):
        value = matmul(left[0], mine[plan.row_cap + s]) + matmul(left[1], theirs[plan.row_cap + s])
        b = group * plan.col_cap + s
        for q in range(plan.row_cap):
            a = group * plan.row_cap + q
            add_tile(plan, total, a, b, value[q * plan.block:(q + 1) * plan.block])

    @pl.when(row == col % plan.rows_n)
    def _():
        for s in range(plan.col_cap):
            a = group * plan.row_cap + 2 * s + col // plan.rows_n
            b = group * plan.col_cap + s
            n = [count[s * plan.cols_n + col] for count in counts]
            pair = (own_diag[s], theirs[plan.row_cap + plan.col_cap + s])
            add_tile(plan, total, a, b, diag_tile(plan, pair, n))

    for copy in reads[plan.row_cap:]:
        copy.wait()


def finish_kernel(plan, block_map, valid_rows, left, mine, theirs, formed, formed_too, *refs):
    halves = plan.halves
    groups = [refs[6 * i: 6 * i + 6] for i in range(halves - 1)]
    _, out, total, count_a, count_b, far, right, sems = refs[6 * (halves - 1):]
    row, col, group, child = plan.here()
    owns = plan.owns_diag(group, col)
    main = row == col % plan.rows_n
    half = plan.half_cap

    for e in range(1, halves):
        direct, swapped = groups[e - 1][4:]
        for k in range(2):
            @pl.when(main)
            def _():
                for s in range(plan.col_cap):
                    right[e - 1, k, s] = formed[e - 1, k, s]

            @pl.when(owns & jnp.logical_not(main))
            def _():
                for s in range(plan.col_cap):
                    right[e - 1, k, s] = formed_too[e - 1, 1 - k, s]

            @pl.when(jnp.logical_not(owns))
            def _():
                for s in range(plan.col_cap):
                    right[e - 1, k, s] = (direct, swapped)[k][s]

    writes = []

    def write(a):
        writes.append(pltpu.make_async_copy(total.at[a], out.at[a], sems.at[len(writes)]))
        writes[-1].start()

    def rights(e, k, s):
        if e > 0:
            return right[e - 1, k, s]
        return (mine, theirs)[k][plan.row_cap + s]

    for g in range(2):
        span = pl.ds(g * half * plan.block, half * plan.block)
        for e in range(1, halves):
            for s in range(plan.col_cap):
                value = matmul(left[0, span, :], rights(e, 0, s))
                value += matmul(left[1, span, :], rights(e, 1, s))
                b = (group + e) % halves * plan.col_cap + s
                for j in range(half):
                    a = group * plan.row_cap + g * half + j
                    add_tile(plan, total, a, b, value[j * plan.block:(j + 1) * plan.block])
        for j in range(half):
            write(group * plan.row_cap + g * half + j)

    for d in range(1, halves):
        aim = (group + d) % halves
        read_map(plan, block_map, valid_rows, child, aim, count_a)
        read_map(plan, block_map, valid_rows, (child + 1) % 2, aim, count_b)
        counts = (count_a, count_b)
        parity = plan.parity(group, col)
        for g in range(2):
            odd = (parity + g) % 2
            for k in range(2):
                for j in range(half):
                    rows = counts[k][(2 * j + odd) * plan.rows_n + row]
                    far[k, pl.ds(j * plan.block, plan.block), :] = keep_rows(
                        plan, groups[d - 1][2 * g + k][j], rows)
            for e in range(halves):
                for s in range(plan.col_cap):
                    value = matmul(far[0], rights(e, 0, s)) + matmul(far[1], rights(e, 1, s))
                    b = (group + e) % halves * plan.col_cap + s
                    for j in range(half):
                        a = aim * plan.row_cap + 2 * j + odd
                        add_tile(plan, total, a, b, value[j * plan.block:(j + 1) * plan.block])
            if g == 0:
                @pl.when(main)
                def _():
                    for s in range(plan.col_cap):
                        a = aim * plan.row_cap + 2 * s + odd
                        b = aim * plan.col_cap + s
                        n = [count[s * plan.cols_n + col] for count in counts]
                        pair = (groups[d - 1][4][s], groups[d - 1][5][s])
                        add_tile(plan, total, a, b, diag_tile(plan, pair, n))
            for j in range(half):
                write(aim * plan.row_cap + 2 * j + odd)
    for copy in writes:
        copy.wait()


def shards(rows_n, cols_n, parent_front, generators, diagonal_blocks, coupling, block_map, valid_rows):
    rows_local, block, cols_local, width = parent_front.shape
    blocks, _, rank = generators.shape
    plan = Plan(rows_n, cols_n, rows_local, cols_local, block, rank, blocks)
    halves, row_cap, col_cap, half = plan.halves, plan.row_cap, plan.col_cap, plan.half_cap
    dt = generators.dtype
    parts = width // LANES
    table = pltpu.SMEM((plan.window,), jnp.int32)

    def shape(*lead):
        return jax.ShapeDtypeStruct(lead + (block, rank), dt)

    def sems(n):
        return pltpu.SemaphoreType.DMA((n,))

    def call(kernel, out_shape, in_specs, out_specs, scratch, mib, args, aliases={}):
        return pl.pallas_call(
            functools.partial(kernel, plan), out_shape=out_shape, in_specs=in_specs,
            out_specs=out_specs, scratch_shapes=scratch,
            input_output_aliases=aliases,
            compiler_params=pltpu.CompilerParams(vmem_limit_bytes=mib << 20))(*args)

    front = parent_front.reshape(rows_local, block, cols_local, parts, LANES)
    front = front.transpose(0, 1, 3, 2, 4).reshape(rows_local, block * plan.step, LANES)
    block_map, valid_rows, generators, diagonal_blocks, coupling, front = map(
        in_hbm, (block_map, valid_rows, generators, diagonal_blocks, coupling, front))

    def send(x, move):
        pairs = [
            (row * cols_n + col, to_row * cols_n + to_col)
            for row in range(rows_n)
            for col in range(cols_n)
            for to_row, to_col in [move(row, col)]
        ]
        return lax.ppermute(x, ("row", "col"), pairs)

    def across(d, k):
        return lambda row, col: (2 * ((row // 2 - d) % halves) + (row % 2 + k) % 2, col)

    def partner(row, col):
        return row ^ 1, col

    def pair(row, col):
        return row, col ^ halves

    flows = [(d, k) for d in range(1, halves) for k in range(2)]
    rows_out = call(
        pack_rows_kernel, [shape(half)] * len(flows), [SMEM, SMEM, ANY],
        [VMEM] * len(flows), [table, table, sems(len(flows) * half)], 8,
        (block_map, valid_rows, generators))
    near = {flow: send(x, across(*flow)) for flow, x in zip(flows, rows_out)}
    mine, *cols_out = call(
        pack_rest_kernel, [shape(row_cap + 2 * col_cap)] + [shape(col_cap)] * (halves - 1),
        [SMEM, SMEM, ANY, ANY, ANY], [VMEM] * halves,
        [table, table, pltpu.VMEM((col_cap, block, rank), dt), pltpu.VMEM((rank, rank), dt),
         sems(1 + 2 * col_cap + row_cap)], 12,
        (block_map, valid_rows, generators, diagonal_blocks, coupling))
    direct = {d: send(cols_out[d - 1], across(d, 0)) for d in range(1, halves)}
    theirs = send(mine, partner)
    total, left = call(
        begin_kernel,
        [jax.ShapeDtypeStruct(front.shape, front.dtype),
         jax.ShapeDtypeStruct((2, row_cap * block, rank), dt)],
        [SMEM, SMEM, ANY, ANY, VMEM, VMEM, ANY], [VMEM] * 2,
        [table, table, table, pltpu.VMEM((row_cap, block, rank), dt),
         pltpu.VMEM((col_cap, block, block), dt), sems(row_cap + col_cap + rows_local)], 24,
        (block_map, valid_rows, generators, diagonal_blocks, mine, theirs, front))
    passed = {flow: send(near[flow], pair) for flow in flows}
    formed = call(
        project_kernel, shape(halves - 1, 2, col_cap),
        [SMEM, SMEM, ANY] + [VMEM] * len(flows), VMEM,
        [table, pltpu.VMEM((2, rank, rank), dt), pltpu.SemaphoreType.DMA], 12,
        (block_map, valid_rows, coupling, *(near[flow] for flow in flows)))
    formed_too = send(formed, partner)
    swapped = {d: send(direct[d], partner) for d in range(1, halves)}
    rest = []
    for d in range(1, halves):
        rest += [near[d, 0], near[d, 1], passed[d, 0], passed[d, 1], direct[d], swapped[d]]
    args = (block_map, valid_rows, left, mine, theirs, formed, formed_too, *rest, total)
    out, _ = call(
        finish_kernel, [jax.ShapeDtypeStruct(front.shape, front.dtype)] * 2,
        [SMEM, SMEM] + [VMEM] * (len(args) - 2), [ANY, VMEM],
        [table, table, pltpu.VMEM((2, half * block, rank), dt),
         pltpu.VMEM((halves - 1, 2, col_cap, block, rank), dt), sems(rows_local)],
        24, args, {len(args) - 1: 1})
    out = out.reshape(rows_local, block, parts, cols_local, LANES)
    return out.transpose(0, 1, 3, 2, 4).reshape(rows_local, block, cols_local, width)


def solution(mesh):
    in_specs = (
        P(None, "row", None, "col"),
        P("row", None, None),
        P("row", None, None),
        P(),
        P(),
        P(),
    )
    out_specs = P(None, "row", None, "col")

    def body(*args):
        return shards(mesh.shape["row"], mesh.shape["col"], *args)

    return jax.shard_map(body, mesh=mesh, in_specs=in_specs, out_specs=out_specs, check_vma=False)
```

time: 95 us -> 42 us (0.44)
  local copies, waits for them, and re-layouts: 20.8 us -> 0 us
  Pallas kernels: 0 us -> 16.4 us
  waiting for transfers between devices: 32.2 us -> 17.9 us
  between operations: 13.5 us -> 0.04 us
  other arithmetic: 13.4 us -> 0 us
  matrix products: 10.3 us -> 0 us
  starting transfers between devices: 4.3 us -> 7.37 us
    all_gather x2 -> x0, waiting for transfers between devices: 32.2 us -> none  [the longest x1 21.1 us: shards(): lax.all_gather(diag_send, 'row', axis=0, tiled=True)]
    ppermute x0 -> x8, waiting for transfers between devices: none -> 17.9 us  [send(): return lax.ppermute(x, ('row', 'col'), pairs)]
    pallas_call x0 -> x5, Pallas kernels: none -> 16.4 us  [call(): pl.pallas_call(functools.partial(kernel, plan), out_shape=out_shape, in_s...]
    add x1 -> x0, local copies, waits for them, and re-layouts: 12.2 us -> none  [shards(): running = running + rounded.astype(jnp.float32)]
    add x4 -> x0, other arithmetic: 10.5 us -> none  [the longest x1 10.5 us: shards(): running = running + rounded.astype(jnp.float32)]
    dot_general x6 -> x0, matrix products: 10.3 us -> none  [the longest x2 4.72 us: shards(): jnp.einsum('axq,bzq->axbz', row_received[child_index], col_received[child...]
    ppermute x0 -> x8, starting transfers between devices: none -> 7.37 us  [send(): return lax.ppermute(x, ('row', 'col'), pairs)]
    all_to_all x1 -> x0, starting transfers between devices: 4.26 us -> none  [shards(): lax.all_to_all(row_send, 'row', split_axis=0, concat_axis=0, tiled=True)]
  transfers between devices with their start and end apart: 3 -> 8, of which waited for: 2 -> 5; matrix products, arithmetic and copies ran while one was open for 11% -> 0% of each run, Pallas kernels for 0% -> 21%
where the time goes in v1:
time: 42 us; the launch traced here: 41.7 us
  waiting for transfers between devices  17.9 us (43%)
  Pallas kernels  16.4 us (39%)
  starting transfers between devices  7.37 us (18%)
    ppermute x8, waiting for transfers between devices, send(): return lax.ppermute(x, ('row', 'col'), pairs)  17.9 us
    pallas_call x5, Pallas kernels, call(): pl.pallas_call(functools.partial(kernel, plan), out_shape=out_shape, in_s...  16.4 us
    ppermute x8, starting transfers between devices, send(): return lax.ppermute(x, ('row', 'col'), pairs)  7.37 us
  transfers between devices with their start and end apart: 8, of which 5 were waited for; matrix products, arithmetic and copies ran while one was open for 0% of the time, Pallas kernels for 21%

profile of v1, /device:TPU:0, one launch (start us, length us, event | category | flops | bytes accessed | tf_op | source)
XLA Modules:
  0.0 41.7 jit_solution(497397295008560075)
XLA Ops:
  0.0 2.2 %shard_map.64 = (bf16[8,256,256]{2,1,0:T(8,128)(2,1)S(1)}, bf16[2,256,256]{2,1,0:T(8,128)(2,1)S(1)}) custom-call(s32[2,24]{1,0:T(2,128)} %block_map.9, s32[2,24]{1,0:T(2,128)} %valid_rows.9, bf16[12,256,256]{2,1,0:T(8,128)(2,1)} %generators.5, bf16[12,256,256]{2,1,0:T(8,128)(2,1)} %diagonal.3, bf16[2,256,256]{2,1,0:T(8,128)(2,1)} %coupling.3), custom_call_target="tpu_custom_call" | custom-call | tf_op jit(solution)/shard_map/pallas_call | solution.py:320
  2.2 0.6 %collective-permute-start = (bf16[8,256,256]{2,1,0:T(8,128)(2,1)S(1)}, bf16[8,256,256]{2,1,0:T(8,128)(2,1)S(1)}, u32[]{:S(2)}, u32[]{:S(2)}) collective-permute-start(bf16[8,256,256]{2,1,0:T(8,128)(2,1)S(1)} %get-tuple-element.12.mine), channel_id=1, source_target_pairs={{0,8},{1,9},{2,10},{3,11},{4,12},{5,13},{6,14},{7,15},{8,0},{9,1},... | collective-permute-start | bytes 3145736 | tf_op jit(solution)/shard_map/ppermute | solution.py:338
  2.8 1.9 %shard_map.66 = (bf16[2,256,256]{2,1,0:T(8,128)(2,1)S(1)}, bf16[2,256,256]{2,1,0:T(8,128)(2,1)S(1)}) custom-call(s32[2,24]{1,0:T(2,128)} %block_map.9, s32[2,24]{1,0:T(2,128)} %valid_rows.9, bf16[12,256,256]{2,1,0:T(8,128)(2,1)} %generators.5), custom_call_target="tpu_custom_call" | custom-call | tf_op jit(solution)/shard_map/pallas_call | solution.py:320
  4.7 2.6 %collective-permute-start.1 = (bf16[2,256,256]{2,1,0:T(8,128)(2,1)S(1)}, bf16[2,256,256]{2,1,0:T(8,128)(2,1)S(1)}, u32[]{:S(2)}, u32[]{:S(2)}) collective-permute-start(bf16[2,256,256]{2,1,0:T(8,128)(2,1)S(1)} %get-tuple-element.14), channel_id=1, source_target_pairs={{0,16},{1,17},{2,18},{3,19},{4,20},{5,21},{6,22},{7,23},{8,24},{9,... | collective-permute-start | bytes 786440 | tf_op jit(solution)/shard_map/ppermute | solution.py:338
  7.3 0.2 collective-permute-start.2
  7.5 1.7 %collective-permute-start.6 = (bf16[2,256,256]{2,1,0:T(8,128)(2,1)S(1)}, bf16[2,256,256]{2,1,0:T(8,128)(2,1)S(1)}, u32[]{:S(2)}, u32[]{:S(2)}) collective-permute-start(bf16[2,256,256]{2,1,0:T(8,128)(2,1)S(1)} %get-tuple-element.16), channel_id=1, source_target_pairs={{0,16},{1,17},{2,18},{3,19},{4,20},{5,21},{6,22},{7,23},{8,24},{9,... | collective-permute-start | bytes 786440 | tf_op jit(solution)/shard_map/ppermute | solution.py:338
  9.1 5.3 %collective-permute-done.1.refs_0_ = bf16[2,256,256]{2,1,0:T(8,128)(2,1)S(1)} collective-permute-done((bf16[2,256,256]{2,1,0:T(8,128)(2,1)S(1)}, bf16[2,256,256]{2,1,0:T(8,128)(2,1)S(1)}, u32[]{:S(2)}, u32[]{:S(2)}) %collective-permute-start.1) | collective-permute-done | bytes 262176 | tf_op jit(solution)/shard_map/ppermute | solution.py:338
  14.4 5.2 %collective-permute-done.2.refs_1_ = bf16[2,256,256]{2,1,0:T(8,128)(2,1)S(1)} collective-permute-done((bf16[2,256,256]{2,1,0:T(8,128)(2,1)S(1)}, bf16[2,256,256]{2,1,0:T(8,128)(2,1)S(1)}, u32[]{:S(2)}, u32[]{:S(2)}) %collective-permute-start.2) | collective-permute-done | bytes 262176 | tf_op jit(solution)/shard_map/ppermute | solution.py:338
  19.7 2.1 %shard_map.67.formed = bf16[1,2,2,256,256]{4,3,2,1,0:T(8,128)(2,1)S(1)} custom-call(s32[2,24]{1,0:T(2,128)} %block_map.9, s32[2,24]{1,0:T(2,128)} %valid_rows.9, bf16[2,256,256]{2,1,0:T(8,128)(2,1)} %coupling.3, bf16[2,256,256]{2,1,0:T(8,128)(2,1)S(1)} %collective-permute-done.1.refs_0_, bf16[2,256,256]{2,1,0:T(8,128)(2,1)S(1)} %collective-permute-done.2.refs_1_), custom_call_target="tpu_custom_call" | custom-call | tf_op jit(solution)/shard_map/pallas_call | solution.py:320
  21.7 0.3 collective-permute-start.3
  22.0 2.1 %collective-permute-start.4 = (bf16[2,256,256]{2,1,0:T(8,128)(2,1)S(1)}, bf16[2,256,256]{2,1,0:T(8,128)(2,1)S(1)}, u32[]{:S(2)}, u32[]{:S(2)}) collective-permute-start(bf16[2,256,256]{2,1,0:T(8,128)(2,1)S(1)} %collective-permute-done.1.refs_0_), channel_id=1, source_target_pairs={{0,2},{1,3},{2,0},{3,1},{4,6},{5,7},{6,4},{7,5},{8,10},{9,11},{10,... | collective-permute-start | bytes 786440 | tf_op jit(solution)/shard_map/ppermute | solution.py:338
  24.1 0.0 collective-permute-start.5
  24.1 1.3 %collective-permute-done.6.refs_4_ = bf16[2,256,256]{2,1,0:T(8,128)(2,1)S(1)} collective-permute-done((bf16[2,256,256]{2,1,0:T(8,128)(2,1)S(1)}, bf16[2,256,256]{2,1,0:T(8,128)(2,1)S(1)}, u32[]{:S(2)}, u32[]{:S(2)}) %collective-permute-start.6) | collective-permute-done | bytes 262176 | tf_op jit(solution)/shard_map/ppermute | solution.py:338
  25.5 0.0 collective-permute-start.7
  25.5 0.0 collective-permute-done.theirs
  25.5 4.8 %shard_map.65 = (f32[8,2048,128]{2,1,0:T(8,128)S(1)}, bf16[2,1024,256]{2,1,0:T(8,128)(2,1)S(1)}) custom-call(s32[2,24]{1,0:T(2,128)} %block_map.9, s32[2,24]{1,0:T(2,128)} %valid_rows.9, bf16[12,256,256]{2,1,0:T(8,128)(2,1)} %generators.5, bf16[12,256,256]{2,1,0:T(8,128)(2,1)} %diagonal.3, bf16[8,256,256]{2,1,0:T(8,128)(2,1)S(1)} %get-tuple-element.12.mine, ...), custom_call_target="tpu_custom_call" | custom-call | tf_op jit(solution)/shard_map/pallas_call | solution.py:320
  30.3 1.0 %collective-permute-done.4.refs_2_ = bf16[2,256,256]{2,1,0:T(8,128)(2,1)S(1)} collective-permute-done((bf16[2,256,256]{2,1,0:T(8,128)(2,1)S(1)}, bf16[2,256,256]{2,1,0:T(8,128)(2,1)S(1)}, u32[]{:S(2)}, u32[]{:S(2)}) %collective-permute-start.4) | collective-permute-done | bytes 262176 | tf_op jit(solution)/shard_map/ppermute | solution.py:338
  31.3 5.0 %collective-permute-done.5.refs_3_ = bf16[2,256,256]{2,1,0:T(8,128)(2,1)S(1)} collective-permute-done((bf16[2,256,256]{2,1,0:T(8,128)(2,1)S(1)}, bf16[2,256,256]{2,1,0:T(8,128)(2,1)S(1)}, u32[]{:S(2)}, u32[]{:S(2)}) %collective-permute-start.5) | collective-permute-done | bytes 262176 | tf_op jit(solution)/shard_map/ppermute | solution.py:338
  36.3 0.0 collective-permute-done.7.refs_5_
  36.3 0.0 collective-permute-done.3.formed_too
  36.3 5.4 %shard_map.68 = (f32[8,2048,128]{2,1,0:T(8,128)}, f32[8,2048,128]{2,1,0:T(8,128)S(1)}) custom-call(s32[2,24]{1,0:T(2,128)} %block_map.9, s32[2,24]{1,0:T(2,128)} %valid_rows.9, bf16[2,1024,256]{2,1,0:T(8,128)(2,1)S(1)} %get-tuple-element.13.left, bf16[8,256,256]{2,1,0:T(8,128)(2,1)S(1)} %get-tuple-element.12.mine, ...), custom_call_target="tpu_custom_call", output_to_operand_aliasing={{1}: (13, {})} | custom-call | tf_op jit(solution)/shard_map/pallas_call | solution.py:320
Async XLA Ops:
  2.2 23.3 %collective-permute-start = (bf16[8,256,256]{2,1,0:T(8,128)(2,1)S(1)}, bf16[8,256,256]{2,1,0:T(8,128)(2,1)S(1)}, u32[]{:S(2)}, u32[]{:S(2)}) collective-permute-start(bf16[8,256,256]{2,1,0:T(8,128)(2,1)S(1)} %get-tuple-element.12.mine), channel_id=1, source_target_pairs={{0,8},{1,9},{2,10},{3,11},{4,12},{5,13},{6,14},{7,15},{8,0},{9,1},... | collective-permute-start | bytes 3145736 | tf_op jit(solution)/shard_map/ppermute | solution.py:338
  4.7 9.7 %collective-permute-start.1 = (bf16[2,256,256]{2,1,0:T(8,128)(2,1)S(1)}, bf16[2,256,256]{2,1,0:T(8,128)(2,1)S(1)}, u32[]{:S(2)}, u32[]{:S(2)}) collective-permute-start(bf16[2,256,256]{2,1,0:T(8,128)(2,1)S(1)} %get-tuple-element.14), channel_id=1, source_target_pairs={{0,16},{1,17},{2,18},{3,19},{4,20},{5,21},{6,22},{7,23},{8,24},{9,... | collective-permute-start | bytes 786440 | tf_op jit(solution)/shard_map/ppermute | solution.py:338
  7.3 12.4 %collective-permute-start.2 = (bf16[2,256,256]{2,1,0:T(8,128)(2,1)S(1)}, bf16[2,256,256]{2,1,0:T(8,128)(2,1)S(1)}, u32[]{:S(2)}, u32[]{:S(2)}) collective-permute-start(bf16[2,256,256]{2,1,0:T(8,128)(2,1)S(1)} %get-tuple-element.15), channel_id=1, source_target_pairs={{0,24},{1,25},{2,26},{3,27},{4,28},{5,29},{6,30},{7,31},{8,16},{9,... | collective-permute-start | bytes 786440 | tf_op jit(solution)/shard_map/ppermute | solution.py:338
  7.5 18.0 %collective-permute-start.6 = (bf16[2,256,256]{2,1,0:T(8,128)(2,1)S(1)}, bf16[2,256,256]{2,1,0:T(8,128)(2,1)S(1)}, u32[]{:S(2)}, u32[]{:S(2)}) collective-permute-start(bf16[2,256,256]{2,1,0:T(8,128)(2,1)S(1)} %get-tuple-element.16), channel_id=1, source_target_pairs={{0,16},{1,17},{2,18},{3,19},{4,20},{5,21},{6,22},{7,23},{8,24},{9,... | collective-permute-start | bytes 786440 | tf_op jit(solution)/shard_map/ppermute | solution.py:338
  21.7 14.5 %collective-permute-start.3 = (bf16[1,2,2,256,256]{4,3,2,1,0:T(8,128)(2,1)S(1)}, bf16[1,2,2,256,256]{4,3,2,1,0:T(8,128)(2,1)S(1)}, u32[]{:S(2)}, u32[]{:S(2)}) collective-permute-start(bf16[1,2,2,256,256]{4,3,2,1,0:T(8,128)(2,1)S(1)} %shard_map.67.formed), channel_id=1, source_target_pairs={{0,8},{1,9},{2,10},{3,11},{4,12},{5,13},{6,14},{7,15},{8,0},{9,1},... | collective-permute-start | bytes 1572872 | tf_op jit(solution)/shard_map/ppermute | solution.py:338
  22.0 9.2 %collective-permute-start.4 = (bf16[2,256,256]{2,1,0:T(8,128)(2,1)S(1)}, bf16[2,256,256]{2,1,0:T(8,128)(2,1)S(1)}, u32[]{:S(2)}, u32[]{:S(2)}) collective-permute-start(bf16[2,256,256]{2,1,0:T(8,128)(2,1)S(1)} %collective-permute-done.1.refs_0_), channel_id=1, source_target_pairs={{0,2},{1,3},{2,0},{3,1},{4,6},{5,7},{6,4},{7,5},{8,10},{9,11},{10,... | collective-permute-start | bytes 786440 | tf_op jit(solution)/shard_map/ppermute | solution.py:338
  24.1 12.2 %collective-permute-start.5 = (bf16[2,256,256]{2,1,0:T(8,128)(2,1)S(1)}, bf16[2,256,256]{2,1,0:T(8,128)(2,1)S(1)}, u32[]{:S(2)}, u32[]{:S(2)}) collective-permute-start(bf16[2,256,256]{2,1,0:T(8,128)(2,1)S(1)} %collective-permute-done.2.refs_1_), channel_id=1, source_target_pairs={{0,2},{1,3},{2,0},{3,1},{4,6},{5,7},{6,4},{7,5},{8,10},{9,11},{10,... | collective-permute-start | bytes 786440 | tf_op jit(solution)/shard_map/ppermute | solution.py:338
  25.5 10.8 %collective-permute-start.7 = (bf16[2,256,256]{2,1,0:T(8,128)(2,1)S(1)}, bf16[2,256,256]{2,1,0:T(8,128)(2,1)S(1)}, u32[]{:S(2)}, u32[]{:S(2)}) collective-permute-start(bf16[2,256,256]{2,1,0:T(8,128)(2,1)S(1)} %collective-permute-done.6.refs_4_), channel_id=1, source_target_pairs={{0,8},{1,9},{2,10},{3,11},{4,12},{5,13},{6,14},{7,15},{8,0},{9,1},... | collective-permute-start | bytes 786440 | tf_op jit(solution)/shard_map/ppermute | solution.py:338

commit v2 on v1

v2 whole, which is shorter than its diff:
```python
import functools

import jax
import jax.numpy as jnp
from jax import lax
from jax.experimental import pallas as pl
from jax.experimental.pallas import tpu as pltpu
from jax.sharding import PartitionSpec as P


ANY = pl.BlockSpec(memory_space=pl.ANY)
SMEM = pl.BlockSpec(memory_space=pltpu.SMEM)
VMEM = pl.BlockSpec(memory_space=pltpu.VMEM)
LANES = 128


def in_hbm(x):
    return pltpu.with_memory_space_constraint(x, pltpu.HBM)


class Plan:
    def __init__(self, rows_n, cols_n, rows_local, cols_local, block, rank, blocks):
        self.rows_n, self.cols_n = rows_n, cols_n
        self.halves = rows_n // 2
        self.window = 2 * rows_local
        self.rows_local, self.cols_local = rows_local, cols_local
        self.row_cap = self.window // rows_n
        self.col_cap = self.window // cols_n
        self.half_cap = self.row_cap // 2
        self.unit = self.half_cap * block // 2
        self.block, self.rank, self.blocks = block, rank, blocks
        self.step = cols_local * (block // LANES)
        assert cols_n == 2 * rows_n and self.half_cap == self.col_cap

    def here(self):
        row, col = lax.axis_index("row"), lax.axis_index("col")
        return row, col, row // 2, row % 2

    def parity(self, group, col):
        return (col // self.rows_n + (col // self.halves) % 2 + 2 * group // self.halves) % 2

    def owns_diag(self, group, col):
        return (col % self.rows_n) // 2 == group


def read_map(plan, block_map, valid_rows, child, group, count, where=None):
    for slot in range(plan.window):
        count[slot] = 0
        if where is not None:
            where[slot] = 0
    for i in range(plan.blocks):
        spot = block_map[child, group * plan.blocks + i] - group * plan.window
        count[spot] = valid_rows[child, group * plan.blocks + i]
        if where is not None:
            where[spot] = i


def keep_rows(x, count, start=0):
    pos = lax.broadcasted_iota(jnp.int32, (x.shape[0], 1), 0) + start
    return jnp.where(pos < count, x, jnp.zeros_like(x))


def keep_both(x, count):
    pos = lax.broadcasted_iota(jnp.int32, (1, x.shape[1]), 1)
    return jnp.where(pos < count, keep_rows(x, count), jnp.zeros_like(x))


def matmul(x, y):
    return jnp.dot(x, y, preferred_element_type=jnp.float32)


def project(x, mixer):
    dims = (((0,), (1,)), ((), ()))
    return lax.dot_general(mixer, x, dims, preferred_element_type=jnp.float32).astype(x.dtype)


def pack_rows_kernel(plan, block_map, valid_rows, generators, *refs):
    outs, (map_s, valid_s, every, where, count, sems) = refs[:-6], refs[-6:]
    _, col, group, child = plan.here()
    copies = [
        pltpu.make_async_copy(source, target, sems.at[i])
        for i, (source, target) in enumerate(
            ((generators, every), (block_map, map_s), (valid_rows, valid_s)))
    ]
    for copy in copies:
        copy.start()
    copies[1].wait()
    copies[2].wait()
    read_map(plan, map_s, valid_s, child, group, count, where)
    copies[0].wait()
    whole = plan.unit // plan.block
    side = col % 2
    for i, out in enumerate(outs):
        d, k = 1 + i // 2, i % 2
        aim = (group + plan.halves - d) % plan.halves
        target = 2 * aim + (child + k) % 2
        parity = plan.parity(aim, col)
        for j in range(max(whole, 1)):
            slot = (2 * (side * whole + j) + parity) * plan.rows_n + target
            if whole:
                out[pl.ds(j * plan.block, plan.block), :] = keep_rows(every[where[slot]], count[slot])
            else:
                start = pl.multiple_of(side * plan.unit, plan.unit)
                part = every[where[slot], pl.ds(start, plan.unit), :]
                out[...] = keep_rows(part, count[slot], start)


def pack_rest_kernel(plan, block_map, valid_rows, generators, diagonal, coupling, mine, own, *refs):
    outs, (where, count, picked, mixer, sems) = refs[:-5], refs[-5:]
    row, col, group, child = plan.here()
    read_map(plan, block_map, valid_rows, child, group, count, where)
    copies = []

    def go(source, target):
        copies.append(pltpu.make_async_copy(source, target, sems.at[len(copies)]))
        copies[-1].start()

    cols = [s * plan.cols_n + col for s in range(plan.col_cap)]
    mates = [q * plan.rows_n + 2 * group + (child + 1) % 2 for q in range(plan.row_cap)]
    selves = [q * plan.rows_n + row for q in range(plan.row_cap)]
    diags = plan.row_cap + plan.col_cap
    go(coupling.at[child], mixer)
    for s in range(plan.col_cap):
        go(generators.at[where[cols[s]]], picked.at[s])
    for s in range(plan.col_cap):
        go(diagonal.at[where[cols[s]]], mine.at[diags + s])
    for q in range(plan.row_cap):
        go(generators.at[where[mates[q]]], mine.at[q])
    for q in range(plan.row_cap):
        go(generators.at[where[selves[q]]], own.at[q])
    for copy in copies:
        copy.wait()
    for s in range(plan.col_cap):
        mine[plan.row_cap + s] = project(keep_rows(picked[s], count[cols[s]]), mixer[...])
        mine[diags + s] = keep_both(mine[diags + s], count[cols[s]])
    for q in range(plan.row_cap):
        mine[q] = keep_rows(mine[q], count[mates[q]])
        own[q] = keep_rows(own[q], count[selves[q]])
    for i, out in enumerate(outs):
        aim = (group + plan.halves - (i + 1)) % plan.halves
        owns = plan.owns_diag(aim, col)

        @pl.when(owns)
        def _():
            for s in range(plan.col_cap):
                out[s] = mine[diags + s]

        @pl.when(jnp.logical_not(owns))
        def _():
            for s in range(plan.col_cap):
                out[s] = mine[plan.row_cap + s]


def join(plan, target, k, here, there, side):
    first = pl.multiple_of(side * plan.unit, plan.unit)
    second = pl.multiple_of((1 - side) * plan.unit, plan.unit)
    target[k, pl.ds(first, plan.unit), :] = here[...]
    target[k, pl.ds(second, plan.unit), :] = there[...]


def project_kernel(plan, coupling, *refs):
    n = 4 * (plan.halves - 1)
    parts, formed, fars = refs[:n], refs[n], refs[n + 1:]
    _, col, _, child = plan.here()
    for d in range(1, plan.halves):
        for k in range(2):
            here, there = parts[4 * (d - 1) + 2 * k: 4 * (d - 1) + 2 * k + 2]
            join(plan, fars[d - 1], k, here, there, col % 2)
            mixer = coupling[(child + k) % 2]
            for j in range(plan.half_cap):
                rows = fars[d - 1][k, pl.ds(j * plan.block, plan.block), :]
                formed[d - 1, k, j] = project(rows, mixer)


def add_tile(plan, total, a, b, value):
    for part in range(plan.block // LANES):
        rows = pl.ds(part * plan.cols_local + b, plan.block, stride=plan.step)
        total[a, rows, :] += value[:, part * LANES:(part + 1) * LANES]


def add_tiles(plan, total, steps, b, value):
    for j, a in enumerate(steps):
        add_tile(plan, total, a, b, value[j * plan.block:(j + 1) * plan.block])


def begin_kernel(plan, own, mine, theirs, front, total, sems):
    row, col, group, _ = plan.here()
    reads = []
    for i in range(plan.rows_local):
        a = (group * plan.row_cap + i) % plan.rows_local
        reads.append(pltpu.make_async_copy(front.at[a], total.at[a], sems.at[i]))
        reads[-1].start()
    for copy in reads[: plan.row_cap]:
        copy.wait()
    rows = plan.row_cap * plan.block
    steps = [group * plan.row_cap + q for q in range(plan.row_cap)]
    left = [own[...].reshape(rows, plan.rank),
            theirs[pl.ds(0, plan.row_cap)].reshape(rows, plan.rank)]
    for s in range(plan.col_cap):
        value = matmul(left[0], mine[plan.row_cap + s]) + matmul(left[1], theirs[plan.row_cap + s])
        add_tiles(plan, total, steps, group * plan.col_cap + s, value)

    @pl.when(row == col % plan.rows_n)
    def _():
        for s in range(plan.col_cap):
            a = group * plan.row_cap + 2 * s + col // plan.rows_n
            slot = plan.row_cap + plan.col_cap + s
            value = mine[slot].astype(jnp.float32) + theirs[slot].astype(jnp.float32)
            add_tile(plan, total, a, group * plan.col_cap + s, value)

    for copy in reads[plan.row_cap:]:
        copy.wait()


def write_out(total, out, steps, sems, copies):
    for a in steps:
        copies.append(pltpu.make_async_copy(total.at[a], out.at[a], sems.at[len(copies)]))
        copies[-1].start()


def middle_kernel(plan, own, mine, theirs, formed, formed_too, *refs):
    halves, half = plan.halves, plan.half_cap
    groups = [refs[3 * i: 3 * i + 3] for i in range(halves - 1)]
    _, out, total, right, sems = refs[3 * (halves - 1):]
    row, col, group, _ = plan.here()
    owns = plan.owns_diag(group, col)
    main = row == col % plan.rows_n

    def choose(pick):
        for e in range(1, halves):
            for k in range(2):
                for s in range(plan.col_cap):
                    right[e, k, s] = pick(e, k, s)

    @pl.when(main)
    def _():
        choose(lambda e, k, s: formed[e - 1, k, s])

    @pl.when(owns & jnp.logical_not(main))
    def _():
        choose(lambda e, k, s: formed_too[e - 1, 1 - k, s])

    @pl.when(jnp.logical_not(owns))
    def _():
        choose(lambda e, k, s: groups[e - 1][k][s])

    for s in range(plan.col_cap):
        right[0, 0, s] = mine[plan.row_cap + s]
        right[0, 1, s] = theirs[plan.row_cap + s]
    copies = []
    rows = half * plan.block
    for g in range(2):
        steps = [group * plan.row_cap + g * half + j for j in range(half)]
        left = [own[pl.ds(g * half, half)].reshape(rows, plan.rank),
                theirs[pl.ds(g * half, half)].reshape(rows, plan.rank)]
        for e in range(1, halves):
            for s in range(plan.col_cap):
                value = matmul(left[0], right[e, 0, s]) + matmul(left[1], right[e, 1, s])
                add_tiles(plan, total, steps, (group + e) % halves * plan.col_cap + s, value)
        write_out(total, out, steps, sems, copies)
    parity = plan.parity(group, col)
    for d in range(1, halves):
        direct, swapped, far = groups[d - 1]
        aim = (group + d) % halves
        steps = [aim * plan.row_cap + 2 * j + parity for j in range(half)]

        @pl.when(main)
        def _():
            for s in range(plan.col_cap):
                value = direct[s].astype(jnp.float32) + swapped[s].astype(jnp.float32)
                add_tile(plan, total, steps[s], aim * plan.col_cap + s, value)

        for e in range(halves):
            for s in range(plan.col_cap):
                value = matmul(far[0], right[e, 0, s]) + matmul(far[1], right[e, 1, s])
                add_tiles(plan, total, steps, (group + e) % halves * plan.col_cap + s, value)
        write_out(total, out, steps, sems, copies)
    for copy in copies:
        copy.wait()


def last_kernel(plan, right, *refs):
    halves, half = plan.halves, plan.half_cap
    n = 4 * (halves - 1)
    parts, (total_in, out_in, out, total, far, sems) = refs[:n], refs[n:]
    _, col, group, _ = plan.here()
    odd = 1 - plan.parity(group, col)
    copies = []
    for d in range(1, halves):
        aim = (group + d) % halves
        steps = [aim * plan.row_cap + 2 * j + odd for j in range(half)]
        for k in range(2):
            here, there = parts[4 * (d - 1) + 2 * k: 4 * (d - 1) + 2 * k + 2]
            join(plan, far, k, here, there, col % 2)
        for e in range(halves):
            for s in range(plan.col_cap):
                value = matmul(far[0], right[e, 0, s]) + matmul(far[1], right[e, 1, s])
                add_tiles(plan, total, steps, (group + e) % halves * plan.col_cap + s, value)
        write_out(total, out, steps, sems, copies)
    for copy in copies:
        copy.wait()


def shards(rows_n, cols_n, parent_front, generators, diagonal_blocks, coupling, block_map, valid_rows):
    rows_local, block, cols_local, width = parent_front.shape
    blocks, _, rank = generators.shape
    plan = Plan(rows_n, cols_n, rows_local, cols_local, block, rank, blocks)
    halves, row_cap, col_cap, half = plan.halves, plan.row_cap, plan.col_cap, plan.half_cap
    dt = generators.dtype
    parts = width // LANES
    table = pltpu.SMEM((plan.window,), jnp.int32)
    turns = range(1, halves)

    def shape(*lead):
        return jax.ShapeDtypeStruct(lead + (block, rank), dt)

    unit = jax.ShapeDtypeStruct((plan.unit, rank), dt)
    joined = jax.ShapeDtypeStruct((2, half * block, rank), dt)

    def sems(n):
        return pltpu.SemaphoreType.DMA((n,))

    def call(kernel, out_shape, in_specs, out_specs, scratch, mib, args, aliases={}):
        return pl.pallas_call(
            functools.partial(kernel, plan), out_shape=out_shape, in_specs=in_specs,
            out_specs=out_specs, scratch_shapes=scratch,
            input_output_aliases=aliases,
            compiler_params=pltpu.CompilerParams(vmem_limit_bytes=mib << 20))(*args)

    front = parent_front.reshape(rows_local, block, cols_local, parts, LANES)
    front = front.transpose(0, 1, 3, 2, 4).reshape(rows_local, block * plan.step, LANES)
    mixers = coupling
    block_map, valid_rows, generators, diagonal_blocks, coupling, front = map(
        in_hbm, (block_map, valid_rows, generators, diagonal_blocks, coupling, front))

    def send(x, move):
        pairs = [
            (row * cols_n + col, to_row * cols_n + to_col)
            for row in range(rows_n)
            for col in range(cols_n)
            for to_row, to_col in [move(row, col)]
        ]
        return lax.ppermute(x, ("row", "col"), pairs)

    def across(d, k):
        return lambda row, col: (2 * ((row // 2 - d) % halves) + (row % 2 + k) % 2, col)

    def partner(row, col):
        return row ^ 1, col

    def beside(row, col):
        return row, col ^ 1

    def along(row, col):
        return row, col ^ halves

    flows = [(d, k) for d in turns for k in range(2)]
    rows_out = call(
        pack_rows_kernel, [unit] * len(flows), [ANY] * 3,
        [VMEM] * len(flows),
        [pltpu.SMEM(block_map.shape, jnp.int32), pltpu.SMEM(block_map.shape, jnp.int32),
         pltpu.VMEM(generators.shape, dt), table, table, sems(3)], 8,
        (block_map, valid_rows, generators))
    near, beside_, along_, far_ = {}, {}, {}, {}
    for (d, k), x in zip(flows, rows_out):
        near[d, k] = send(x, across(d, k))
    mine, own, *cols_out = call(
        pack_rest_kernel,
        [shape(row_cap + 2 * col_cap), shape(row_cap)] + [shape(col_cap)] * (halves - 1),
        [SMEM, SMEM, ANY, ANY, ANY], [VMEM] * (halves + 1),
        [table, table, pltpu.VMEM((col_cap, block, rank), dt), pltpu.VMEM((rank, rank), dt),
         sems(1 + 2 * col_cap + 2 * row_cap)], 12,
        (block_map, valid_rows, generators, diagonal_blocks, coupling))
    direct = {d: send(cols_out[d - 1], across(d, 0)) for d in turns}
    theirs = send(mine, partner)
    for d, k in flows:
        beside_[d, k] = send(near[d, k], beside)
        along_[d, k] = send(near[d, k], along)
    total = call(
        begin_kernel, jax.ShapeDtypeStruct(front.shape, front.dtype),
        [VMEM] * 3 + [ANY], VMEM, [sems(rows_local)], 24, (own, mine, theirs, front))
    for d in turns:
        far_[d, 0] = send(beside_[d, 0], along)
        far_[d, 1] = send(along_[d, 1], beside)
    args = (mixers,) + tuple(x[flow] for flow in flows for x in (near, beside_))
    formed, *fars = call(
        project_kernel, [shape(halves - 1, 2, col_cap)] + [joined] * (halves - 1),
        [VMEM] * len(args), [VMEM] * halves, [], 12, args)
    formed_too = send(formed, partner)
    swapped = {d: send(direct[d], partner) for d in turns}
    args = (own, mine, theirs, formed, formed_too) + tuple(
        x for d in turns for x in (direct[d], swapped[d], fars[d - 1])) + (total,)
    whole = jax.ShapeDtypeStruct(front.shape, front.dtype)
    out, total, right = call(
        middle_kernel, [whole, whole, shape(halves, 2, col_cap)],
        [VMEM] * len(args), [ANY, VMEM, VMEM], [sems(rows_local)],
        24, args, {len(args) - 1: 1})
    args = (right,) + tuple(x[flow] for flow in flows for x in (along_, far_)) + (total, out)
    out, _ = call(
        last_kernel, [whole] * 2, [VMEM] * (len(args) - 1) + [ANY], [ANY, VMEM],
        [pltpu.VMEM(joined.shape, dt), sems(rows_local)],
        24, args, {len(args) - 1: 0, len(args) - 2: 1})
    out = out.reshape(rows_local, block, parts, cols_local, LANES)
    return out.transpose(0, 1, 3, 2, 4).reshape(rows_local, block, cols_local, width)


def solution(mesh):
    in_specs = (
        P(None, "row", None, "col"),
        P("row", None, None),
        P("row", None, None),
        P(),
        P(),
        P(),
    )
    out_specs = P(None, "row", None, "col")

    def body(*args):
        return shards(mesh.shape["row"], mesh.shape["col"], *args)

    return jax.shard_map(body, mesh=mesh, in_specs=in_specs, out_specs=out_specs, check_vma=False)
```

time: 42 us -> 42.2 us (level)
  starting transfers between devices: 7.37 us -> 12.5 us
  waiting for transfers between devices: 17.9 us -> 14.2 us
  Pallas kernels: 16.4 us -> 14.3 us
  local copies, waits for them, and re-layouts: 0 us -> 0.95 us
    ppermute x8 -> x12, starting transfers between devices: 7.37 us -> 12.5 us  [send(): return lax.ppermute(x, ('row', 'col'), pairs)]
    ppermute x8 -> x12, waiting for transfers between devices: 17.9 us -> 14.2 us  [send(): return lax.ppermute(x, ('row', 'col'), pairs)]
    pallas_call x5 -> x6, Pallas kernels: 16.4 us -> 14.3 us  [call(): pl.pallas_call(functools.partial(kernel, plan), out_shape=out_shape, in_s...]
    unnamed x0 -> x2, local copies, waits for them, and re-layouts: none -> 0.95 us
  transfers between devices with their start and end apart: 8 -> 12, of which waited for: 5 -> 5; matrix products, arithmetic and copies ran while one was open for 0% -> 0% of each run, Pallas kernels for 21% -> 22%
where the time goes in v2:
time: 42.2 us; the launch traced here: 42 us
  Pallas kernels  14.3 us (34%)
  waiting for transfers between devices  14.2 us (34%)
  starting transfers between devices  12.5 us (30%)
  local copies, waits for them, and re-layouts  0.95 us (2%)
    pallas_call x6, Pallas kernels, call(): pl.pallas_call(functools.partial(kernel, plan), out_shape=out_shape, in_s...  14.3 us
    ppermute x12, waiting for transfers between devices, send(): return lax.ppermute(x, ('row', 'col'), pairs)  14.2 us
    ppermute x12, starting transfers between devices, send(): return lax.ppermute(x, ('row', 'col'), pairs)  12.5 us
    unnamed x2, local copies, waits for them, and re-layouts  0.95 us
  transfers between devices with their start and end apart: 12, of which 5 were waited for; matrix products, arithmetic and copies ran while one was open for 0% of the time, Pallas kernels for 22%

profile of v2, /device:TPU:0, one launch (start us, length us, event | category | flops | bytes accessed | tf_op | source)
XLA Modules:
  0.0 42.0 jit_solution(6903125997182867395)
XLA Ops:
  0.0 2.8 %shard_map.64 = (bf16[8,256,256]{2,1,0:T(8,128)(2,1)S(1)}, bf16[4,256,256]{2,1,0:T(8,128)(2,1)S(1)}, bf16[2,256,256]{2,1,0:T(8,128)(2,1)S(1)}) custom-call(s32[2,24]{1,0:T(2,128)} %block_map.3, s32[2,24]{1,0:T(2,128)} %valid_rows.3, bf16[12,256,256]{2,1,0:T(8,128)(2,1)} %generators.3, bf16[12,256,256]{2,1,0:T(8,128)(2,1)} %diagonal.1, ...), custom_call_target="tpu_custom_call" | custom-call | tf_op jit(solution)/shard_map/pallas_call | solution.py:324
  2.8 0.6 %collective-permute-start = (bf16[8,256,256]{2,1,0:T(8,128)(2,1)S(1)}, bf16[8,256,256]{2,1,0:T(8,128)(2,1)S(1)}, u32[]{:S(2)}, u32[]{:S(2)}) collective-permute-start(bf16[8,256,256]{2,1,0:T(8,128)(2,1)S(1)} %get-tuple-element.17.mine), channel_id=1, source_target_pairs={{0,8},{1,9},{2,10},{3,11},{4,12},{5,13},{6,14},{7,15},{8,0},{9,1},... | collective-permute-start | bytes 3145736 | tf_op jit(solution)/shard_map/ppermute | solution.py:343
  3.4 1.5 %shard_map.65 = (bf16[256,256]{1,0:T(8,128)(2,1)S(1)}, bf16[256,256]{1,0:T(8,128)(2,1)S(1)}) custom-call(s32[2,24]{1,0:T(2,128)} %block_map.3, s32[2,24]{1,0:T(2,128)} %valid_rows.3, bf16[12,256,256]{2,1,0:T(8,128)(2,1)} %generators.3), custom_call_target="tpu_custom_call" | custom-call | tf_op jit(solution)/shard_map/pallas_call | solution.py:324
  4.8 2.6 %collective-permute-start.1 = (bf16[256,256]{1,0:T(8,128)(2,1)S(1)}, bf16[256,256]{1,0:T(8,128)(2,1)S(1)}, u32[]{:S(2)}, u32[]{:S(2)}) collective-permute-start(bf16[256,256]{1,0:T(8,128)(2,1)S(1)} %get-tuple-element.18), channel_id=1, source_target_pairs={{0,16},{1,17},{2,18},{3,19},{4,20},{5,21},{6,22},{7,23},{8,24},{9,... | collective-permute-start | bytes 393224 | tf_op jit(solution)/shard_map/ppermute | solution.py:343
  7.4 0.2 collective-permute-start.3
  7.6 4.2 %collective-permute-done.1.refs_0_ = bf16[256,256]{1,0:T(8,128)(2,1)S(1)} collective-permute-done((bf16[256,256]{1,0:T(8,128)(2,1)S(1)}, bf16[256,256]{1,0:T(8,128)(2,1)S(1)}, u32[]{:S(2)}, u32[]{:S(2)}) %collective-permute-start.1) | collective-permute-done | bytes 131104 | tf_op jit(solution)/shard_map/ppermute | solution.py:343
  11.8 2.0 %collective-permute-start.2 = (bf16[256,256]{1,0:T(8,128)(2,1)S(1)}, bf16[256,256]{1,0:T(8,128)(2,1)S(1)}, u32[]{:S(2)}, u32[]{:S(2)}) collective-permute-start(bf16[256,256]{1,0:T(8,128)(2,1)S(1)} %collective-permute-done.1.refs_0_), channel_id=1, source_target_pairs={{0,1},{1,0},{2,3},{3,2},{4,5},{5,4},{6,7},{7,6},{8,9},{9,8},{10,11... | collective-permute-start | bytes 393224 | tf_op jit(solution)/shard_map/ppermute | solution.py:343
  13.8 0.4 %collective-permute-done.3.refs_2_ = bf16[256,256]{1,0:T(8,128)(2,1)S(1)} collective-permute-done((bf16[256,256]{1,0:T(8,128)(2,1)S(1)}, bf16[256,256]{1,0:T(8,128)(2,1)S(1)}, u32[]{:S(2)}, u32[]{:S(2)}) %collective-permute-start.3) | collective-permute-done | bytes 131104 | tf_op jit(solution)/shard_map/ppermute | solution.py:343
  14.2 1.4 %collective-permute-start.4 = (bf16[256,256]{1,0:T(8,128)(2,1)S(1)}, bf16[256,256]{1,0:T(8,128)(2,1)S(1)}, u32[]{:S(2)}, u32[]{:S(2)}) collective-permute-start(bf16[256,256]{1,0:T(8,128)(2,1)S(1)} %collective-permute-done.3.refs_2_), channel_id=1, source_target_pairs={{0,1},{1,0},{2,3},{3,2},{4,5},{5,4},{6,7},{7,6},{8,9},{9,8},{10,11... | collective-permute-start | bytes 393224 | tf_op jit(solution)/shard_map/ppermute | solution.py:343
  15.6 1.5 %collective-permute-start.6 = (bf16[2,256,256]{2,1,0:T(8,128)(2,1)S(1)}, bf16[2,256,256]{2,1,0:T(8,128)(2,1)S(1)}, u32[]{:S(2)}, u32[]{:S(2)}) collective-permute-start(bf16[2,256,256]{2,1,0:T(8,128)(2,1)S(1)} %get-tuple-element.21), channel_id=1, source_target_pairs={{0,16},{1,17},{2,18},{3,19},{4,20},{5,21},{6,22},{7,23},{8,24},{9,... | collective-permute-start | bytes 786440 | tf_op jit(solution)/shard_map/ppermute | solution.py:343
  17.1 0.0 collective-permute-done.2.refs_1_
  17.1 2.6 %collective-permute-done.4.refs_3_ = bf16[256,256]{1,0:T(8,128)(2,1)S(1)} collective-permute-done((bf16[256,256]{1,0:T(8,128)(2,1)S(1)}, bf16[256,256]{1,0:T(8,128)(2,1)S(1)}, u32[]{:S(2)}, u32[]{:S(2)}) %collective-permute-start.4) | collective-permute-done | bytes 131104 | tf_op jit(solution)/shard_map/ppermute | solution.py:343
  19.7 0.0 copy-start
  19.7 0.9 %copy-done = bf16[2,256,256]{2,1,0:T(8,128)(2,1)S(1)} copy-done((bf16[2,256,256]{2,1,0:T(8,128)(2,1)S(1)}, bf16[2,256,256]{2,1,0:T(8,128)(2,1)}, u32[]{:S(2)}) %copy-start) | copy-done | bytes 262168
  20.7 0.4 shard_map.66
  21.1 0.1 collective-permute-start.5
  21.2 2.7 %collective-permute-done.6.refs_0_ = bf16[2,256,256]{2,1,0:T(8,128)(2,1)S(1)} collective-permute-done((bf16[2,256,256]{2,1,0:T(8,128)(2,1)S(1)}, bf16[2,256,256]{2,1,0:T(8,128)(2,1)S(1)}, u32[]{:S(2)}, u32[]{:S(2)}) %collective-permute-start.6) | collective-permute-done | bytes 262176 | tf_op jit(solution)/shard_map/ppermute | solution.py:343
  23.9 0.0 collective-permute-start.7
  23.9 1.6 %collective-permute-start.10 = (bf16[256,256]{1,0:T(8,128)(2,1)S(1)}, bf16[256,256]{1,0:T(8,128)(2,1)S(1)}, u32[]{:S(2)}, u32[]{:S(2)}) collective-permute-start(bf16[256,256]{1,0:T(8,128)(2,1)S(1)} %collective-permute-done.3.refs_2_), channel_id=1, source_target_pairs={{0,2},{1,3},{2,0},{3,1},{4,6},{5,7},{6,4},{7,5},{8,10},{9,11},{10,... | collective-permute-start | bytes 393224 | tf_op jit(solution)/shard_map/ppermute | solution.py:343
  25.4 0.4 %collective-permute-start.8 = (bf16[256,256]{1,0:T(8,128)(2,1)S(1)}, bf16[256,256]{1,0:T(8,128)(2,1)S(1)}, u32[]{:S(2)}, u32[]{:S(2)}) collective-permute-start(bf16[256,256]{1,0:T(8,128)(2,1)S(1)} %collective-permute-done.1.refs_0_), channel_id=1, source_target_pairs={{0,2},{1,3},{2,0},{3,1},{4,6},{5,7},{6,4},{7,5},{8,10},{9,11},{10,... | collective-permute-start | bytes 393224 | tf_op jit(solution)/shard_map/ppermute | solution.py:343
  25.9 4.3 %collective-permute-done.10.refs_2_ = bf16[256,256]{1,0:T(8,128)(2,1)S(1)} collective-permute-done((bf16[256,256]{1,0:T(8,128)(2,1)S(1)}, bf16[256,256]{1,0:T(8,128)(2,1)S(1)}, u32[]{:S(2)}, u32[]{:S(2)}) %collective-permute-start.10) | collective-permute-done | bytes 131104 | tf_op jit(solution)/shard_map/ppermute | solution.py:343
  30.2 1.6 %collective-permute-start.9 = (bf16[256,256]{1,0:T(8,128)(2,1)S(1)}, bf16[256,256]{1,0:T(8,128)(2,1)S(1)}, u32[]{:S(2)}, u32[]{:S(2)}) collective-permute-start(bf16[256,256]{1,0:T(8,128)(2,1)S(1)} %collective-permute-done.2.refs_1_), channel_id=1, source_target_pairs={{0,2},{1,3},{2,0},{3,1},{4,6},{5,7},{6,4},{7,5},{8,10},{9,11},{10,... | collective-permute-start | bytes 393224 | tf_op jit(solution)/shard_map/ppermute | solution.py:343
  31.8 0.0 collective-permute-done.theirs
  31.8 0.5 %collective-permute-start.11 = (bf16[256,256]{1,0:T(8,128)(2,1)S(1)}, bf16[256,256]{1,0:T(8,128)(2,1)S(1)}, u32[]{:S(2)}, u32[]{:S(2)}) collective-permute-start(bf16[256,256]{1,0:T(8,128)(2,1)S(1)} %collective-permute-done.10.refs_2_), channel_id=1, source_target_pairs={{0,1},{1,0},{2,3},{3,2},{4,5},{5,4},{6,7},{7,6},{8,9},{9,8},{10,11... | collective-permute-start | bytes 393224 | tf_op jit(solution)/shard_map/ppermute | solution.py:343
  32.3 3.5 %shard_map.67.refs_3_ = f32[8,2048,128]{2,1,0:T(8,128)S(1)} custom-call(bf16[4,256,256]{2,1,0:T(8,128)(2,1)S(1)} %get-tuple-element.16.own, bf16[8,256,256]{2,1,0:T(8,128)(2,1)S(1)} %get-tuple-element.17.mine, bf16[8,256,256]{2,1,0:T(8,128)(2,1)S(1)} %collective-permute-done.theirs, f32[8,2048,128]{2,1,0:T(8,128)} %bitcast.10), custom_call_target="tpu_custom_call" | custom-call | tf_op jit(solution)/shard_map/pallas_call | solution.py:324
  35.8 0.0 collective-permute-done.7.refs_1_
  35.8 0.0 collective-permute-done.5.formed_too
  35.8 3.7 %shard_map.68 = (f32[8,2048,128]{2,1,0:T(8,128)}, f32[8,2048,128]{2,1,0:T(8,128)S(1)}, bf16[2,2,2,256,256]{4,3,2,1,0:T(8,128)(2,1)S(1)}) custom-call(bf16[4,256,256]{2,1,0:T(8,128)(2,1)S(1)} %get-tuple-element.16.own, bf16[8,256,256]{2,1,0:T(8,128)(2,1)S(1)} %get-tuple-element.17.mine, ...), custom_call_target="tpu_custom_call", output_to_operand_aliasing={{1}: (8, {})} | custom-call | tf_op jit(solution)/shard_map/pallas_call | solution.py:324
  39.5 0.0 collective-permute-done.8.refs_0_
  39.6 0.0 collective-permute-done.9.refs_1_
  39.6 0.0 collective-permute-done.11.refs_3_
  39.6 2.4 %shard_map.69 = (f32[8,2048,128]{2,1,0:T(8,128)}, f32[8,2048,128]{2,1,0:T(8,128)S(1)}) custom-call(bf16[2,2,2,256,256]{4,3,2,1,0:T(8,128)(2,1)S(1)} %get-tuple-element.23.right, bf16[256,256]{1,0:T(8,128)(2,1)S(1)} %collective-permute-done.8.refs_0_, ...), custom_call_target="tpu_custom_call", output_to_operand_aliasing={{0}: (6, {}), {1}: (5, {})} | custom-call | tf_op jit(solution)/shard_map/pallas_call | solution.py:324
Async XLA Ops:
  2.8 29.0 %collective-permute-start = (bf16[8,256,256]{2,1,0:T(8,128)(2,1)S(1)}, bf16[8,256,256]{2,1,0:T(8,128)(2,1)S(1)}, u32[]{:S(2)}, u32[]{:S(2)}) collective-permute-start(bf16[8,256,256]{2,1,0:T(8,128)(2,1)S(1)} %get-tuple-element.17.mine), channel_id=1, source_target_pairs={{0,8},{1,9},{2,10},{3,11},{4,12},{5,13},{6,14},{7,15},{8,0},{9,1},... | collective-permute-start | bytes 3145736 | tf_op jit(solution)/shard_map/ppermute | solution.py:343
  4.8 6.9 %collective-permute-start.1 = (bf16[256,256]{1,0:T(8,128)(2,1)S(1)}, bf16[256,256]{1,0:T(8,128)(2,1)S(1)}, u32[]{:S(2)}, u32[]{:S(2)}) collective-permute-start(bf16[256,256]{1,0:T(8,128)(2,1)S(1)} %get-tuple-element.18), channel_id=1, source_target_pairs={{0,16},{1,17},{2,18},{3,19},{4,20},{5,21},{6,22},{7,23},{8,24},{9,... | collective-permute-start | bytes 393224 | tf_op jit(solution)/shard_map/ppermute | solution.py:343
  7.4 6.8 %collective-permute-start.3 = (bf16[256,256]{1,0:T(8,128)(2,1)S(1)}, bf16[256,256]{1,0:T(8,128)(2,1)S(1)}, u32[]{:S(2)}, u32[]{:S(2)}) collective-permute-start(bf16[256,256]{1,0:T(8,128)(2,1)S(1)} %get-tuple-element.19), channel_id=1, source_target_pairs={{0,24},{1,25},{2,26},{3,27},{4,28},{5,29},{6,30},{7,31},{8,16},{9,... | collective-permute-start | bytes 393224 | tf_op jit(solution)/shard_map/ppermute | solution.py:343
  11.8 5.4 %collective-permute-start.2 = (bf16[256,256]{1,0:T(8,128)(2,1)S(1)}, bf16[256,256]{1,0:T(8,128)(2,1)S(1)}, u32[]{:S(2)}, u32[]{:S(2)}) collective-permute-start(bf16[256,256]{1,0:T(8,128)(2,1)S(1)} %collective-permute-done.1.refs_0_), channel_id=1, source_target_pairs={{0,1},{1,0},{2,3},{3,2},{4,5},{5,4},{6,7},{7,6},{8,9},{9,8},{10,11... | collective-permute-start | bytes 393224 | tf_op jit(solution)/shard_map/ppermute | solution.py:343
  14.2 5.5 %collective-permute-start.4 = (bf16[256,256]{1,0:T(8,128)(2,1)S(1)}, bf16[256,256]{1,0:T(8,128)(2,1)S(1)}, u32[]{:S(2)}, u32[]{:S(2)}) collective-permute-start(bf16[256,256]{1,0:T(8,128)(2,1)S(1)} %collective-permute-done.3.refs_2_), channel_id=1, source_target_pairs={{0,1},{1,0},{2,3},{3,2},{4,5},{5,4},{6,7},{7,6},{8,9},{9,8},{10,11... | collective-permute-start | bytes 393224 | tf_op jit(solution)/shard_map/ppermute | solution.py:343
  15.6 8.2 %collective-permute-start.6 = (bf16[2,256,256]{2,1,0:T(8,128)(2,1)S(1)}, bf16[2,256,256]{2,1,0:T(8,128)(2,1)S(1)}, u32[]{:S(2)}, u32[]{:S(2)}) collective-permute-start(bf16[2,256,256]{2,1,0:T(8,128)(2,1)S(1)} %get-tuple-element.21), channel_id=1, source_target_pairs={{0,16},{1,17},{2,18},{3,19},{4,20},{5,21},{6,22},{7,23},{8,24},{9,... | collective-permute-start | bytes 786440 | tf_op jit(solution)/shard_map/ppermute | solution.py:343
  19.7 1.0 %copy-start = (bf16[2,256,256]{2,1,0:T(8,128)(2,1)S(1)}, bf16[2,256,256]{2,1,0:T(8,128)(2,1)}, u32[]{:S(2)}) copy-start(bf16[2,256,256]{2,1,0:T(8,128)(2,1)} %coupling.3) | copy-start | bytes 786436
  21.1 14.8 %collective-permute-start.5 = (bf16[1,2,2,256,256]{4,3,2,1,0:T(8,128)(2,1)S(1)}, bf16[1,2,2,256,256]{4,3,2,1,0:T(8,128)(2,1)S(1)}, u32[]{:S(2)}, u32[]{:S(2)}) collective-permute-start(bf16[1,2,2,256,256]{4,3,2,1,0:T(8,128)(2,1)S(1)} %get-tuple-element.20.formed), channel_id=1, source_target_pairs={{0,8},{1,9},{2,10},{3,11},{4,12},{5,13},{6,14},{7,15},{8,0},{9,1},... | collective-permute-start | bytes 1572872 | tf_op jit(solution)/shard_map/ppermute | solution.py:343
  23.9 12.0 %collective-permute-start.7 = (bf16[2,256,256]{2,1,0:T(8,128)(2,1)S(1)}, bf16[2,256,256]{2,1,0:T(8,128)(2,1)S(1)}, u32[]{:S(2)}, u32[]{:S(2)}) collective-permute-start(bf16[2,256,256]{2,1,0:T(8,128)(2,1)S(1)} %collective-permute-done.6.refs_0_), channel_id=1, source_target_pairs={{0,8},{1,9},{2,10},{3,11},{4,12},{5,13},{6,14},{7,15},{8,0},{9,1},... | collective-permute-start | bytes 786440 | tf_op jit(solution)/shard_map/ppermute | solution.py:343
  23.9 6.4 %collective-permute-start.10 = (bf16[256,256]{1,0:T(8,128)(2,1)S(1)}, bf16[256,256]{1,0:T(8,128)(2,1)S(1)}, u32[]{:S(2)}, u32[]{:S(2)}) collective-permute-start(bf16[256,256]{1,0:T(8,128)(2,1)S(1)} %collective-permute-done.3.refs_2_), channel_id=1, source_target_pairs={{0,2},{1,3},{2,0},{3,1},{4,6},{5,7},{6,4},{7,5},{8,10},{9,11},{10,... | collective-permute-start | bytes 393224 | tf_op jit(solution)/shard_map/ppermute | solution.py:343
  25.4 14.1 %collective-permute-start.8 = (bf16[256,256]{1,0:T(8,128)(2,1)S(1)}, bf16[256,256]{1,0:T(8,128)(2,1)S(1)}, u32[]{:S(2)}, u32[]{:S(2)}) collective-permute-start(bf16[256,256]{1,0:T(8,128)(2,1)S(1)} %collective-permute-done.1.refs_0_), channel_id=1, source_target_pairs={{0,2},{1,3},{2,0},{3,1},{4,6},{5,7},{6,4},{7,5},{8,10},{9,11},{10,... | collective-permute-start | bytes 393224 | tf_op jit(solution)/shard_map/ppermute | solution.py:343
  30.2 9.3 %collective-permute-start.9 = (bf16[256,256]{1,0:T(8,128)(2,1)S(1)}, bf16[256,256]{1,0:T(8,128)(2,1)S(1)}, u32[]{:S(2)}, u32[]{:S(2)}) collective-permute-start(bf16[256,256]{1,0:T(8,128)(2,1)S(1)} %collective-permute-done.2.refs_1_), channel_id=1, source_target_pairs={{0,2},{1,3},{2,0},{3,1},{4,6},{5,7},{6,4},{7,5},{8,10},{9,11},{10,... | collective-permute-start | bytes 393224 | tf_op jit(solution)/shard_map/ppermute | solution.py:343
  31.8 7.8 %collective-permute-start.11 = (bf16[256,256]{1,0:T(8,128)(2,1)S(1)}, bf16[256,256]{1,0:T(8,128)(2,1)S(1)}, u32[]{:S(2)}, u32[]{:S(2)}) collective-permute-start(bf16[256,256]{1,0:T(8,128)(2,1)S(1)} %collective-permute-done.10.refs_2_), channel_id=1, source_target_pairs={{0,1},{1,0},{2,3},{3,2},{4,5},{5,4},{6,7},{7,6},{8,9},{9,8},{10,11... | collective-permute-start | bytes 393224 | tf_op jit(solution)/shard_map/ppermute | solution.py:343

commit v3 on v2

v3 whole, which is shorter than its diff:
```python
import functools

import jax
import jax.numpy as jnp
from jax import lax
from jax.experimental import pallas as pl
from jax.experimental.pallas import tpu as pltpu
from jax.sharding import PartitionSpec as P


ANY = pl.BlockSpec(memory_space=pl.ANY)
SMEM = pl.BlockSpec(memory_space=pltpu.SMEM)
VMEM = pl.BlockSpec(memory_space=pltpu.VMEM)
LANES = 128
PIECES = 4


def in_hbm(x):
    return pltpu.with_memory_space_constraint(x, pltpu.HBM)


class Plan:
    def __init__(self, rows_n, cols_n, rows_local, cols_local, block, rank, blocks):
        self.rows_n, self.cols_n = rows_n, cols_n
        self.halves = rows_n // 2
        self.window = 2 * rows_local
        self.rows_local, self.cols_local = rows_local, cols_local
        self.row_cap = self.window // rows_n
        self.col_cap = self.window // cols_n
        self.half_cap = self.row_cap // 2
        self.unit = self.half_cap * block // 2
        self.block, self.rank, self.blocks = block, rank, blocks
        self.step = cols_local * (block // LANES)
        assert cols_n == 2 * rows_n and self.half_cap == self.col_cap

    def here(self):
        row, col = lax.axis_index("row"), lax.axis_index("col")
        return row, col, row // 2, row % 2

    def parity(self, group, col):
        return (col // self.rows_n + (col // self.halves) % 2 + 2 * group // self.halves) % 2

    def owns_diag(self, group, col):
        return (col % self.rows_n) // 2 == group


def read_map(plan, block_map, valid_rows, child, group, count, where=None):
    for slot in range(plan.window):
        count[slot] = 0
        if where is not None:
            where[slot] = 0
    for i in range(plan.blocks):
        spot = block_map[child, group * plan.blocks + i] - group * plan.window
        count[spot] = valid_rows[child, group * plan.blocks + i]
        if where is not None:
            where[spot] = i


def keep_rows(x, count, start=0):
    pos = lax.broadcasted_iota(jnp.int32, (x.shape[0], 1), 0) + start
    return jnp.where(pos < count, x, jnp.zeros_like(x))


def keep_both(x, count):
    pos = lax.broadcasted_iota(jnp.int32, (1, x.shape[1]), 1)
    return jnp.where(pos < count, keep_rows(x, count), jnp.zeros_like(x))


def matmul(x, y):
    return jnp.dot(x, y, preferred_element_type=jnp.float32)


def project(x, mixer):
    dims = (((0,), (1,)), ((), ()))
    return lax.dot_general(mixer, x, dims, preferred_element_type=jnp.float32).astype(x.dtype)


def pack_rows_kernel(plan, block_map, valid_rows, generators, coupling, every, mixers, *refs):
    outs, (map_s, valid_s, where, count, sems) = refs[:-5], refs[-5:]
    _, col, group, child = plan.here()
    copies = [
        pltpu.make_async_copy(source, target, sems.at[i])
        for i, (source, target) in enumerate(
            ((generators, every), (block_map, map_s), (valid_rows, valid_s), (coupling, mixers)))
    ]
    for copy in copies:
        copy.start()
    copies[1].wait()
    copies[2].wait()
    read_map(plan, map_s, valid_s, child, group, count, where)
    copies[0].wait()
    whole = plan.unit // plan.block
    side = col % 2
    for i, out in enumerate(outs):
        d, k = 1 + i // 2, i % 2
        aim = (group + plan.halves - d) % plan.halves
        target = 2 * aim + (child + k) % 2
        parity = plan.parity(aim, col)
        for j in range(max(whole, 1)):
            slot = (2 * (side * whole + j) + parity) * plan.rows_n + target
            if whole:
                out[pl.ds(j * plan.block, plan.block), :] = keep_rows(every[where[slot]], count[slot])
            else:
                start = pl.multiple_of(side * plan.unit, plan.unit)
                part = every[where[slot], pl.ds(start, plan.unit), :]
                out[...] = keep_rows(part, count[slot], start)
    copies[3].wait()


def pack_rest_kernel(plan, block_map, valid_rows, every, mixers, diagonal, front,
                     mine, own, base, *refs):
    outs, (map_s, valid_s, where, count, sems) = refs[:-5], refs[-5:]
    row, col, group, child = plan.here()
    diags = plan.row_cap + plan.col_cap
    copies = [
        pltpu.make_async_copy(source, target, sems.at[i])
        for i, (source, target) in enumerate(
            ((block_map, map_s), (valid_rows, valid_s),
             (front.at[pl.ds(group * plan.row_cap, plan.row_cap)], base)))
    ]
    for copy in copies:
        copy.start()
    copies[0].wait()
    copies[1].wait()
    read_map(plan, map_s, valid_s, child, group, count, where)
    loads = []
    for s in range(plan.col_cap):
        source = diagonal.at[where[s * plan.cols_n + col]]
        loads.append(pltpu.make_async_copy(source, mine.at[diags + s], sems.at[3 + s]))
        loads[-1].start()
    for s in range(plan.col_cap):
        slot = s * plan.cols_n + col
        masked = keep_rows(every[where[slot]], count[slot])
        mine[plan.row_cap + s] = project(masked, mixers[child])
    for target, to in ((mine, 2 * group + (child + 1) % 2), (own, row)):
        for q in range(plan.row_cap):
            slot = q * plan.rows_n + to
            target[q] = keep_rows(every[where[slot]], count[slot])
    for s in range(plan.col_cap):
        loads[s].wait()
        mine[diags + s] = keep_both(mine[diags + s], count[s * plan.cols_n + col])
    for i, out in enumerate(outs):
        aim = (group + plan.halves - (i + 1)) % plan.halves
        owns = plan.owns_diag(aim, col)

        @pl.when(owns)
        def _():
            for s in range(plan.col_cap):
                out[s] = mine[diags + s]

        @pl.when(jnp.logical_not(owns))
        def _():
            for s in range(plan.col_cap):
                out[s] = mine[plan.row_cap + s]

    copies[2].wait()


def join(plan, target, k, here, there, side):
    first = pl.multiple_of(side * plan.unit, plan.unit)
    second = pl.multiple_of((1 - side) * plan.unit, plan.unit)
    target[k, pl.ds(first, plan.unit), :] = here[...]
    target[k, pl.ds(second, plan.unit), :] = there[...]


def project_kernel(plan, coupling, *refs):
    turns = plan.halves - 1
    directs, refs = refs[:turns], refs[turns:]
    parts, (formed, leave), fars = refs[: 4 * turns], refs[4 * turns: 4 * turns + 2], refs[4 * turns + 2:]
    row, col, _, child = plan.here()
    main = row == col % plan.rows_n
    for d in range(1, plan.halves):
        for k in range(2):
            here, there = parts[4 * (d - 1) + 2 * k: 4 * (d - 1) + 2 * k + 2]
            join(plan, fars[d - 1], k, here, there, col % 2)

    @pl.when(main)
    def _():
        for d in range(1, plan.halves):
            for k in range(2):
                mixer = coupling[(child + k) % 2]
                for j in range(plan.half_cap):
                    rows = fars[d - 1][k, pl.ds(j * plan.block, plan.block), :]
                    value = project(rows, mixer)
                    formed[d - 1, k, j] = value
                    leave[d - 1, k, j] = value

    @pl.when(jnp.logical_not(main))
    def _():
        for d in range(1, plan.halves):
            for j in range(plan.half_cap):
                leave[d - 1, 0, j] = directs[d - 1][j]


def put_across(plan, base, from_a, total, a, b, value):
    for part in range(plan.block // LANES):
        rows = pl.ds(part * plan.cols_local + b, plan.block, stride=plan.step)
        total[a, rows, :] = base[from_a, rows, :] + value[:, part * LANES:(part + 1) * LANES]


def put_tile(plan, base, total, a, b, value):
    put_across(plan, base, a, total, a, b, value)


def put_tiles(plan, base, total, steps, b, value):
    for j, a in enumerate(steps):
        put_tile(plan, base, total, a, b, value[j * plan.block:(j + 1) * plan.block])


def in_pieces(source, target, sems, copies):
    step = source.shape[0] // PIECES
    for i in range(PIECES):
        part = pl.ds(i * step, step)
        copies.append(pltpu.make_async_copy(source.at[part], target.at[part], sems.at[len(copies)]))
        copies[-1].start()


def begin_kernel(plan, own, mine, theirs, base, front, total, rest, sems):
    row, col, group, _ = plan.here()
    reads = []
    for i in range(plan.rows_local - plan.row_cap):
        a = (group * plan.row_cap + plan.row_cap + i) % plan.rows_local
        in_pieces(front.at[a], rest.at[i], sems, reads)
    rows = plan.row_cap * plan.block
    left = own[...].reshape(rows, plan.rank)
    right = theirs[pl.ds(0, plan.row_cap)].reshape(rows, plan.rank)
    for s in range(plan.col_cap):
        value = matmul(left, mine[plan.row_cap + s]) + matmul(right, theirs[plan.row_cap + s])
        put_tiles(plan, base, total, range(plan.row_cap), group * plan.col_cap + s, value)

    @pl.when(row == col % plan.rows_n)
    def _():
        for s in range(plan.col_cap):
            slot = plan.row_cap + plan.col_cap + s
            value = mine[slot].astype(jnp.float32) + theirs[slot].astype(jnp.float32)
            put_tile(plan, total, total, 2 * s + col // plan.rows_n, group * plan.col_cap + s, value)

    for copy in reads:
        copy.wait()


def even_kernel(plan, mine, theirs, *refs):
    fars, (rest, even) = refs[:-2], refs[-2:]
    half = plan.half_cap
    _, col, group, _ = plan.here()
    parity = plan.parity(group, col)
    for d in range(1, plan.halves):
        far = fars[d - 1]
        for s in range(plan.col_cap):
            value = matmul(far[0], mine[plan.row_cap + s]) + matmul(far[1], theirs[plan.row_cap + s])
            for j in range(half):
                put_across(plan, rest, (d - 1) * plan.row_cap + 2 * j + parity,
                           even, (d - 1) * half + j, group * plan.col_cap + s,
                           value[j * plan.block:(j + 1) * plan.block])


def spread(plan, left, right, base, total, steps, group):
    for e in range(1, plan.halves):
        for s in range(plan.col_cap):
            value = matmul(left(0), right[e, 0, s]) + matmul(left(1), right[e, 1, s])
            put_tiles(plan, base, total, steps, (group + e) % plan.halves * plan.col_cap + s, value)


def middle_kernel(plan, own, mine, theirs, formed, swapped, *refs):
    halves, half, turns = plan.halves, plan.half_cap, plan.halves - 1
    directs, fars = refs[:turns], refs[turns: 2 * turns]
    base, rest, _, _, out, near, even, right, sems = refs[2 * turns:]
    row, col, group, _ = plan.here()
    owns = plan.owns_diag(group, col)
    main = row == col % plan.rows_n

    def choose(pick):
        for e in range(1, halves):
            for k in range(2):
                for s in range(plan.col_cap):
                    right[e, k, s] = pick(e - 1, k, s)

    @pl.when(main)
    def _():
        choose(lambda e, k, s: formed[e, k, s])

    @pl.when(owns & jnp.logical_not(main))
    def _():
        choose(lambda e, k, s: swapped[e, 1 - k, s])

    @pl.when(jnp.logical_not(owns))
    def _():
        choose(lambda e, k, s: swapped[e, 0, s] if k else directs[e][s])

    for s in range(plan.col_cap):
        right[0, 0, s] = mine[plan.row_cap + s]
        right[0, 1, s] = theirs[plan.row_cap + s]
    rows = half * plan.block
    copies = []
    for g in range(2):
        def left(k):
            return (own, theirs)[k][pl.ds(g * half, half)].reshape(rows, plan.rank)

        spread(plan, left, right, base, near, [g * half + j for j in range(half)], group)
        for q in range(half if g == 0 else 0):
            in_pieces(near.at[q], out.at[group * plan.row_cap + q], sems, copies)
    parity = plan.parity(group, col)
    for d in range(1, halves):
        def left(k):
            return fars[d - 1][k]

        first = (d - 1) * plan.row_cap

        @pl.when(row >= 0)
        def _():
            for e in range(1, halves):
                for s in range(plan.col_cap):
                    value = matmul(left(0), right[e, 0, s]) + matmul(left(1), right[e, 1, s])
                    b = (group + e) % halves * plan.col_cap + s
                    for j in range(half):
                        put_across(plan, rest, first + 2 * j + parity, even, (d - 1) * half + j, b,
                                   value[j * plan.block:(j + 1) * plan.block])

        @pl.when(main)
        def _():
            for s in range(plan.col_cap):
                value = directs[d - 1][s].astype(jnp.float32) + swapped[d - 1, 0, s].astype(jnp.float32)
                b = (group + d) % halves * plan.col_cap + s
                put_tile(plan, even, even, (d - 1) * half + s, b, value)
    for copy in copies:
        copy.wait()


def last_kernel(plan, right, *refs):
    halves, half, turns = plan.halves, plan.half_cap, plan.halves - 1
    parts, (rest, near, even, out_in, out, odd, far, sems) = refs[: 4 * turns], refs[4 * turns:]
    _, col, group, _ = plan.here()
    parity = plan.parity(group, col)
    copies = []

    def write(source, a):
        in_pieces(source, out.at[a], sems, copies)

    for q in range(half, plan.row_cap):
        write(near.at[q], group * plan.row_cap + q)
    for d in range(1, halves):
        for j in range(half):
            a = (group + d) % halves * plan.row_cap + 2 * j + parity
            write(even.at[(d - 1) * half + j], a)
    for d in range(1, halves):
        for k in range(2):
            here, there = parts[4 * (d - 1) + 2 * k: 4 * (d - 1) + 2 * k + 2]
            join(plan, far, k, here, there, col % 2)
        for j in range(half):
            for e in range(halves):
                for s in range(plan.col_cap):
                    rows = pl.ds(j * plan.block, plan.block)
                    value = matmul(far[0, rows, :], right[e, 0, s])
                    value += matmul(far[1, rows, :], right[e, 1, s])
                    b = (group + e) % halves * plan.col_cap + s
                    put_across(plan, rest, (d - 1) * plan.row_cap + 2 * j + 1 - parity,
                               odd, (d - 1) * half + j, b, value)
            a = (group + d) % halves * plan.row_cap + 2 * j + 1 - parity
            write(odd.at[(d - 1) * half + j], a)
    for copy in copies:
        copy.wait()


def shards(rows_n, cols_n, parent_front, generators, diagonal_blocks, coupling, block_map, valid_rows):
    rows_local, block, cols_local, width = parent_front.shape
    blocks, _, rank = generators.shape
    plan = Plan(rows_n, cols_n, rows_local, cols_local, block, rank, blocks)
    halves, row_cap, col_cap, half = plan.halves, plan.row_cap, plan.col_cap, plan.half_cap
    dt = generators.dtype
    parts = width // LANES
    table = pltpu.SMEM((plan.window,), jnp.int32)
    turns = range(1, halves)

    def shape(*lead):
        return jax.ShapeDtypeStruct(lead + (block, rank), dt)

    unit = jax.ShapeDtypeStruct((plan.unit, rank), dt)
    joined = jax.ShapeDtypeStruct((2, half * block, rank), dt)

    def sems(n):
        return pltpu.SemaphoreType.DMA((n,))

    def call(kernel, out_shape, in_specs, out_specs, scratch, mib, args, aliases={}):
        return pl.pallas_call(
            functools.partial(kernel, plan), out_shape=out_shape, in_specs=in_specs,
            out_specs=out_specs, scratch_shapes=scratch,
            input_output_aliases=aliases,
            compiler_params=pltpu.CompilerParams(vmem_limit_bytes=mib << 20))(*args)

    front = parent_front.reshape(rows_local, block, cols_local, parts, LANES)
    front = front.transpose(0, 1, 3, 2, 4).reshape(rows_local, block * plan.step, LANES)
    block_map, valid_rows, generators, diagonal_blocks, coupling, front = map(
        in_hbm, (block_map, valid_rows, generators, diagonal_blocks, coupling, front))

    def strip(n):
        return jax.ShapeDtypeStruct((n,) + front.shape[1:], front.dtype)

    def send(x, move):
        pairs = [
            (row * cols_n + col, to_row * cols_n + to_col)
            for row in range(rows_n)
            for col in range(cols_n)
            for to_row, to_col in [move(row, col)]
        ]
        return lax.ppermute(x, ("row", "col"), pairs)

    def across(d, k):
        return lambda row, col: (2 * ((row // 2 - d) % halves) + (row % 2 + k) % 2, col)

    def partner(row, col):
        return row ^ 1, col

    def beside(row, col):
        return row, col ^ 1

    def along(row, col):
        return row, col ^ halves

    flows = [(d, k) for d in turns for k in range(2)]
    maps = [pltpu.SMEM(block_map.shape, jnp.int32)] * 2 + [table] * 2
    every, mixers, *rows_out = call(
        pack_rows_kernel, [shape(blocks), shape(2)] + [unit] * len(flows), [ANY] * 4,
        [VMEM] * (2 + len(flows)), maps + [sems(4)], 8,
        (block_map, valid_rows, generators, coupling))
    near, beside_, along_, far_ = {}, {}, {}, {}
    for (d, k), x in zip(flows, rows_out):
        near[d, k] = send(x, across(d, k))
    mine, own, base, *cols_out = call(
        pack_rest_kernel,
        [shape(row_cap + 2 * col_cap), shape(row_cap), strip(row_cap)] + [shape(col_cap)] * (halves - 1),
        [ANY, ANY, VMEM, VMEM, ANY, ANY], [VMEM] * (halves + 2), maps + [sems(3 + col_cap)], 12,
        (block_map, valid_rows, every, mixers, diagonal_blocks, front))
    direct = {d: send(cols_out[d - 1], across(d, 0)) for d in turns}
    theirs = send(mine, partner)
    for d, k in flows:
        beside_[d, k] = send(near[d, k], beside)
        along_[d, k] = send(near[d, k], along)
    for d in turns:
        far_[d, 0] = send(beside_[d, 0], along)
        far_[d, 1] = send(along_[d, 1], beside)
    others = rows_local - row_cap
    args = (own, mine, theirs, base, front)
    near_rows, rest = call(
        begin_kernel, [strip(row_cap), strip(others)],
        [VMEM] * 4 + [ANY], [VMEM] * 2, [sems(others * PIECES)], 12, args)
    args = (mixers,) + tuple(direct[d] for d in turns) + tuple(
        x[flow] for flow in flows for x in (near, beside_))
    formed, leave, *fars = call(
        project_kernel, [shape(halves - 1, 2, col_cap)] * 2 + [joined] * (halves - 1),
        [VMEM] * len(args), [VMEM] * (1 + halves), [], 12, args)
    swapped = send(leave, partner)
    args = (mine, theirs, *fars, rest)
    even = call(even_kernel, strip(others // 2), [VMEM] * len(args), VMEM, [], 12, args)
    args = (own, mine, theirs, formed, swapped, *(direct[d] for d in turns), *fars,
            base, rest, near_rows, even)
    n = len(args)
    out, near_rows, even, right = call(
        middle_kernel,
        [strip(rows_local), strip(row_cap), strip(others // 2), shape(halves, 2, col_cap)],
        [VMEM] * n, [ANY] + [VMEM] * 3, [sems(half * PIECES)], 12, args, {n - 2: 1, n - 1: 2})
    args = (right,) + tuple(x[flow] for flow in flows for x in (along_, far_)) + (
        rest, near_rows, even, out)
    out = call(
        last_kernel, strip(rows_local), [VMEM] * (len(args) - 1) + [ANY], ANY,
        [pltpu.VMEM((others // 2,) + front.shape[1:], front.dtype),
         pltpu.VMEM(joined.shape, dt), sems((others + half) * PIECES)], 16, args, {len(args) - 1: 0})
    out = out.reshape(rows_local, block, parts, cols_local, LANES)
    return out.transpose(0, 1, 3, 2, 4).reshape(rows_local, block, cols_local, width)


def solution(mesh):
    in_specs = (
        P(None, "row", None, "col"),
        P("row", None, None),
        P("row", None, None),
        P(),
        P(),
        P(),
    )
    out_specs = P(None, "row", None, "col")

    def body(*args):
        return shards(mesh.shape["row"], mesh.shape["col"], *args)

    return jax.shard_map(body, mesh=mesh, in_specs=in_specs, out_specs=out_specs, check_vma=False)
```

time: 42.2 us -> 44.3 us (1.050)
  waiting for transfers between devices: 14.2 us -> 17.2 us
  starting transfers between devices: 12.5 us -> 13.5 us
  local copies, waits for them, and re-layouts: 0.95 us -> 0 us
  Pallas kernels: 14.3 us -> 13.4 us
    ppermute x12 -> x11, waiting for transfers between devices: 14.2 us -> 17.2 us  [send(): return lax.ppermute(x, ('row', 'col'), pairs)]
    ppermute x12 -> x11, starting transfers between devices: 12.5 us -> 13.5 us  [send(): return lax.ppermute(x, ('row', 'col'), pairs)]
    unnamed x2 -> x0, local copies, waits for them, and re-layouts: 0.95 us -> none
    pallas_call x6 -> x7, Pallas kernels: 14.3 us -> 13.4 us  [call(): pl.pallas_call(functools.partial(kernel, plan), out_shape=out_shape, in_s...]
  transfers between devices with their start and end apart: 12 -> 11, of which waited for: 5 -> 5; matrix products, arithmetic and copies ran while one was open for 0% -> 0% of each run, Pallas kernels for 22% -> 14%
where the time goes in v3:
time: 44.3 us; the launch traced here: 44.1 us
  waiting for transfers between devices  17.2 us (39%)
  starting transfers between devices  13.5 us (30%)
  Pallas kernels  13.4 us (30%)
    ppermute x11, waiting for transfers between devices, send(): return lax.ppermute(x, ('row', 'col'), pairs)  17.2 us
    ppermute x11, starting transfers between devices, send(): return lax.ppermute(x, ('row', 'col'), pairs)  13.5 us
    pallas_call x7, Pallas kernels, call(): pl.pallas_call(functools.partial(kernel, plan), out_shape=out_shape, in_s...  13.4 us
  transfers between devices with their start and end apart: 11, of which 5 were waited for; matrix products, arithmetic and copies ran while one was open for 0% of the time, Pallas kernels for 14%

profile of v3, /device:TPU:0, one launch (start us, length us, event | category | flops | bytes accessed | tf_op | source)
XLA Modules:
  0.0 44.1 jit_solution(7343780263226106621)
XLA Ops:
  0.0 1.5 %shard_map.64 = (bf16[12,256,256]{2,1,0:T(8,128)(2,1)S(1)}, bf16[2,256,256]{2,1,0:T(8,128)(2,1)S(1)}, bf16[256,256]{1,0:T(8,128)(2,1)S(1)}, bf16[256,256]{1,0:T(8,128)(2,1)S(1)}) custom-call(s32[2,24]{1,0:T(2,128)} %block_map.3, s32[2,24]{1,0:T(2,128)} %valid_rows.3, bf16[12,256,256]{2,1,0:T(8,128)(2,1)} %generators.1, bf16[2,256,256]{2,1,0:T(8,128)(2,1)} %coupling.1), custom_call_target="tpu_custom_call" | custom-call | tf_op jit(solution)/shard_map/pallas_call | solution.py:384
  1.5 2.5 %shard_map.65 = (bf16[8,256,256]{2,1,0:T(8,128)(2,1)S(1)}, bf16[4,256,256]{2,1,0:T(8,128)(2,1)S(1)}, f32[4,2048,128]{2,1,0:T(8,128)S(1)}, bf16[2,256,256]{2,1,0:T(8,128)(2,1)S(1)}) custom-call(s32[2,24]{1,0:T(2,128)} %block_map.3, s32[2,24]{1,0:T(2,128)} %valid_rows.3, bf16[12,256,256]{2,1,0:T(8,128)(2,1)S(1)} %get-tuple-element.22.every, ...), custom_call_target="tpu_custom_call" | custom-call | tf_op jit(solution)/shard_map/pallas_call | solution.py:384
  4.0 0.6 %collective-permute-start = (bf16[8,256,256]{2,1,0:T(8,128)(2,1)S(1)}, bf16[8,256,256]{2,1,0:T(8,128)(2,1)S(1)}, u32[]{:S(2)}, u32[]{:S(2)}) collective-permute-start(bf16[8,256,256]{2,1,0:T(8,128)(2,1)S(1)} %get-tuple-element.25.mine), channel_id=1, source_target_pairs={{0,8},{1,9},{2,10},{3,11},{4,12},{5,13},{6,14},{7,15},{8,0},{9,1},... | collective-permute-start | bytes 3145736 | tf_op jit(solution)/shard_map/ppermute | solution.py:405
  4.6 2.6 %collective-permute-start.1 = (bf16[2,256,256]{2,1,0:T(8,128)(2,1)S(1)}, bf16[2,256,256]{2,1,0:T(8,128)(2,1)S(1)}, u32[]{:S(2)}, u32[]{:S(2)}) collective-permute-start(bf16[2,256,256]{2,1,0:T(8,128)(2,1)S(1)} %get-tuple-element.26), channel_id=1, source_target_pairs={{0,16},{1,17},{2,18},{3,19},{4,20},{5,21},{6,22},{7,23},{8,24},{9,... | collective-permute-start | bytes 786440 | tf_op jit(solution)/shard_map/ppermute | solution.py:405
  7.2 0.1 collective-permute-start.2
  7.2 1.4 %collective-permute-start.4 = (bf16[256,256]{1,0:T(8,128)(2,1)S(1)}, bf16[256,256]{1,0:T(8,128)(2,1)S(1)}, u32[]{:S(2)}, u32[]{:S(2)}) collective-permute-start(bf16[256,256]{1,0:T(8,128)(2,1)S(1)} %get-tuple-element.28), channel_id=1, source_target_pairs={{0,24},{1,25},{2,26},{3,27},{4,28},{5,29},{6,30},{7,31},{8,16},{9,... | collective-permute-start | bytes 393224 | tf_op jit(solution)/shard_map/ppermute | solution.py:405
  8.7 8.5 %collective-permute-done.2.refs_1_ = bf16[256,256]{1,0:T(8,128)(2,1)S(1)} collective-permute-done((bf16[256,256]{1,0:T(8,128)(2,1)S(1)}, bf16[256,256]{1,0:T(8,128)(2,1)S(1)}, u32[]{:S(2)}, u32[]{:S(2)}) %collective-permute-start.2) | collective-permute-done | bytes 131104 | tf_op jit(solution)/shard_map/ppermute | solution.py:405
  17.1 2.0 %collective-permute-start.3 = (bf16[256,256]{1,0:T(8,128)(2,1)S(1)}, bf16[256,256]{1,0:T(8,128)(2,1)S(1)}, u32[]{:S(2)}, u32[]{:S(2)}) collective-permute-start(bf16[256,256]{1,0:T(8,128)(2,1)S(1)} %collective-permute-done.2.refs_1_), channel_id=1, source_target_pairs={{0,1},{1,0},{2,3},{3,2},{4,5},{5,4},{6,7},{7,6},{8,9},{9,8},{10,11... | collective-permute-start | bytes 393224 | tf_op jit(solution)/shard_map/ppermute | solution.py:405
  19.1 0.3 collective-permute-done.4.refs_3_
  19.4 1.4 %collective-permute-start.5 = (bf16[256,256]{1,0:T(8,128)(2,1)S(1)}, bf16[256,256]{1,0:T(8,128)(2,1)S(1)}, u32[]{:S(2)}, u32[]{:S(2)}) collective-permute-start(bf16[256,256]{1,0:T(8,128)(2,1)S(1)} %collective-permute-done.4.refs_3_), channel_id=1, source_target_pairs={{0,1},{1,0},{2,3},{3,2},{4,5},{5,4},{6,7},{7,6},{8,9},{9,8},{10,11... | collective-permute-start | bytes 393224 | tf_op jit(solution)/shard_map/ppermute | solution.py:405
  20.8 0.0 collective-permute-done.1.refs_0_
  20.8 1.3 %collective-permute-done.3.refs_2_ = bf16[256,256]{1,0:T(8,128)(2,1)S(1)} collective-permute-done((bf16[256,256]{1,0:T(8,128)(2,1)S(1)}, bf16[256,256]{1,0:T(8,128)(2,1)S(1)}, u32[]{:S(2)}, u32[]{:S(2)}) %collective-permute-start.3) | collective-permute-done | bytes 131104 | tf_op jit(solution)/shard_map/ppermute | solution.py:405
  22.1 2.8 %collective-permute-done.5.refs_4_ = bf16[256,256]{1,0:T(8,128)(2,1)S(1)} collective-permute-done((bf16[256,256]{1,0:T(8,128)(2,1)S(1)}, bf16[256,256]{1,0:T(8,128)(2,1)S(1)}, u32[]{:S(2)}, u32[]{:S(2)}) %collective-permute-start.5) | collective-permute-done | bytes 131104 | tf_op jit(solution)/shard_map/ppermute | solution.py:405
  24.9 0.4 shard_map.66
  25.3 0.1 collective-permute-start.6
  25.4 1.8 %collective-permute-start.9 = (bf16[256,256]{1,0:T(8,128)(2,1)S(1)}, bf16[256,256]{1,0:T(8,128)(2,1)S(1)}, u32[]{:S(2)}, u32[]{:S(2)}) collective-permute-start(bf16[256,256]{1,0:T(8,128)(2,1)S(1)} %collective-permute-done.4.refs_3_), channel_id=1, source_target_pairs={{0,2},{1,3},{2,0},{3,1},{4,6},{5,7},{6,4},{7,5},{8,10},{9,11},{10,... | collective-permute-start | bytes 393224 | tf_op jit(solution)/shard_map/ppermute | solution.py:405
  27.2 0.3 collective-permute-start.7
  27.5 4.3 %collective-permute-done.9.refs_2_ = bf16[256,256]{1,0:T(8,128)(2,1)S(1)} collective-permute-done((bf16[256,256]{1,0:T(8,128)(2,1)S(1)}, bf16[256,256]{1,0:T(8,128)(2,1)S(1)}, u32[]{:S(2)}, u32[]{:S(2)}) %collective-permute-start.9) | collective-permute-done | bytes 131104 | tf_op jit(solution)/shard_map/ppermute | solution.py:405
  31.8 1.7 %collective-permute-start.10 = (bf16[256,256]{1,0:T(8,128)(2,1)S(1)}, bf16[256,256]{1,0:T(8,128)(2,1)S(1)}, u32[]{:S(2)}, u32[]{:S(2)}) collective-permute-start(bf16[256,256]{1,0:T(8,128)(2,1)S(1)} %collective-permute-done.9.refs_2_), channel_id=1, source_target_pairs={{0,1},{1,0},{2,3},{3,2},{4,5},{5,4},{6,7},{7,6},{8,9},{9,8},{10,11... | collective-permute-start | bytes 393224 | tf_op jit(solution)/shard_map/ppermute | solution.py:405
  33.5 1.5 %collective-permute-start.8 = (bf16[256,256]{1,0:T(8,128)(2,1)S(1)}, bf16[256,256]{1,0:T(8,128)(2,1)S(1)}, u32[]{:S(2)}, u32[]{:S(2)}) collective-permute-start(bf16[256,256]{1,0:T(8,128)(2,1)S(1)} %collective-permute-done.3.refs_2_), channel_id=1, source_target_pairs={{0,2},{1,3},{2,0},{3,1},{4,6},{5,7},{6,4},{7,5},{8,10},{9,11},{10,... | collective-permute-start | bytes 393224 | tf_op jit(solution)/shard_map/ppermute | solution.py:405
  35.1 0.0 collective-permute-done.theirs
  35.1 3.1 %shard_map.67 = (f32[4,2048,128]{2,1,0:T(8,128)S(1)}, f32[4,2048,128]{2,1,0:T(8,128)S(1)}) custom-call(bf16[4,256,256]{2,1,0:T(8,128)(2,1)S(1)} %get-tuple-element.24.own, bf16[8,256,256]{2,1,0:T(8,128)(2,1)S(1)} %get-tuple-element.25.mine, bf16[8,256,256]{2,1,0:T(8,128)(2,1)S(1)} %collective-permute-done.theirs, ...), custom_call_target="tpu_custom_call" | custom-call | tf_op jit(solution)/shard_map/pallas_call | solution.py:384
  38.2 0.6 %shard_map.68.refs_5_ = f32[2,2048,128]{2,1,0:T(8,128)S(1)} custom-call(bf16[8,256,256]{2,1,0:T(8,128)(2,1)S(1)} %get-tuple-element.25.mine, bf16[8,256,256]{2,1,0:T(8,128)(2,1)S(1)} %collective-permute-done.theirs, bf16[2,512,256]{2,1,0:T(8,128)(2,1)S(1)} %get-tuple-element.31.refs_0_.refs_1_, f32[4,2048,128]{2,1,0:T(8,128)S(1)} %get-tuple-element.33.refs_1_.refs_3_.refs_4_), custom_call_target="tpu_custom_call" | custom-call | tf_op jit(solution)/shard_map/pallas_call | solution.py:384
  38.8 0.0 collective-permute-done.6.swapped
  38.8 2.1 %shard_map.69 = (f32[8,2048,128]{2,1,0:T(8,128)}, f32[4,2048,128]{2,1,0:T(8,128)S(1)}, f32[2,2048,128]{2,1,0:T(8,128)S(1)}, bf16[2,2,2,256,256]{4,3,2,1,0:T(8,128)(2,1)S(1)}) custom-call(bf16[4,256,256]{2,1,0:T(8,128)(2,1)S(1)} %get-tuple-element.24.own, ...), custom_call_target="tpu_custom_call", output_to_operand_aliasing={{1}: (9, {}), {2}: (10, {})} | custom-call | tf_op jit(solution)/shard_map/pallas_call | solution.py:384
  40.9 0.0 collective-permute-done.7.refs_0_
  40.9 0.0 collective-permute-done.10.refs_3_
  40.9 0.0 collective-permute-done.8.refs_1_
  40.9 3.2 %shard_map.70 = f32[8,2048,128]{2,1,0:T(8,128)} custom-call(bf16[2,2,2,256,256]{4,3,2,1,0:T(8,128)(2,1)S(1)} %get-tuple-element.35.right, bf16[256,256]{1,0:T(8,128)(2,1)S(1)} %collective-permute-done.7.refs_0_, bf16[256,256]{1,0:T(8,128)(2,1)S(1)} %collective-permute-done.8.refs_1_, ...), custom_call_target="tpu_custom_call", output_to_operand_aliasing={{}: (8, {})} | custom-call | tf_op jit(solution)/shard_map/pallas_call | solution.py:384
Async XLA Ops:
  4.0 31.1 %collective-permute-start = (bf16[8,256,256]{2,1,0:T(8,128)(2,1)S(1)}, bf16[8,256,256]{2,1,0:T(8,128)(2,1)S(1)}, u32[]{:S(2)}, u32[]{:S(2)}) collective-permute-start(bf16[8,256,256]{2,1,0:T(8,128)(2,1)S(1)} %get-tuple-element.25.mine), channel_id=1, source_target_pairs={{0,8},{1,9},{2,10},{3,11},{4,12},{5,13},{6,14},{7,15},{8,0},{9,1},... | collective-permute-start | bytes 3145736 | tf_op jit(solution)/shard_map/ppermute | solution.py:405
  4.6 16.3 %collective-permute-start.1 = (bf16[2,256,256]{2,1,0:T(8,128)(2,1)S(1)}, bf16[2,256,256]{2,1,0:T(8,128)(2,1)S(1)}, u32[]{:S(2)}, u32[]{:S(2)}) collective-permute-start(bf16[2,256,256]{2,1,0:T(8,128)(2,1)S(1)} %get-tuple-element.26), channel_id=1, source_target_pairs={{0,16},{1,17},{2,18},{3,19},{4,20},{5,21},{6,22},{7,23},{8,24},{9,... | collective-permute-start | bytes 786440 | tf_op jit(solution)/shard_map/ppermute | solution.py:405
  7.2 10.0 %collective-permute-start.2 = (bf16[256,256]{1,0:T(8,128)(2,1)S(1)}, bf16[256,256]{1,0:T(8,128)(2,1)S(1)}, u32[]{:S(2)}, u32[]{:S(2)}) collective-permute-start(bf16[256,256]{1,0:T(8,128)(2,1)S(1)} %get-tuple-element.27), channel_id=1, source_target_pairs={{0,16},{1,17},{2,18},{3,19},{4,20},{5,21},{6,22},{7,23},{8,24},{9,... | collective-permute-start | bytes 393224 | tf_op jit(solution)/shard_map/ppermute | solution.py:405
  7.2 12.2 %collective-permute-start.4 = (bf16[256,256]{1,0:T(8,128)(2,1)S(1)}, bf16[256,256]{1,0:T(8,128)(2,1)S(1)}, u32[]{:S(2)}, u32[]{:S(2)}) collective-permute-start(bf16[256,256]{1,0:T(8,128)(2,1)S(1)} %get-tuple-element.28), channel_id=1, source_target_pairs={{0,24},{1,25},{2,26},{3,27},{4,28},{5,29},{6,30},{7,31},{8,16},{9,... | collective-permute-start | bytes 393224 | tf_op jit(solution)/shard_map/ppermute | solution.py:405
  17.1 5.0 %collective-permute-start.3 = (bf16[256,256]{1,0:T(8,128)(2,1)S(1)}, bf16[256,256]{1,0:T(8,128)(2,1)S(1)}, u32[]{:S(2)}, u32[]{:S(2)}) collective-permute-start(bf16[256,256]{1,0:T(8,128)(2,1)S(1)} %collective-permute-done.2.refs_1_), channel_id=1, source_target_pairs={{0,1},{1,0},{2,3},{3,2},{4,5},{5,4},{6,7},{7,6},{8,9},{9,8},{10,11... | collective-permute-start | bytes 393224 | tf_op jit(solution)/shard_map/ppermute | solution.py:405
  19.4 5.5 %collective-permute-start.5 = (bf16[256,256]{1,0:T(8,128)(2,1)S(1)}, bf16[256,256]{1,0:T(8,128)(2,1)S(1)}, u32[]{:S(2)}, u32[]{:S(2)}) collective-permute-start(bf16[256,256]{1,0:T(8,128)(2,1)S(1)} %collective-permute-done.4.refs_3_), channel_id=1, source_target_pairs={{0,1},{1,0},{2,3},{3,2},{4,5},{5,4},{6,7},{7,6},{8,9},{9,8},{10,11... | collective-permute-start | bytes 393224 | tf_op jit(solution)/shard_map/ppermute | solution.py:405
  25.3 13.4 %collective-permute-start.6 = (bf16[1,2,2,256,256]{4,3,2,1,0:T(8,128)(2,1)S(1)}, bf16[1,2,2,256,256]{4,3,2,1,0:T(8,128)(2,1)S(1)}, u32[]{:S(2)}, u32[]{:S(2)}) collective-permute-start(bf16[1,2,2,256,256]{4,3,2,1,0:T(8,128)(2,1)S(1)} %get-tuple-element.30), channel_id=1, source_target_pairs={{0,8},{1,9},{2,10},{3,11},{4,12},{5,13},{6,14},{7,15},{8,0},{9,1},... | collective-permute-start | bytes 1572872 | tf_op jit(solution)/shard_map/ppermute | solution.py:405
  25.4 6.4 %collective-permute-start.9 = (bf16[256,256]{1,0:T(8,128)(2,1)S(1)}, bf16[256,256]{1,0:T(8,128)(2,1)S(1)}, u32[]{:S(2)}, u32[]{:S(2)}) collective-permute-start(bf16[256,256]{1,0:T(8,128)(2,1)S(1)} %collective-permute-done.4.refs_3_), channel_id=1, source_target_pairs={{0,2},{1,3},{2,0},{3,1},{4,6},{5,7},{6,4},{7,5},{8,10},{9,11},{10,... | collective-permute-start | bytes 393224 | tf_op jit(solution)/shard_map/ppermute | solution.py:405
  27.2 13.7 %collective-permute-start.7 = (bf16[256,256]{1,0:T(8,128)(2,1)S(1)}, bf16[256,256]{1,0:T(8,128)(2,1)S(1)}, u32[]{:S(2)}, u32[]{:S(2)}) collective-permute-start(bf16[256,256]{1,0:T(8,128)(2,1)S(1)} %collective-permute-done.2.refs_1_), channel_id=1, source_target_pairs={{0,2},{1,3},{2,0},{3,1},{4,6},{5,7},{6,4},{7,5},{8,10},{9,11},{10,... | collective-permute-start | bytes 393224 | tf_op jit(solution)/shard_map/ppermute | solution.py:405
  31.8 9.0 %collective-permute-start.10 = (bf16[256,256]{1,0:T(8,128)(2,1)S(1)}, bf16[256,256]{1,0:T(8,128)(2,1)S(1)}, u32[]{:S(2)}, u32[]{:S(2)}) collective-permute-start(bf16[256,256]{1,0:T(8,128)(2,1)S(1)} %collective-permute-done.9.refs_2_), channel_id=1, source_target_pairs={{0,1},{1,0},{2,3},{3,2},{4,5},{5,4},{6,7},{7,6},{8,9},{9,8},{10,11... | collective-permute-start | bytes 393224 | tf_op jit(solution)/shard_map/ppermute | solution.py:405
  33.5 7.4 %collective-permute-start.8 = (bf16[256,256]{1,0:T(8,128)(2,1)S(1)}, bf16[256,256]{1,0:T(8,128)(2,1)S(1)}, u32[]{:S(2)}, u32[]{:S(2)}) collective-permute-start(bf16[256,256]{1,0:T(8,128)(2,1)S(1)} %collective-permute-done.3.refs_2_), channel_id=1, source_target_pairs={{0,2},{1,3},{2,0},{3,1},{4,6},{5,7},{6,4},{7,5},{8,10},{9,11},{10,... | collective-permute-start | bytes 393224 | tf_op jit(solution)/shard_map/ppermute | solution.py:405

commit v4 on v3

--- a/solution.py
+++ b/solution.py
@@ -12,7 +12,7 @@
 SMEM = pl.BlockSpec(memory_space=pltpu.SMEM)
 VMEM = pl.BlockSpec(memory_space=pltpu.VMEM)
 LANES = 128
-PIECES = 4
+PIECES = 1
 
 
 def in_hbm(x):
@@ -73,6 +73,18 @@
 def project(x, mixer):
     dims = (((0,), (1,)), ((), ()))
     return lax.dot_general(mixer, x, dims, preferred_element_type=jnp.float32).astype(x.dtype)
+
+
+def fill_unit(plan, out, every, where, count, target, parity, side):
+    whole = plan.unit // plan.block
+    for j in range(max(whole, 1)):
+        slot = (2 * (side * whole + j) + parity) * plan.rows_n + target
+        if whole:
+            out[pl.ds(j * plan.block, plan.block), :] = keep_rows(every[where[slot]], count[slot])
+        else:
+            start = pl.multiple_of(side * plan.unit, plan.unit)
+            part = every[where[slot], pl.ds(start, plan.unit), :]
+            out[...] = keep_rows(part, count[slot], start)
 
 
 def pack_rows_kernel(plan, block_map, valid_rows, generators, coupling, every, mixers, *refs):
@@ -89,27 +101,18 @@
     copies[2].wait()
     read_map(plan, map_s, valid_s, child, group, count, where)
     copies[0].wait()
-    whole = plan.unit // plan.block
     side = col % 2
     for i, out in enumerate(outs):
         d, k = 1 + i // 2, i % 2
         aim = (group + plan.halves - d) % plan.halves
-        target = 2 * aim + (child + k) % 2
-        parity = plan.parity(aim, col)
-        for j in range(max(whole, 1)):
-            slot = (2 * (side * whole + j) + parity) * plan.rows_n + target
-            if whole:
-                out[pl.ds(j * plan.block, plan.block), :] = keep_rows(every[where[slot]], count[slot])
-            else:
-                start = pl.multiple_of(side * plan.unit, plan.unit)
-                part = every[where[slot], pl.ds(start, plan.unit), :]
-                out[...] = keep_rows(part, count[slot], start)
+        fill_unit(plan, out, every, where, count, 2 * aim + (child + k) % 2, plan.parity(aim, col), side)
     copies[3].wait()
 
 
 def pack_rest_kernel(plan, block_map, valid_rows, every, mixers, diagonal, front,
                      mine, own, base, *refs):
-    outs, (map_s, valid_s, where, count, sems) = refs[:-5], refs[-5:]
+    turns = plan.halves - 1
+    far_outs, outs, (map_s, valid_s, where, count, sems) = refs[:turns], refs[turns:-5], refs[-5:]
     row, col, group, child = plan.here()
     diags = plan.row_cap + plan.col_cap
     copies = [
@@ -136,6 +139,10 @@
         for q in range(plan.row_cap):
             slot = q * plan.rows_n + to
             target[q] = keep_rows(every[where[slot]], count[slot])
+    for i, out in enumerate(far_outs):
+        aim = (group + plan.halves - (i + 1)) % plan.halves
+        fill_unit(plan, out, every, where, count, 2 * aim + (child + 1) % 2,
+                  1 - plan.parity(aim, col), 1 - col % 2)
     for s in range(plan.col_cap):
         loads[s].wait()
         mine[diags + s] = keep_both(mine[diags + s], count[s * plan.cols_n + col])
@@ -215,12 +222,18 @@
         copies[-1].start()
 
 
-def begin_kernel(plan, own, mine, theirs, base, front, total, rest, sems):
-    row, col, group, _ = plan.here()
+def load_kernel(plan, front, rest, sems):
+    _, _, group, _ = plan.here()
     reads = []
     for i in range(plan.rows_local - plan.row_cap):
         a = (group * plan.row_cap + plan.row_cap + i) % plan.rows_local
         in_pieces(front.at[a], rest.at[i], sems, reads)
+    for copy in reads:
+        copy.wait()
+
+
+def begin_kernel(plan, own, mine, theirs, base, total):
+    row, col, group, _ = plan.here()
     rows = plan.row_cap * plan.block
     left = own[...].reshape(rows, plan.rank)
     right = theirs[pl.ds(0, plan.row_cap)].reshape(rows, plan.rank)
@@ -234,9 +247,6 @@
             slot = plan.row_cap + plan.col_cap + s
             value = mine[slot].astype(jnp.float32) + theirs[slot].astype(jnp.float32)
             put_tile(plan, total, total, 2 * s + col // plan.rows_n, group * plan.col_cap + s, value)
-
-    for copy in reads:
-        copy.wait()
 
 
 def even_kernel(plan, mine, theirs, *refs):
@@ -254,17 +264,10 @@
                            value[j * plan.block:(j + 1) * plan.block])
 
 
-def spread(plan, left, right, base, total, steps, group):
-    for e in range(1, plan.halves):
-        for s in range(plan.col_cap):
-            value = matmul(left(0), right[e, 0, s]) + matmul(left(1), right[e, 1, s])
-            put_tiles(plan, base, total, steps, (group + e) % plan.halves * plan.col_cap + s, value)
-
-
-def middle_kernel(plan, own, mine, theirs, formed, swapped, *refs):
+def finish_kernel(plan, own, mine, theirs, formed, swapped, *refs):
     halves, half, turns = plan.halves, plan.half_cap, plan.halves - 1
-    directs, fars = refs[:turns], refs[turns: 2 * turns]
-    base, rest, _, _, out, near, even, right, sems = refs[2 * turns:]
+    directs, fars, parts = refs[:turns], refs[turns: 2 * turns], refs[2 * turns: 6 * turns]
+    base, rest, _, _, out, near, even, odd, far, right, sems = refs[6 * turns:]
     row, col, group, _ = plan.here()
     owns = plan.owns_diag(group, col)
     main = row == col % plan.rows_n
@@ -290,73 +293,56 @@
     for s in range(plan.col_cap):
         right[0, 0, s] = mine[plan.row_cap + s]
         right[0, 1, s] = theirs[plan.row_cap + s]
-    rows = half * plan.block
     copies = []
+
+    def write(source, a):
+        in_pieces(source, out.at[a], sems, copies)
+
+    def spread(left, start, source, sources, total, places, first):
+        rows = pl.ds(start, len(places) * plan.block)
+        for e in range(first, halves):
+            for s in range(plan.col_cap):
+                value = matmul(left(0, rows), right[e, 0, s]) + matmul(left(1, rows), right[e, 1, s])
+                b = (group + e) % halves * plan.col_cap + s
+                for j, (a, place) in enumerate(zip(sources, places)):
+                    put_across(plan, source, a, total, place, b,
+                               value[j * plan.block:(j + 1) * plan.block])
+
     for g in range(2):
-        def left(k):
-            return (own, theirs)[k][pl.ds(g * half, half)].reshape(rows, plan.rank)
-
-        spread(plan, left, right, base, near, [g * half + j for j in range(half)], group)
-        for q in range(half if g == 0 else 0):
-            in_pieces(near.at[q], out.at[group * plan.row_cap + q], sems, copies)
+        def left(k, rows):
+            value = (own, theirs)[k][pl.ds(g * half, half)]
+            return value.reshape(half * plan.block, plan.rank)
+
+        steps = range(g * half, g * half + half)
+        spread(left, 0, base, steps, near, steps, 1)
+        for q in steps:
+            write(near.at[q], group * plan.row_cap + q)
     parity = plan.parity(group, col)
     for d in range(1, halves):
-        def left(k):
-            return fars[d - 1][k]
-
+        places = range((d - 1) * half, d * half)
         first = (d - 1) * plan.row_cap
+        top = (group + d) % halves * plan.row_cap
 
         @pl.when(row >= 0)
         def _():
-            for e in range(1, halves):
-                for s in range(plan.col_cap):
-                    value = matmul(left(0), right[e, 0, s]) + matmul(left(1), right[e, 1, s])
-                    b = (group + e) % halves * plan.col_cap + s
-                    for j in range(half):
-                        put_across(plan, rest, first + 2 * j + parity, even, (d - 1) * half + j, b,
-                                   value[j * plan.block:(j + 1) * plan.block])
+            spread(lambda k, rows: fars[d - 1][k], 0, rest,
+                   [first + 2 * j + parity for j in range(half)], even, places, 1)
 
         @pl.when(main)
         def _():
             for s in range(plan.col_cap):
                 value = directs[d - 1][s].astype(jnp.float32) + swapped[d - 1, 0, s].astype(jnp.float32)
-                b = (group + d) % halves * plan.col_cap + s
-                put_tile(plan, even, even, (d - 1) * half + s, b, value)
-    for copy in copies:
-        copy.wait()
-
-
-def last_kernel(plan, right, *refs):
-    halves, half, turns = plan.halves, plan.half_cap, plan.halves - 1
-    parts, (rest, near, even, out_in, out, odd, far, sems) = refs[: 4 * turns], refs[4 * turns:]
-    _, col, group, _ = plan.here()
-    parity = plan.parity(group, col)
-    copies = []
-
-    def write(source, a):
-        in_pieces(source, out.at[a], sems, copies)
-
-    for q in range(half, plan.row_cap):
-        write(near.at[q], group * plan.row_cap + q)
-    for d in range(1, halves):
+                put_tile(plan, even, even, places[s], (group + d) % halves * plan.col_cap + s, value)
+
         for j in range(half):
-            a = (group + d) % halves * plan.row_cap + 2 * j + parity
-            write(even.at[(d - 1) * half + j], a)
-    for d in range(1, halves):
+            write(even.at[places[j]], top + 2 * j + parity)
         for k in range(2):
             here, there = parts[4 * (d - 1) + 2 * k: 4 * (d - 1) + 2 * k + 2]
             join(plan, far, k, here, there, col % 2)
         for j in range(half):
-            for e in range(halves):
-                for s in range(plan.col_cap):
-                    rows = pl.ds(j * plan.block, plan.block)
-                    value = matmul(far[0, rows, :], right[e, 0, s])
-                    value += matmul(far[1, rows, :], right[e, 1, s])
-                    b = (group + e) % halves * plan.col_cap + s
-                    put_across(plan, rest, (d - 1) * plan.row_cap + 2 * j + 1 - parity,
-                               odd, (d - 1) * half + j, b, value)
-            a = (group + d) % halves * plan.row_cap + 2 * j + 1 - parity
-            write(odd.at[(d - 1) * half + j], a)
+            spread(lambda k, rows: far[k, rows, :], j * plan.block, rest,
+                   [first + 2 * j + 1 - parity], odd, [places[j]], 0)
+            write(odd.at[places[j]], top + 2 * j + 1 - parity)
     for copy in copies:
         copy.wait()
 
@@ -425,11 +411,13 @@
     near, beside_, along_, far_ = {}, {}, {}, {}
     for (d, k), x in zip(flows, rows_out):
         near[d, k] = send(x, across(d, k))
-    mine, own, base, *cols_out = call(
+    mine, own, base, *sent = call(
         pack_rest_kernel,
-        [shape(row_cap + 2 * col_cap), shape(row_cap), strip(row_cap)] + [shape(col_cap)] * (halves - 1),
-        [ANY, ANY, VMEM, VMEM, ANY, ANY], [VMEM] * (halves + 2), maps + [sems(3 + col_cap)], 12,
+        [shape(row_cap + 2 * col_cap), shape(row_cap), strip(row_cap)]
+        + [unit] * (halves - 1) + [shape(col_cap)] * (halves - 1),
+        [ANY, ANY, VMEM, VMEM, ANY, ANY], [VMEM] * (2 * halves + 1), maps + [sems(3 + col_cap)], 12,
         (block_map, valid_rows, every, mixers, diagonal_blocks, front))
+    far_outs, cols_out = sent[: halves - 1], sent[halves - 1:]
     direct = {d: send(cols_out[d - 1], across(d, 0)) for d in turns}
     theirs = send(mine, partner)
     for d, k in flows:
@@ -437,12 +425,11 @@
         along_[d, k] = send(near[d, k], along)
     for d in turns:
         far_[d, 0] = send(beside_[d, 0], along)
-        far_[d, 1] = send(along_[d, 1], beside)
+        far_[d, 1] = send(far_outs[d - 1], across(d, 1))
     others = rows_local - row_cap
-    args = (own, mine, theirs, base, front)
-    near_rows, rest = call(
-        begin_kernel, [strip(row_cap), strip(others)],
-        [VMEM] * 4 + [ANY], [VMEM] * 2, [sems(others * PIECES)], 12, args)
+    rest = call(load_kernel, strip(others), [ANY], VMEM, [sems(others * PIECES)], 12, (front,))
+    args = (own, mine, theirs, base)
+    near_rows = call(begin_kernel, strip(row_cap), [VMEM] * 4, VMEM, [], 12, args)
     args = (mixers,) + tuple(direct[d] for d in turns) + tuple(
         x[flow] for flow in flows for x in (near, beside_))
     formed, leave, *fars = call(
@@ -451,19 +438,15 @@
     swapped = send(leave, partner)
     args = (mine, theirs, *fars, rest)
     even = call(even_kernel, strip(others // 2), [VMEM] * len(args), VMEM, [], 12, args)
-    args = (own, mine, theirs, formed, swapped, *(direct[d] for d in turns), *fars,
-            base, rest, near_rows, even)
+    args = (own, mine, theirs, formed, swapped, *(direct[d] for d in turns), *fars) + tuple(
+        x[flow] for flow in flows for x in (along_, far_)) + (base, rest, near_rows, even)
     n = len(args)
-    out, near_rows, even, right = call(
-        middle_kernel,
-        [strip(rows_local), strip(row_cap), strip(others // 2), shape(halves, 2, col_cap)],
-        [VMEM] * n, [ANY] + [VMEM] * 3, [sems(half * PIECES)], 12, args, {n - 2: 1, n - 1: 2})
-    args = (right,) + tuple(x[flow] for flow in flows for x in (along_, far_)) + (
-        rest, near_rows, even, out)
-    out = call(
-        last_kernel, strip(rows_local), [VMEM] * (len(args) - 1) + [ANY], ANY,
-        [pltpu.VMEM((others // 2,) + front.shape[1:], front.dtype),
-         pltpu.VMEM(joined.shape, dt), sems((others + half) * PIECES)], 16, args, {len(args) - 1: 0})
+    out, _, _ = call(
+        finish_kernel, [strip(rows_local), strip(row_cap), strip(others // 2)],
+        [VMEM] * n, [ANY] + [VMEM] * 2,
+        [pltpu.VMEM((others // 2,) + front.shape[1:], front.dtype), pltpu.VMEM(joined.shape, dt),
+         pltpu.VMEM((halves, 2, col_cap, block, rank), dt), sems(rows_local * PIECES)],
+        16, args, {n - 2: 1, n - 1: 2})
     out = out.reshape(rows_local, block, parts, cols_local, LANES)
     return out.transpose(0, 1, 3, 2, 4).reshape(rows_local, block, cols_local, width)
 

time: 44.3 us -> 37.3 us (0.84)
  waiting for transfers between devices: 17.2 us -> 10.7 us
  Pallas kernels: 13.4 us -> 12.5 us
  starting transfers between devices: 13.5 us -> 14 us
    ppermute x11, waiting for transfers between devices: 17.2 us -> 10.7 us  [send(): return lax.ppermute(x, ('row', 'col'), pairs)]
    pallas_call x7, Pallas kernels: 13.4 us -> 12.5 us  [call(): pl.pallas_call(functools.partial(kernel, plan), out_shape=out_shape, in_s...]
    ppermute x11, starting transfers between devices: 13.5 us -> 14 us  [send(): return lax.ppermute(x, ('row', 'col'), pairs)]
  transfers between devices with their start and end apart: 11 -> 11, of which waited for: 5 -> 6; matrix products, arithmetic and copies ran while one was open for 0% -> 0% of each run, Pallas kernels for 14% -> 12%
where the time goes in v4:
time: 37.3 us; the launch traced here: 37.1 us
  starting transfers between devices  14 us (38%)
  Pallas kernels  12.5 us (34%)
  waiting for transfers between devices  10.7 us (29%)
    ppermute x11, starting transfers between devices, send(): return lax.ppermute(x, ('row', 'col'), pairs)  14 us
    pallas_call x7, Pallas kernels, call(): pl.pallas_call(functools.partial(kernel, plan), out_shape=out_shape, in_s...  12.5 us
    ppermute x11, waiting for transfers between devices, send(): return lax.ppermute(x, ('row', 'col'), pairs)  10.7 us
  transfers between devices with their start and end apart: 11, of which 6 were waited for; matrix products, arithmetic and copies ran while one was open for 0% of the time, Pallas kernels for 12%

profile of v4, /device:TPU:0, one launch (start us, length us, event | category | flops | bytes accessed | tf_op | source)
XLA Modules:
  0.0 37.1 jit_solution(3668437294340873805)
XLA Ops:
  0.0 1.5 %shard_map.64 = (bf16[12,256,256]{2,1,0:T(8,128)(2,1)S(1)}, bf16[2,256,256]{2,1,0:T(8,128)(2,1)S(1)}, bf16[256,256]{1,0:T(8,128)(2,1)S(1)}, bf16[256,256]{1,0:T(8,128)(2,1)S(1)}) custom-call(s32[2,24]{1,0:T(2,128)} %block_map.3, s32[2,24]{1,0:T(2,128)} %valid_rows.3, bf16[12,256,256]{2,1,0:T(8,128)(2,1)} %generators.1, bf16[2,256,256]{2,1,0:T(8,128)(2,1)} %coupling.1), custom_call_target="tpu_custom_call" | custom-call | tf_op jit(solution)/shard_map/pallas_call | solution.py:370
  1.5 2.5 %shard_map.65 = (bf16[8,256,256]{2,1,0:T(8,128)(2,1)S(1)}, bf16[4,256,256]{2,1,0:T(8,128)(2,1)S(1)}, f32[4,2048,128]{2,1,0:T(8,128)S(1)}, bf16[256,256]{1,0:T(8,128)(2,1)S(1)}, bf16[2,256,256]{2,1,0:T(8,128)(2,1)S(1)}) custom-call(s32[2,24]{1,0:T(2,128)} %block_map.3, s32[2,24]{1,0:T(2,128)} %valid_rows.3, ...), custom_call_target="tpu_custom_call" | custom-call | tf_op jit(solution)/shard_map/pallas_call | solution.py:370
  4.0 0.6 %collective-permute-start = (bf16[8,256,256]{2,1,0:T(8,128)(2,1)S(1)}, bf16[8,256,256]{2,1,0:T(8,128)(2,1)S(1)}, u32[]{:S(2)}, u32[]{:S(2)}) collective-permute-start(bf16[8,256,256]{2,1,0:T(8,128)(2,1)S(1)} %get-tuple-element.21.mine), channel_id=1, source_target_pairs={{0,8},{1,9},{2,10},{3,11},{4,12},{5,13},{6,14},{7,15},{8,0},{9,1},... | collective-permute-start | bytes 3145736 | tf_op jit(solution)/shard_map/ppermute | solution.py:391
  4.6 2.6 %collective-permute-start.2 = (bf16[256,256]{1,0:T(8,128)(2,1)S(1)}, bf16[256,256]{1,0:T(8,128)(2,1)S(1)}, u32[]{:S(2)}, u32[]{:S(2)}) collective-permute-start(bf16[256,256]{1,0:T(8,128)(2,1)S(1)} %get-tuple-element.23), channel_id=1, source_target_pairs={{0,16},{1,17},{2,18},{3,19},{4,20},{5,21},{6,22},{7,23},{8,24},{9,... | collective-permute-start | bytes 393224 | tf_op jit(solution)/shard_map/ppermute | solution.py:391
  7.2 0.0 collective-permute-start.4
  7.2 1.7 %collective-permute-start.1 = (bf16[2,256,256]{2,1,0:T(8,128)(2,1)S(1)}, bf16[2,256,256]{2,1,0:T(8,128)(2,1)S(1)}, u32[]{:S(2)}, u32[]{:S(2)}) collective-permute-start(bf16[2,256,256]{2,1,0:T(8,128)(2,1)S(1)} %get-tuple-element.22), channel_id=1, source_target_pairs={{0,16},{1,17},{2,18},{3,19},{4,20},{5,21},{6,22},{7,23},{8,24},{9,... | collective-permute-start | bytes 786440 | tf_op jit(solution)/shard_map/ppermute | solution.py:391
  9.0 2.6 %collective-permute-done.2.refs_1_ = bf16[256,256]{1,0:T(8,128)(2,1)S(1)} collective-permute-done((bf16[256,256]{1,0:T(8,128)(2,1)S(1)}, bf16[256,256]{1,0:T(8,128)(2,1)S(1)}, u32[]{:S(2)}, u32[]{:S(2)}) %collective-permute-start.2) | collective-permute-done | bytes 131104 | tf_op jit(solution)/shard_map/ppermute | solution.py:391
  11.5 2.0 %collective-permute-start.3 = (bf16[256,256]{1,0:T(8,128)(2,1)S(1)}, bf16[256,256]{1,0:T(8,128)(2,1)S(1)}, u32[]{:S(2)}, u32[]{:S(2)}) collective-permute-start(bf16[256,256]{1,0:T(8,128)(2,1)S(1)} %collective-permute-done.2.refs_1_), channel_id=1, source_target_pairs={{0,1},{1,0},{2,3},{3,2},{4,5},{5,4},{6,7},{7,6},{8,9},{9,8},{10,11... | collective-permute-start | bytes 393224 | tf_op jit(solution)/shard_map/ppermute | solution.py:391
  13.5 0.4 collective-permute-done.4.refs_3_
  13.9 1.5 %collective-permute-start.5 = (bf16[256,256]{1,0:T(8,128)(2,1)S(1)}, bf16[256,256]{1,0:T(8,128)(2,1)S(1)}, u32[]{:S(2)}, u32[]{:S(2)}) collective-permute-start(bf16[256,256]{1,0:T(8,128)(2,1)S(1)} %collective-permute-done.4.refs_3_), channel_id=1, source_target_pairs={{0,1},{1,0},{2,3},{3,2},{4,5},{5,4},{6,7},{7,6},{8,9},{9,8},{10,11... | collective-permute-start | bytes 393224 | tf_op jit(solution)/shard_map/ppermute | solution.py:391
  15.4 1.2 %collective-permute-done.3.refs_2_ = bf16[256,256]{1,0:T(8,128)(2,1)S(1)} collective-permute-done((bf16[256,256]{1,0:T(8,128)(2,1)S(1)}, bf16[256,256]{1,0:T(8,128)(2,1)S(1)}, u32[]{:S(2)}, u32[]{:S(2)}) %collective-permute-start.3) | collective-permute-done | bytes 131104 | tf_op jit(solution)/shard_map/ppermute | solution.py:391
  16.5 3.3 %collective-permute-done.5.refs_4_ = bf16[256,256]{1,0:T(8,128)(2,1)S(1)} collective-permute-done((bf16[256,256]{1,0:T(8,128)(2,1)S(1)}, bf16[256,256]{1,0:T(8,128)(2,1)S(1)}, u32[]{:S(2)}, u32[]{:S(2)}) %collective-permute-start.5) | collective-permute-done | bytes 131104 | tf_op jit(solution)/shard_map/ppermute | solution.py:391
  19.8 0.0 collective-permute-done.1.refs_0_
  19.8 0.4 %shard_map.66 = (bf16[1,2,2,256,256]{4,3,2,1,0:T(8,128)(2,1)S(1)}, bf16[1,2,2,256,256]{4,3,2,1,0:T(8,128)(2,1)S(1)}, bf16[2,512,256]{2,1,0:T(8,128)(2,1)S(1)}) custom-call(bf16[2,256,256]{2,1,0:T(8,128)(2,1)S(1)} %get-tuple-element.19.mixers.coupling, bf16[2,256,256]{2,1,0:T(8,128)(2,1)S(1)} %collective-permute-done.1.refs_0_, ...), custom_call_target="tpu_custom_call" | custom-call | tf_op jit(solution)/shard_map/pallas_call | solution.py:370
  20.2 0.1 collective-permute-start.6
  20.3 1.6 %collective-permute-start.10 = (bf16[256,256]{1,0:T(8,128)(2,1)S(1)}, bf16[256,256]{1,0:T(8,128)(2,1)S(1)}, u32[]{:S(2)}, u32[]{:S(2)}) collective-permute-start(bf16[256,256]{1,0:T(8,128)(2,1)S(1)} %get-tuple-element.28), channel_id=1, source_target_pairs={{0,24},{1,25},{2,26},{3,27},{4,28},{5,29},{6,30},{7,31},{8,16},{9,... | collective-permute-start | bytes 393224 | tf_op jit(solution)/shard_map/ppermute | solution.py:391
  21.8 1.9 %collective-permute-start.7 = (bf16[256,256]{1,0:T(8,128)(2,1)S(1)}, bf16[256,256]{1,0:T(8,128)(2,1)S(1)}, u32[]{:S(2)}, u32[]{:S(2)}) collective-permute-start(bf16[256,256]{1,0:T(8,128)(2,1)S(1)} %collective-permute-done.2.refs_1_), channel_id=1, source_target_pairs={{0,2},{1,3},{2,0},{3,1},{4,6},{5,7},{6,4},{7,5},{8,10},{9,11},{10,... | collective-permute-start | bytes 393224 | tf_op jit(solution)/shard_map/ppermute | solution.py:391
  23.7 0.1 collective-permute-start.9
  23.9 0.0 collective-permute-done.theirs
  23.9 1.9 %collective-permute-start.8 = (bf16[256,256]{1,0:T(8,128)(2,1)S(1)}, bf16[256,256]{1,0:T(8,128)(2,1)S(1)}, u32[]{:S(2)}, u32[]{:S(2)}) collective-permute-start(bf16[256,256]{1,0:T(8,128)(2,1)S(1)} %collective-permute-done.3.refs_2_), channel_id=1, source_target_pairs={{0,2},{1,3},{2,0},{3,1},{4,6},{5,7},{6,4},{7,5},{8,10},{9,11},{10,... | collective-permute-start | bytes 393224 | tf_op jit(solution)/shard_map/ppermute | solution.py:391
  25.8 2.2 %shard_map.67.refs_1_.refs_7_ = f32[4,2048,128]{2,1,0:T(8,128)S(1)} custom-call(f32[8,2048,128]{2,1,0:T(8,128)} %bitcast.11), custom_call_target="tpu_custom_call" | custom-call | tf_op jit(solution)/shard_map/pallas_call | solution.py:370
  28.0 0.6 %shard_map.69.refs_9_ = f32[2,2048,128]{2,1,0:T(8,128)S(1)} custom-call(bf16[8,256,256]{2,1,0:T(8,128)(2,1)S(1)} %get-tuple-element.21.mine, bf16[8,256,256]{2,1,0:T(8,128)(2,1)S(1)} %collective-permute-done.theirs, bf16[2,512,256]{2,1,0:T(8,128)(2,1)S(1)} %get-tuple-element.27.refs_0_.refs_1_, f32[4,2048,128]{2,1,0:T(8,128)S(1)} %shard_map.67.refs_1_.refs_7_), custom_call_target="tpu_custom_call" | custom-call | tf_op jit(solution)/shard_map/pallas_call | solution.py:370
  28.6 1.2 %shard_map.68.refs_8_ = f32[4,2048,128]{2,1,0:T(8,128)S(1)} custom-call(bf16[4,256,256]{2,1,0:T(8,128)(2,1)S(1)} %get-tuple-element.20.own, bf16[8,256,256]{2,1,0:T(8,128)(2,1)S(1)} %get-tuple-element.21.mine, bf16[8,256,256]{2,1,0:T(8,128)(2,1)S(1)} %collective-permute-done.theirs, f32[4,2048,128]{2,1,0:T(8,128)S(1)} %get-tuple-element.29.base.refs_6_), custom_call_target="tpu_custom_call" | custom-call | tf_op jit(solution)/shard_map/pallas_call | solution.py:370
  29.8 0.0 collective-permute-done.10.refs_5_
  29.8 0.0 collective-permute-done.7.refs_2_
  29.8 1.2 %collective-permute-done.9.refs_4_ = bf16[256,256]{1,0:T(8,128)(2,1)S(1)} collective-permute-done((bf16[256,256]{1,0:T(8,128)(2,1)S(1)}, bf16[256,256]{1,0:T(8,128)(2,1)S(1)}, u32[]{:S(2)}, u32[]{:S(2)}) %collective-permute-start.9) | collective-permute-done | bytes 131104 | tf_op jit(solution)/shard_map/ppermute | solution.py:391
  31.0 2.1 %collective-permute-done.8.refs_3_ = bf16[256,256]{1,0:T(8,128)(2,1)S(1)} collective-permute-done((bf16[256,256]{1,0:T(8,128)(2,1)S(1)}, bf16[256,256]{1,0:T(8,128)(2,1)S(1)}, u32[]{:S(2)}, u32[]{:S(2)}) %collective-permute-start.8) | collective-permute-done | bytes 131104 | tf_op jit(solution)/shard_map/ppermute | solution.py:391
  33.1 0.0 collective-permute-done.6.swapped
  33.1 4.0 %shard_map.70 = (f32[8,2048,128]{2,1,0:T(8,128)}, f32[4,2048,128]{2,1,0:T(8,128)S(1)}, f32[2,2048,128]{2,1,0:T(8,128)S(1)}) custom-call(bf16[4,256,256]{2,1,0:T(8,128)(2,1)S(1)} %get-tuple-element.20.own, bf16[8,256,256]{2,1,0:T(8,128)(2,1)S(1)} %get-tuple-element.21.mine, ...), custom_call_target="tpu_custom_call", output_to_operand_aliasing={{1}: (13, {}), {2}: (14, {})} | custom-call | tf_op jit(solution)/shard_map/pallas_call | solution.py:370
Async XLA Ops:
  4.0 19.8 %collective-permute-start = (bf16[8,256,256]{2,1,0:T(8,128)(2,1)S(1)}, bf16[8,256,256]{2,1,0:T(8,128)(2,1)S(1)}, u32[]{:S(2)}, u32[]{:S(2)}) collective-permute-start(bf16[8,256,256]{2,1,0:T(8,128)(2,1)S(1)} %get-tuple-element.21.mine), channel_id=1, source_target_pairs={{0,8},{1,9},{2,10},{3,11},{4,12},{5,13},{6,14},{7,15},{8,0},{9,1},... | collective-permute-start | bytes 3145736 | tf_op jit(solution)/shard_map/ppermute | solution.py:391
  4.6 6.9 %collective-permute-start.2 = (bf16[256,256]{1,0:T(8,128)(2,1)S(1)}, bf16[256,256]{1,0:T(8,128)(2,1)S(1)}, u32[]{:S(2)}, u32[]{:S(2)}) collective-permute-start(bf16[256,256]{1,0:T(8,128)(2,1)S(1)} %get-tuple-element.23), channel_id=1, source_target_pairs={{0,16},{1,17},{2,18},{3,19},{4,20},{5,21},{6,22},{7,23},{8,24},{9,... | collective-permute-start | bytes 393224 | tf_op jit(solution)/shard_map/ppermute | solution.py:391
  7.2 6.7 %collective-permute-start.4 = (bf16[256,256]{1,0:T(8,128)(2,1)S(1)}, bf16[256,256]{1,0:T(8,128)(2,1)S(1)}, u32[]{:S(2)}, u32[]{:S(2)}) collective-permute-start(bf16[256,256]{1,0:T(8,128)(2,1)S(1)} %get-tuple-element.24), channel_id=1, source_target_pairs={{0,24},{1,25},{2,26},{3,27},{4,28},{5,29},{6,30},{7,31},{8,16},{9,... | collective-permute-start | bytes 393224 | tf_op jit(solution)/shard_map/ppermute | solution.py:391
  7.2 12.6 %collective-permute-start.1 = (bf16[2,256,256]{2,1,0:T(8,128)(2,1)S(1)}, bf16[2,256,256]{2,1,0:T(8,128)(2,1)S(1)}, u32[]{:S(2)}, u32[]{:S(2)}) collective-permute-start(bf16[2,256,256]{2,1,0:T(8,128)(2,1)S(1)} %get-tuple-element.22), channel_id=1, source_target_pairs={{0,16},{1,17},{2,18},{3,19},{4,20},{5,21},{6,22},{7,23},{8,24},{9,... | collective-permute-start | bytes 786440 | tf_op jit(solution)/shard_map/ppermute | solution.py:391
  11.5 5.0 %collective-permute-start.3 = (bf16[256,256]{1,0:T(8,128)(2,1)S(1)}, bf16[256,256]{1,0:T(8,128)(2,1)S(1)}, u32[]{:S(2)}, u32[]{:S(2)}) collective-permute-start(bf16[256,256]{1,0:T(8,128)(2,1)S(1)} %collective-permute-done.2.refs_1_), channel_id=1, source_target_pairs={{0,1},{1,0},{2,3},{3,2},{4,5},{5,4},{6,7},{7,6},{8,9},{9,8},{10,11... | collective-permute-start | bytes 393224 | tf_op jit(solution)/shard_map/ppermute | solution.py:391
  13.9 5.9 %collective-permute-start.5 = (bf16[256,256]{1,0:T(8,128)(2,1)S(1)}, bf16[256,256]{1,0:T(8,128)(2,1)S(1)}, u32[]{:S(2)}, u32[]{:S(2)}) collective-permute-start(bf16[256,256]{1,0:T(8,128)(2,1)S(1)} %collective-permute-done.4.refs_3_), channel_id=1, source_target_pairs={{0,1},{1,0},{2,3},{3,2},{4,5},{5,4},{6,7},{7,6},{8,9},{9,8},{10,11... | collective-permute-start | bytes 393224 | tf_op jit(solution)/shard_map/ppermute | solution.py:391
  20.2 12.9 %collective-permute-start.6 = (bf16[1,2,2,256,256]{4,3,2,1,0:T(8,128)(2,1)S(1)}, bf16[1,2,2,256,256]{4,3,2,1,0:T(8,128)(2,1)S(1)}, u32[]{:S(2)}, u32[]{:S(2)}) collective-permute-start(bf16[1,2,2,256,256]{4,3,2,1,0:T(8,128)(2,1)S(1)} %get-tuple-element.26), channel_id=1, source_target_pairs={{0,8},{1,9},{2,10},{3,11},{4,12},{5,13},{6,14},{7,15},{8,0},{9,1},... | collective-permute-start | bytes 1572872 | tf_op jit(solution)/shard_map/ppermute | solution.py:391
  20.3 9.5 %collective-permute-start.10 = (bf16[256,256]{1,0:T(8,128)(2,1)S(1)}, bf16[256,256]{1,0:T(8,128)(2,1)S(1)}, u32[]{:S(2)}, u32[]{:S(2)}) collective-permute-start(bf16[256,256]{1,0:T(8,128)(2,1)S(1)} %get-tuple-element.28), channel_id=1, source_target_pairs={{0,24},{1,25},{2,26},{3,27},{4,28},{5,29},{6,30},{7,31},{8,16},{9,... | collective-permute-start | bytes 393224 | tf_op jit(solution)/shard_map/ppermute | solution.py:391
  21.8 8.0 %collective-permute-start.7 = (bf16[256,256]{1,0:T(8,128)(2,1)S(1)}, bf16[256,256]{1,0:T(8,128)(2,1)S(1)}, u32[]{:S(2)}, u32[]{:S(2)}) collective-permute-start(bf16[256,256]{1,0:T(8,128)(2,1)S(1)} %collective-permute-done.2.refs_1_), channel_id=1, source_target_pairs={{0,2},{1,3},{2,0},{3,1},{4,6},{5,7},{6,4},{7,5},{8,10},{9,11},{10,... | collective-permute-start | bytes 393224 | tf_op jit(solution)/shard_map/ppermute | solution.py:391
  23.7 7.3 %collective-permute-start.9 = (bf16[256,256]{1,0:T(8,128)(2,1)S(1)}, bf16[256,256]{1,0:T(8,128)(2,1)S(1)}, u32[]{:S(2)}, u32[]{:S(2)}) collective-permute-start(bf16[256,256]{1,0:T(8,128)(2,1)S(1)} %collective-permute-done.4.refs_3_), channel_id=1, source_target_pairs={{0,2},{1,3},{2,0},{3,1},{4,6},{5,7},{6,4},{7,5},{8,10},{9,11},{10,... | collective-permute-start | bytes 393224 | tf_op jit(solution)/shard_map/ppermute | solution.py:391
  23.9 9.2 %collective-permute-start.8 = (bf16[256,256]{1,0:T(8,128)(2,1)S(1)}, bf16[256,256]{1,0:T(8,128)(2,1)S(1)}, u32[]{:S(2)}, u32[]{:S(2)}) collective-permute-start(bf16[256,256]{1,0:T(8,128)(2,1)S(1)} %collective-permute-done.3.refs_2_), channel_id=1, source_target_pairs={{0,2},{1,3},{2,0},{3,1},{4,6},{5,7},{6,4},{7,5},{8,10},{9,11},{10,... | collective-permute-start | bytes 393224 | tf_op jit(solution)/shard_map/ppermute | solution.py:391

commit v5 on v4

--- a/solution.py
+++ b/solution.py
@@ -12,11 +12,16 @@
 SMEM = pl.BlockSpec(memory_space=pltpu.SMEM)
 VMEM = pl.BlockSpec(memory_space=pltpu.VMEM)
 LANES = 128
+COST = 4 * 10**9
 PIECES = 1
 
 
 def in_hbm(x):
     return pltpu.with_memory_space_constraint(x, pltpu.HBM)
+
+
+def in_vmem(x):
+    return pltpu.with_memory_space_constraint(x, pltpu.VMEM)
 
 
 class Plan:
@@ -222,16 +227,6 @@
         copies[-1].start()
 
 
-def load_kernel(plan, front, rest, sems):
-    _, _, group, _ = plan.here()
-    reads = []
-    for i in range(plan.rows_local - plan.row_cap):
-        a = (group * plan.row_cap + plan.row_cap + i) % plan.rows_local
-        in_pieces(front.at[a], rest.at[i], sems, reads)
-    for copy in reads:
-        copy.wait()
-
-
 def begin_kernel(plan, own, mine, theirs, base, total):
     row, col, group, _ = plan.here()
     rows = plan.row_cap * plan.block
@@ -250,7 +245,7 @@
 
 
 def even_kernel(plan, mine, theirs, *refs):
-    fars, (rest, even) = refs[:-2], refs[-2:]
+    fars, (front, even) = refs[:-2], refs[-2:]
     half = plan.half_cap
     _, col, group, _ = plan.here()
     parity = plan.parity(group, col)
@@ -259,7 +254,7 @@
         for s in range(plan.col_cap):
             value = matmul(far[0], mine[plan.row_cap + s]) + matmul(far[1], theirs[plan.row_cap + s])
             for j in range(half):
-                put_across(plan, rest, (d - 1) * plan.row_cap + 2 * j + parity,
+                put_across(plan, front, (group + d) % plan.halves * plan.row_cap + 2 * j + parity,
                            even, (d - 1) * half + j, group * plan.col_cap + s,
                            value[j * plan.block:(j + 1) * plan.block])
 
@@ -267,7 +262,7 @@
 def finish_kernel(plan, own, mine, theirs, formed, swapped, *refs):
     halves, half, turns = plan.halves, plan.half_cap, plan.halves - 1
     directs, fars, parts = refs[:turns], refs[turns: 2 * turns], refs[2 * turns: 6 * turns]
-    base, rest, _, _, out, near, even, odd, far, right, sems = refs[6 * turns:]
+    base, front, _, _, out, near, even, odd, far, right, sems = refs[6 * turns:]
     row, col, group, _ = plan.here()
     owns = plan.owns_diag(group, col)
     main = row == col % plan.rows_n
@@ -290,10 +285,10 @@
     def _():
         choose(lambda e, k, s: swapped[e, 0, s] if k else directs[e][s])
 
-    for s in range(plan.col_cap):
-        right[0, 0, s] = mine[plan.row_cap + s]
-        right[0, 1, s] = theirs[plan.row_cap + s]
     copies = []
+
+    def rights(e, k, s):
+        return right[e, k, s] if e else (mine, theirs)[k][plan.row_cap + s]
 
     def write(source, a):
         in_pieces(source, out.at[a], sems, copies)
@@ -302,31 +297,24 @@
         rows = pl.ds(start, len(places) * plan.block)
         for e in range(first, halves):
             for s in range(plan.col_cap):
-                value = matmul(left(0, rows), right[e, 0, s]) + matmul(left(1, rows), right[e, 1, s])
+                value = matmul(left(0, rows), rights(e, 0, s)) + matmul(left(1, rows), rights(e, 1, s))
                 b = (group + e) % halves * plan.col_cap + s
                 for j, (a, place) in enumerate(zip(sources, places)):
                     put_across(plan, source, a, total, place, b,
                                value[j * plan.block:(j + 1) * plan.block])
 
-    for g in range(2):
-        def left(k, rows):
-            value = (own, theirs)[k][pl.ds(g * half, half)]
-            return value.reshape(half * plan.block, plan.rank)
-
-        steps = range(g * half, g * half + half)
-        spread(left, 0, base, steps, near, steps, 1)
-        for q in steps:
-            write(near.at[q], group * plan.row_cap + q)
+    for q in range(plan.row_cap):
+        spread(lambda k, rows: (own, theirs)[k][q], 0, base, [q], near, [q], 1)
+        write(near.at[q], group * plan.row_cap + q)
     parity = plan.parity(group, col)
     for d in range(1, halves):
         places = range((d - 1) * half, d * half)
-        first = (d - 1) * plan.row_cap
         top = (group + d) % halves * plan.row_cap
 
         @pl.when(row >= 0)
         def _():
-            spread(lambda k, rows: fars[d - 1][k], 0, rest,
-                   [first + 2 * j + parity for j in range(half)], even, places, 1)
+            spread(lambda k, rows: fars[d - 1][k], 0, front,
+                   [top + 2 * j + parity for j in range(half)], even, places, 1)
 
         @pl.when(main)
         def _():
@@ -340,8 +328,8 @@
             here, there = parts[4 * (d - 1) + 2 * k: 4 * (d - 1) + 2 * k + 2]
             join(plan, far, k, here, there, col % 2)
         for j in range(half):
-            spread(lambda k, rows: far[k, rows, :], j * plan.block, rest,
-                   [first + 2 * j + 1 - parity], odd, [places[j]], 0)
+            spread(lambda k, rows: far[k, rows, :], j * plan.block, front,
+                   [top + 2 * j + 1 - parity], odd, [places[j]], 0)
             write(odd.at[places[j]], top + 2 * j + 1 - parity)
     for copy in copies:
         copy.wait()
@@ -371,6 +359,7 @@
             functools.partial(kernel, plan), out_shape=out_shape, in_specs=in_specs,
             out_specs=out_specs, scratch_shapes=scratch,
             input_output_aliases=aliases,
+            cost_estimate=pl.CostEstimate(flops=COST, bytes_accessed=1 << 20, transcendentals=0),
             compiler_params=pltpu.CompilerParams(vmem_limit_bytes=mib << 20))(*args)
 
     front = parent_front.reshape(rows_local, block, cols_local, parts, LANES)
@@ -424,10 +413,10 @@
         beside_[d, k] = send(near[d, k], beside)
         along_[d, k] = send(near[d, k], along)
     for d in turns:
-        far_[d, 0] = send(beside_[d, 0], along)
+        far_[d, 0] = send(along_[d, 0], beside)
         far_[d, 1] = send(far_outs[d - 1], across(d, 1))
     others = rows_local - row_cap
-    rest = call(load_kernel, strip(others), [ANY], VMEM, [sems(others * PIECES)], 12, (front,))
+    held = in_vmem(front)
     args = (own, mine, theirs, base)
     near_rows = call(begin_kernel, strip(row_cap), [VMEM] * 4, VMEM, [], 12, args)
     args = (mixers,) + tuple(direct[d] for d in turns) + tuple(
@@ -436,10 +425,10 @@
         project_kernel, [shape(halves - 1, 2, col_cap)] * 2 + [joined] * (halves - 1),
         [VMEM] * len(args), [VMEM] * (1 + halves), [], 12, args)
     swapped = send(leave, partner)
-    args = (mine, theirs, *fars, rest)
+    args = (mine, theirs, *fars, held)
     even = call(even_kernel, strip(others // 2), [VMEM] * len(args), VMEM, [], 12, args)
     args = (own, mine, theirs, formed, swapped, *(direct[d] for d in turns), *fars) + tuple(
-        x[flow] for flow in flows for x in (along_, far_)) + (base, rest, near_rows, even)
+        x[flow] for flow in flows for x in (along_, far_)) + (base, held, near_rows, even)
     n = len(args)
     out, _, _ = call(
         finish_kernel, [strip(rows_local), strip(row_cap), strip(others // 2)],

time: 37.3 us -> 32.1 us (0.86)
  waiting for transfers between devices: 10.7 us -> 7.06 us
  Pallas kernels: 12.5 us -> 10.1 us
  starting transfers between devices: 14 us -> 14.7 us
    ppermute x11, waiting for transfers between devices: 10.7 us -> 7.06 us  [send(): return lax.ppermute(x, ('row', 'col'), pairs)]
    pallas_call x7 -> x6, Pallas kernels: 12.5 us -> 10.1 us  [call(): pl.pallas_call(functools.partial(kernel, plan), out_shape=out_shape, in_s...]
    ppermute x11, starting transfers between devices: 14 us -> 14.7 us  [send(): return lax.ppermute(x, ('row', 'col'), pairs)]
  transfers between devices with their start and end apart: 11 -> 11, of which waited for: 6 -> 5; matrix products, arithmetic and copies ran while one was open for 0% -> 0% of each run, Pallas kernels for 12% -> 7%
where the time goes in v5:
time: 32.1 us; the launch traced here: 32 us
  starting transfers between devices  14.7 us (46%)
  Pallas kernels  10.1 us (31%)
  waiting for transfers between devices  7.06 us (22%)
    ppermute x11, starting transfers between devices, send(): return lax.ppermute(x, ('row', 'col'), pairs)  14.7 us
    pallas_call x6, Pallas kernels, call(): pl.pallas_call(functools.partial(kernel, plan), out_shape=out_shape, in_s...  10.1 us
    ppermute x11, waiting for transfers between devices, send(): return lax.ppermute(x, ('row', 'col'), pairs)  7.06 us
  transfers between devices with their start and end apart: 11, of which 5 were waited for; matrix products, arithmetic and copies ran while one was open for 0% of the time, Pallas kernels for 7%

profile of v5, /device:TPU:0, one launch (start us, length us, event | category | flops | bytes accessed | tf_op | source)
XLA Modules:
  0.0 32.0 jit_solution(13869890769776992235)
XLA Ops:
  0.0 1.5 %shard_map.64 = (bf16[12,256,256]{2,1,0:T(8,128)(2,1)S(1)}, bf16[2,256,256]{2,1,0:T(8,128)(2,1)S(1)}, bf16[256,256]{1,0:T(8,128)(2,1)S(1)}, bf16[256,256]{1,0:T(8,128)(2,1)S(1)}) custom-call(s32[2,24]{1,0:T(2,128)} %block_map.3, s32[2,24]{1,0:T(2,128)} %valid_rows.3, bf16[12,256,256]{2,1,0:T(8,128)(2,1)} %generators.1, bf16[2,256,256]{2,1,0:T(8,128)(2,1)} %coupling.1), custom_call_target="tpu_custom_call" | custom-call | flops 4000000000 | bytes 1048576 | tf_op jit(solution)/shard_map/pallas_call | solution.py:358
  1.5 0.0 slice-start
  1.5 2.7 %shard_map.65 = (bf16[8,256,256]{2,1,0:T(8,128)(2,1)S(1)}, bf16[4,256,256]{2,1,0:T(8,128)(2,1)S(1)}, f32[4,2048,128]{2,1,0:T(8,128)S(1)}, bf16[256,256]{1,0:T(8,128)(2,1)S(1)}, bf16[2,256,256]{2,1,0:T(8,128)(2,1)S(1)}) custom-call(s32[2,24]{1,0:T(2,128)} %block_map.3, s32[2,24]{1,0:T(2,128)} %valid_rows.3, ...), custom_call_target="tpu_custom_call" | custom-call | flops 4000000000 | bytes 1048576 | tf_op jit(solution)/shard_map/pallas_call | solution.py:358
  4.2 0.6 %collective-permute-start = (bf16[8,256,256]{2,1,0:T(8,128)(2,1)S(1)}, bf16[8,256,256]{2,1,0:T(8,128)(2,1)S(1)}, u32[]{:S(2)}, u32[]{:S(2)}) collective-permute-start(bf16[8,256,256]{2,1,0:T(8,128)(2,1)S(1)} %get-tuple-element.21.mine), channel_id=1, source_target_pairs={{0,8},{1,9},{2,10},{3,11},{4,12},{5,13},{6,14},{7,15},{8,0},{9,1},... | collective-permute-start | bytes 3145736 | tf_op jit(solution)/shard_map/ppermute | solution.py:380
  4.7 2.6 %collective-permute-start.2 = (bf16[256,256]{1,0:T(8,128)(2,1)S(1)}, bf16[256,256]{1,0:T(8,128)(2,1)S(1)}, u32[]{:S(2)}, u32[]{:S(2)}) collective-permute-start(bf16[256,256]{1,0:T(8,128)(2,1)S(1)} %get-tuple-element.23), channel_id=1, source_target_pairs={{0,16},{1,17},{2,18},{3,19},{4,20},{5,21},{6,22},{7,23},{8,24},{9,... | collective-permute-start | bytes 393224 | tf_op jit(solution)/shard_map/ppermute | solution.py:380
  7.3 0.0 slice-start.1
  7.3 0.0 collective-permute-start.4
  7.4 1.7 %collective-permute-start.1 = (bf16[2,256,256]{2,1,0:T(8,128)(2,1)S(1)}, bf16[2,256,256]{2,1,0:T(8,128)(2,1)S(1)}, u32[]{:S(2)}, u32[]{:S(2)}) collective-permute-start(bf16[2,256,256]{2,1,0:T(8,128)(2,1)S(1)} %get-tuple-element.22), channel_id=1, source_target_pairs={{0,16},{1,17},{2,18},{3,19},{4,20},{5,21},{6,22},{7,23},{8,24},{9,... | collective-permute-start | bytes 786440 | tf_op jit(solution)/shard_map/ppermute | solution.py:380
  9.1 2.6 %collective-permute-done.2.refs_1_ = bf16[256,256]{1,0:T(8,128)(2,1)S(1)} collective-permute-done((bf16[256,256]{1,0:T(8,128)(2,1)S(1)}, bf16[256,256]{1,0:T(8,128)(2,1)S(1)}, u32[]{:S(2)}, u32[]{:S(2)}) %collective-permute-start.2) | collective-permute-done | bytes 131104 | tf_op jit(solution)/shard_map/ppermute | solution.py:380
  11.7 2.0 %collective-permute-start.3 = (bf16[256,256]{1,0:T(8,128)(2,1)S(1)}, bf16[256,256]{1,0:T(8,128)(2,1)S(1)}, u32[]{:S(2)}, u32[]{:S(2)}) collective-permute-start(bf16[256,256]{1,0:T(8,128)(2,1)S(1)} %collective-permute-done.2.refs_1_), channel_id=1, source_target_pairs={{0,1},{1,0},{2,3},{3,2},{4,5},{5,4},{6,7},{7,6},{8,9},{9,8},{10,11... | collective-permute-start | bytes 393224 | tf_op jit(solution)/shard_map/ppermute | solution.py:380
  13.7 0.4 %collective-permute-done.4.refs_3_ = bf16[256,256]{1,0:T(8,128)(2,1)S(1)} collective-permute-done((bf16[256,256]{1,0:T(8,128)(2,1)S(1)}, bf16[256,256]{1,0:T(8,128)(2,1)S(1)}, u32[]{:S(2)}, u32[]{:S(2)}) %collective-permute-start.4) | collective-permute-done | bytes 131104 | tf_op jit(solution)/shard_map/ppermute | solution.py:380
  14.0 1.5 %collective-permute-start.5 = (bf16[256,256]{1,0:T(8,128)(2,1)S(1)}, bf16[256,256]{1,0:T(8,128)(2,1)S(1)}, u32[]{:S(2)}, u32[]{:S(2)}) collective-permute-start(bf16[256,256]{1,0:T(8,128)(2,1)S(1)} %collective-permute-done.4.refs_3_), channel_id=1, source_target_pairs={{0,1},{1,0},{2,3},{3,2},{4,5},{5,4},{6,7},{7,6},{8,9},{9,8},{10,11... | collective-permute-start | bytes 393224 | tf_op jit(solution)/shard_map/ppermute | solution.py:380
  15.5 1.6 %collective-permute-start.10 = (bf16[256,256]{1,0:T(8,128)(2,1)S(1)}, bf16[256,256]{1,0:T(8,128)(2,1)S(1)}, u32[]{:S(2)}, u32[]{:S(2)}) collective-permute-start(bf16[256,256]{1,0:T(8,128)(2,1)S(1)} %get-tuple-element.28), channel_id=1, source_target_pairs={{0,24},{1,25},{2,26},{3,27},{4,28},{5,29},{6,30},{7,31},{8,16},{9,... | collective-permute-start | bytes 393224 | tf_op jit(solution)/shard_map/ppermute | solution.py:380
  17.1 0.0 collective-permute-done.3.refs_2_
  17.2 1.6 %collective-permute-start.7 = (bf16[256,256]{1,0:T(8,128)(2,1)S(1)}, bf16[256,256]{1,0:T(8,128)(2,1)S(1)}, u32[]{:S(2)}, u32[]{:S(2)}) collective-permute-start(bf16[256,256]{1,0:T(8,128)(2,1)S(1)} %collective-permute-done.2.refs_1_), channel_id=1, source_target_pairs={{0,2},{1,3},{2,0},{3,1},{4,6},{5,7},{6,4},{7,5},{8,10},{9,11},{10,... | collective-permute-start | bytes 393224 | tf_op jit(solution)/shard_map/ppermute | solution.py:380
  18.7 1.2 %collective-permute-done.5.refs_4_ = bf16[256,256]{1,0:T(8,128)(2,1)S(1)} collective-permute-done((bf16[256,256]{1,0:T(8,128)(2,1)S(1)}, bf16[256,256]{1,0:T(8,128)(2,1)S(1)}, u32[]{:S(2)}, u32[]{:S(2)}) %collective-permute-start.5) | collective-permute-done | bytes 131104 | tf_op jit(solution)/shard_map/ppermute | solution.py:380
  20.0 1.8 %collective-permute-start.9 = (bf16[256,256]{1,0:T(8,128)(2,1)S(1)}, bf16[256,256]{1,0:T(8,128)(2,1)S(1)}, u32[]{:S(2)}, u32[]{:S(2)}) collective-permute-start(bf16[256,256]{1,0:T(8,128)(2,1)S(1)} %collective-permute-done.4.refs_3_), channel_id=1, source_target_pairs={{0,2},{1,3},{2,0},{3,1},{4,6},{5,7},{6,4},{7,5},{8,10},{9,11},{10,... | collective-permute-start | bytes 393224 | tf_op jit(solution)/shard_map/ppermute | solution.py:380
  21.8 0.0 collective-permute-done.1.refs_0_
  21.8 0.4 %shard_map.66 = (bf16[1,2,2,256,256]{4,3,2,1,0:T(8,128)(2,1)S(1)}, bf16[1,2,2,256,256]{4,3,2,1,0:T(8,128)(2,1)S(1)}, bf16[2,512,256]{2,1,0:T(8,128)(2,1)S(1)}) custom-call(bf16[2,256,256]{2,1,0:T(8,128)(2,1)S(1)} %get-tuple-element.19.mixers.coupling, bf16[2,256,256]{2,1,0:T(8,128)(2,1)S(1)} %collective-permute-done.1.refs_0_, ...), custom_call_target="tpu_custom_call" | custom-call | flops 4000000000 | bytes 1048576 | tf_op jit(solution)/shard_map/pallas_call | solution.py:358
  22.2 0.1 collective-permute-start.6
  22.3 0.2 collective-permute-done.7.refs_2_
  22.4 1.2 %collective-permute-start.8 = (bf16[256,256]{1,0:T(8,128)(2,1)S(1)}, bf16[256,256]{1,0:T(8,128)(2,1)S(1)}, u32[]{:S(2)}, u32[]{:S(2)}) collective-permute-start(bf16[256,256]{1,0:T(8,128)(2,1)S(1)} %collective-permute-done.7.refs_2_), channel_id=1, source_target_pairs={{0,1},{1,0},{2,3},{3,2},{4,5},{5,4},{6,7},{7,6},{8,9},{9,8},{10,11... | collective-permute-start | bytes 393224 | tf_op jit(solution)/shard_map/ppermute | solution.py:380
  23.6 0.0 collective-permute-done.theirs
  23.6 0.0 slice-done
  23.6 0.0 slice-done.1
  23.6 0.6 %shard_map.68.refs_9_ = f32[2,2048,128]{2,1,0:T(8,128)S(1)} custom-call(bf16[8,256,256]{2,1,0:T(8,128)(2,1)S(1)} %get-tuple-element.21.mine, bf16[8,256,256]{2,1,0:T(8,128)(2,1)S(1)} %collective-permute-done.theirs, bf16[2,512,256]{2,1,0:T(8,128)(2,1)S(1)} %get-tuple-element.27.refs_0_.refs_1_, f32[8,2048,128]{2,1,0:T(8,128)S(1)} %bitcast.13), custom_call_target="tpu_custom_call" | custom-call | flops 4000000000 | bytes 1048576 | tf_op jit(solution)/shard_map/pallas_call | solution.py:358
  24.2 1.2 %shard_map.67.refs_8_ = f32[4,2048,128]{2,1,0:T(8,128)S(1)} custom-call(bf16[4,256,256]{2,1,0:T(8,128)(2,1)S(1)} %get-tuple-element.20.own, bf16[8,256,256]{2,1,0:T(8,128)(2,1)S(1)} %get-tuple-element.21.mine, bf16[8,256,256]{2,1,0:T(8,128)(2,1)S(1)} %collective-permute-done.theirs, f32[4,2048,128]{2,1,0:T(8,128)S(1)} %get-tuple-element.29.base.refs_6_), custom_call_target="tpu_custom_call" | custom-call | flops 4000000000 | bytes 1048576 | tf_op jit(solution)/shard_map/pallas_call | solution.py:358
  25.4 0.0 collective-permute-done.10.refs_5_
  25.4 0.0 collective-permute-done.9.refs_4_
  25.5 2.7 %collective-permute-done.8.refs_3_ = bf16[256,256]{1,0:T(8,128)(2,1)S(1)} collective-permute-done((bf16[256,256]{1,0:T(8,128)(2,1)S(1)}, bf16[256,256]{1,0:T(8,128)(2,1)S(1)}, u32[]{:S(2)}, u32[]{:S(2)}) %collective-permute-start.8) | collective-permute-done | bytes 131104 | tf_op jit(solution)/shard_map/ppermute | solution.py:380
  28.2 0.0 collective-permute-done.6.swapped
  28.2 3.8 %shard_map.69 = (f32[8,2048,128]{2,1,0:T(8,128)}, f32[4,2048,128]{2,1,0:T(8,128)S(1)}, f32[2,2048,128]{2,1,0:T(8,128)S(1)}) custom-call(bf16[4,256,256]{2,1,0:T(8,128)(2,1)S(1)} %get-tuple-element.20.own, bf16[8,256,256]{2,1,0:T(8,128)(2,1)S(1)} %get-tuple-element.21.mine, ...), custom_call_target="tpu_custom_call", output_to_operand_aliasing={{1}: (13, {}), {2}: (14, {})} | custom-call | flops 4000000000 | bytes 1048576 | tf_op jit(solution)/shard_map/pallas_call | solution.py:358
  (1 shorter events, 0.0 us)
Async XLA Ops:
  1.5 22.1 %slice-start = ((s8[8388608]{0:T(1024)(128)(4,1)}), s8[4194304]{0:T(1024)(128)(4,1)S(1)}, s32[]{:S(2)}) async-start(s8[8388608]{0:T(1024)(128)(4,1)} %bitcast.11), calls=%async_computation | async-start | bytes 8388608
  4.2 19.4 %collective-permute-start = (bf16[8,256,256]{2,1,0:T(8,128)(2,1)S(1)}, bf16[8,256,256]{2,1,0:T(8,128)(2,1)S(1)}, u32[]{:S(2)}, u32[]{:S(2)}) collective-permute-start(bf16[8,256,256]{2,1,0:T(8,128)(2,1)S(1)} %get-tuple-element.21.mine), channel_id=1, source_target_pairs={{0,8},{1,9},{2,10},{3,11},{4,12},{5,13},{6,14},{7,15},{8,0},{9,1},... | collective-permute-start | bytes 3145736 | tf_op jit(solution)/shard_map/ppermute | solution.py:380
  4.7 6.9 %collective-permute-start.2 = (bf16[256,256]{1,0:T(8,128)(2,1)S(1)}, bf16[256,256]{1,0:T(8,128)(2,1)S(1)}, u32[]{:S(2)}, u32[]{:S(2)}) collective-permute-start(bf16[256,256]{1,0:T(8,128)(2,1)S(1)} %get-tuple-element.23), channel_id=1, source_target_pairs={{0,16},{1,17},{2,18},{3,19},{4,20},{5,21},{6,22},{7,23},{8,24},{9,... | collective-permute-start | bytes 393224 | tf_op jit(solution)/shard_map/ppermute | solution.py:380
  7.3 16.3 %slice-start.1 = ((s8[8388608]{0:T(1024)(128)(4,1)}), s8[4194304]{0:T(1024)(128)(4,1)S(1)}, s32[]{:S(2)}) async-start(s8[8388608]{0:T(1024)(128)(4,1)} %bitcast.11), calls=%async_computation.1 | async-start | bytes 8388608
  7.3 6.7 %collective-permute-start.4 = (bf16[256,256]{1,0:T(8,128)(2,1)S(1)}, bf16[256,256]{1,0:T(8,128)(2,1)S(1)}, u32[]{:S(2)}, u32[]{:S(2)}) collective-permute-start(bf16[256,256]{1,0:T(8,128)(2,1)S(1)} %get-tuple-element.24), channel_id=1, source_target_pairs={{0,24},{1,25},{2,26},{3,27},{4,28},{5,29},{6,30},{7,31},{8,16},{9,... | collective-permute-start | bytes 393224 | tf_op jit(solution)/shard_map/ppermute | solution.py:380
  7.4 14.4 %collective-permute-start.1 = (bf16[2,256,256]{2,1,0:T(8,128)(2,1)S(1)}, bf16[2,256,256]{2,1,0:T(8,128)(2,1)S(1)}, u32[]{:S(2)}, u32[]{:S(2)}) collective-permute-start(bf16[2,256,256]{2,1,0:T(8,128)(2,1)S(1)} %get-tuple-element.22), channel_id=1, source_target_pairs={{0,16},{1,17},{2,18},{3,19},{4,20},{5,21},{6,22},{7,23},{8,24},{9,... | collective-permute-start | bytes 786440 | tf_op jit(solution)/shard_map/ppermute | solution.py:380
  11.7 5.5 %collective-permute-start.3 = (bf16[256,256]{1,0:T(8,128)(2,1)S(1)}, bf16[256,256]{1,0:T(8,128)(2,1)S(1)}, u32[]{:S(2)}, u32[]{:S(2)}) collective-permute-start(bf16[256,256]{1,0:T(8,128)(2,1)S(1)} %collective-permute-done.2.refs_1_), channel_id=1, source_target_pairs={{0,1},{1,0},{2,3},{3,2},{4,5},{5,4},{6,7},{7,6},{8,9},{9,8},{10,11... | collective-permute-start | bytes 393224 | tf_op jit(solution)/shard_map/ppermute | solution.py:380
  14.0 5.9 %collective-permute-start.5 = (bf16[256,256]{1,0:T(8,128)(2,1)S(1)}, bf16[256,256]{1,0:T(8,128)(2,1)S(1)}, u32[]{:S(2)}, u32[]{:S(2)}) collective-permute-start(bf16[256,256]{1,0:T(8,128)(2,1)S(1)} %collective-permute-done.4.refs_3_), channel_id=1, source_target_pairs={{0,1},{1,0},{2,3},{3,2},{4,5},{5,4},{6,7},{7,6},{8,9},{9,8},{10,11... | collective-permute-start | bytes 393224 | tf_op jit(solution)/shard_map/ppermute | solution.py:380
  15.5 9.9 %collective-permute-start.10 = (bf16[256,256]{1,0:T(8,128)(2,1)S(1)}, bf16[256,256]{1,0:T(8,128)(2,1)S(1)}, u32[]{:S(2)}, u32[]{:S(2)}) collective-permute-start(bf16[256,256]{1,0:T(8,128)(2,1)S(1)} %get-tuple-element.28), channel_id=1, source_target_pairs={{0,24},{1,25},{2,26},{3,27},{4,28},{5,29},{6,30},{7,31},{8,16},{9,... | collective-permute-start | bytes 393224 | tf_op jit(solution)/shard_map/ppermute | solution.py:380
  17.2 5.3 %collective-permute-start.7 = (bf16[256,256]{1,0:T(8,128)(2,1)S(1)}, bf16[256,256]{1,0:T(8,128)(2,1)S(1)}, u32[]{:S(2)}, u32[]{:S(2)}) collective-permute-start(bf16[256,256]{1,0:T(8,128)(2,1)S(1)} %collective-permute-done.2.refs_1_), channel_id=1, source_target_pairs={{0,2},{1,3},{2,0},{3,1},{4,6},{5,7},{6,4},{7,5},{8,10},{9,11},{10,... | collective-permute-start | bytes 393224 | tf_op jit(solution)/shard_map/ppermute | solution.py:380
  20.0 5.5 %collective-permute-start.9 = (bf16[256,256]{1,0:T(8,128)(2,1)S(1)}, bf16[256,256]{1,0:T(8,128)(2,1)S(1)}, u32[]{:S(2)}, u32[]{:S(2)}) collective-permute-start(bf16[256,256]{1,0:T(8,128)(2,1)S(1)} %collective-permute-done.4.refs_3_), channel_id=1, source_target_pairs={{0,2},{1,3},{2,0},{3,1},{4,6},{5,7},{6,4},{7,5},{8,10},{9,11},{10,... | collective-permute-start | bytes 393224 | tf_op jit(solution)/shard_map/ppermute | solution.py:380
  22.2 6.0 %collective-permute-start.6 = (bf16[1,2,2,256,256]{4,3,2,1,0:T(8,128)(2,1)S(1)}, bf16[1,2,2,256,256]{4,3,2,1,0:T(8,128)(2,1)S(1)}, u32[]{:S(2)}, u32[]{:S(2)}) collective-permute-start(bf16[1,2,2,256,256]{4,3,2,1,0:T(8,128)(2,1)S(1)} %get-tuple-element.26), channel_id=1, source_target_pairs={{0,8},{1,9},{2,10},{3,11},{4,12},{5,13},{6,14},{7,15},{8,0},{9,1},... | collective-permute-start | bytes 1572872 | tf_op jit(solution)/shard_map/ppermute | solution.py:380
  22.4 5.7 %collective-permute-start.8 = (bf16[256,256]{1,0:T(8,128)(2,1)S(1)}, bf16[256,256]{1,0:T(8,128)(2,1)S(1)}, u32[]{:S(2)}, u32[]{:S(2)}) collective-permute-start(bf16[256,256]{1,0:T(8,128)(2,1)S(1)} %collective-permute-done.7.refs_2_), channel_id=1, source_target_pairs={{0,1},{1,0},{2,3},{3,2},{4,5},{5,4},{6,7},{7,6},{8,9},{9,8},{10,11... | collective-permute-start | bytes 393224 | tf_op jit(solution)/shard_map/ppermute | solution.py:380

commit v6 on v5

--- a/solution.py
+++ b/solution.py
@@ -114,8 +114,8 @@
     copies[3].wait()
 
 
-def pack_rest_kernel(plan, block_map, valid_rows, every, mixers, diagonal, front,
-                     mine, own, base, *refs):
+def pack_rest_kernel(plan, block_map, valid_rows, every, mixers, diagonal,
+                     mine, own, *refs):
     turns = plan.halves - 1
     far_outs, outs, (map_s, valid_s, where, count, sems) = refs[:turns], refs[turns:-5], refs[-5:]
     row, col, group, child = plan.here()
@@ -123,8 +123,7 @@
     copies = [
         pltpu.make_async_copy(source, target, sems.at[i])
         for i, (source, target) in enumerate(
-            ((block_map, map_s), (valid_rows, valid_s),
-             (front.at[pl.ds(group * plan.row_cap, plan.row_cap)], base)))
+            ((block_map, map_s), (valid_rows, valid_s)))
     ]
     for copy in copies:
         copy.start()
@@ -134,7 +133,7 @@
     loads = []
     for s in range(plan.col_cap):
         source = diagonal.at[where[s * plan.cols_n + col]]
-        loads.append(pltpu.make_async_copy(source, mine.at[diags + s], sems.at[3 + s]))
+        loads.append(pltpu.make_async_copy(source, mine.at[diags + s], sems.at[2 + s]))
         loads[-1].start()
     for s in range(plan.col_cap):
         slot = s * plan.cols_n + col
@@ -165,8 +164,6 @@
             for s in range(plan.col_cap):
                 out[s] = mine[plan.row_cap + s]
 
-    copies[2].wait()
-
 
 def join(plan, target, k, here, there, side):
     first = pl.multiple_of(side * plan.unit, plan.unit)
@@ -214,11 +211,6 @@
     put_across(plan, base, a, total, a, b, value)
 
 
-def put_tiles(plan, base, total, steps, b, value):
-    for j, a in enumerate(steps):
-        put_tile(plan, base, total, a, b, value[j * plan.block:(j + 1) * plan.block])
-
-
 def in_pieces(source, target, sems, copies):
     step = source.shape[0] // PIECES
     for i in range(PIECES):
@@ -227,14 +219,16 @@
         copies[-1].start()
 
 
-def begin_kernel(plan, own, mine, theirs, base, total):
+def begin_kernel(plan, own, mine, theirs, front, total):
     row, col, group, _ = plan.here()
     rows = plan.row_cap * plan.block
     left = own[...].reshape(rows, plan.rank)
     right = theirs[pl.ds(0, plan.row_cap)].reshape(rows, plan.rank)
     for s in range(plan.col_cap):
         value = matmul(left, mine[plan.row_cap + s]) + matmul(right, theirs[plan.row_cap + s])
-        put_tiles(plan, base, total, range(plan.row_cap), group * plan.col_cap + s, value)
+        for q in range(plan.row_cap):
+            put_across(plan, front, group * plan.row_cap + q, total, q, group * plan.col_cap + s,
+                       value[q * plan.block:(q + 1) * plan.block])
 
     @pl.when(row == col % plan.rows_n)
     def _():
@@ -262,7 +256,7 @@
 def finish_kernel(plan, own, mine, theirs, formed, swapped, *refs):
     halves, half, turns = plan.halves, plan.half_cap, plan.halves - 1
     directs, fars, parts = refs[:turns], refs[turns: 2 * turns], refs[2 * turns: 6 * turns]
-    base, front, _, _, out, near, even, odd, far, right, sems = refs[6 * turns:]
+    front, _, _, out, near, even, odd, far, right, sems = refs[6 * turns:]
     row, col, group, _ = plan.here()
     owns = plan.owns_diag(group, col)
     main = row == col % plan.rows_n
@@ -304,7 +298,8 @@
                                value[j * plan.block:(j + 1) * plan.block])
 
     for q in range(plan.row_cap):
-        spread(lambda k, rows: (own, theirs)[k][q], 0, base, [q], near, [q], 1)
+        spread(lambda k, rows: (own, theirs)[k][q], 0, front,
+               [group * plan.row_cap + q], near, [q], 1)
         write(near.at[q], group * plan.row_cap + q)
     parity = plan.parity(group, col)
     for d in range(1, halves):
@@ -392,6 +387,7 @@
         return row, col ^ halves
 
     flows = [(d, k) for d in turns for k in range(2)]
+    held = in_vmem(front)
     maps = [pltpu.SMEM(block_map.shape, jnp.int32)] * 2 + [table] * 2
     every, mixers, *rows_out = call(
         pack_rows_kernel, [shape(blocks), shape(2)] + [unit] * len(flows), [ANY] * 4,
@@ -400,12 +396,12 @@
     near, beside_, along_, far_ = {}, {}, {}, {}
     for (d, k), x in zip(flows, rows_out):
         near[d, k] = send(x, across(d, k))
-    mine, own, base, *sent = call(
+    mine, own, *sent = call(
         pack_rest_kernel,
-        [shape(row_cap + 2 * col_cap), shape(row_cap), strip(row_cap)]
+        [shape(row_cap + 2 * col_cap), shape(row_cap)]
         + [unit] * (halves - 1) + [shape(col_cap)] * (halves - 1),
-        [ANY, ANY, VMEM, VMEM, ANY, ANY], [VMEM] * (2 * halves + 1), maps + [sems(3 + col_cap)], 12,
-        (block_map, valid_rows, every, mixers, diagonal_blocks, front))
+        [ANY, ANY, VMEM, VMEM, ANY], [VMEM] * (2 * halves), maps + [sems(2 + col_cap)], 12,
+        (block_map, valid_rows, every, mixers, diagonal_blocks))
     far_outs, cols_out = sent[: halves - 1], sent[halves - 1:]
     direct = {d: send(cols_out[d - 1], across(d, 0)) for d in turns}
     theirs = send(mine, partner)
@@ -416,8 +412,7 @@
         far_[d, 0] = send(along_[d, 0], beside)
         far_[d, 1] = send(far_outs[d - 1], across(d, 1))
     others = rows_local - row_cap
-    held = in_vmem(front)
-    args = (own, mine, theirs, base)
+    args = (own, mine, theirs, held)
     near_rows = call(begin_kernel, strip(row_cap), [VMEM] * 4, VMEM, [], 12, args)
     args = (mixers,) + tuple(direct[d] for d in turns) + tuple(
         x[flow] for flow in flows for x in (near, beside_))
@@ -428,7 +423,7 @@
     args = (mine, theirs, *fars, held)
     even = call(even_kernel, strip(others // 2), [VMEM] * len(args), VMEM, [], 12, args)
     args = (own, mine, theirs, formed, swapped, *(direct[d] for d in turns), *fars) + tuple(
-        x[flow] for flow in flows for x in (along_, far_)) + (base, held, near_rows, even)
+        x[flow] for flow in flows for x in (along_, far_)) + (held, near_rows, even)
     n = len(args)
     out, _, _ = call(
         finish_kernel, [strip(rows_local), strip(row_cap), strip(others // 2)],

time: 32.1 us -> 31.8 us (level)
  Pallas kernels: 10.1 us -> 9.76 us
    pallas_call x6, Pallas kernels: 10.1 us -> 9.76 us  [call(): pl.pallas_call(functools.partial(kernel, plan), out_shape=out_shape, in_s...]
where the time goes in v6:
time: 31.8 us; the launch traced here: 31.6 us
  starting transfers between devices  14.7 us (46%)
  Pallas kernels  9.76 us (31%)
  waiting for transfers between devices  7.06 us (22%)
    ppermute x11, starting transfers between devices, send(): return lax.ppermute(x, ('row', 'col'), pairs)  14.7 us
    pallas_call x6, Pallas kernels, call(): pl.pallas_call(functools.partial(kernel, plan), out_shape=out_shape, in_s...  9.76 us
    ppermute x11, waiting for transfers between devices, send(): return lax.ppermute(x, ('row', 'col'), pairs)  7.06 us
  transfers between devices with their start and end apart: 11, of which 5 were waited for; matrix products, arithmetic and copies ran while one was open for 0% of the time, Pallas kernels for 7%

profile of v6, /device:TPU:0, one launch (start us, length us, event | category | flops | bytes accessed | tf_op | source)
XLA Modules:
  0.0 31.6 jit_solution(7084561058029769917)
XLA Ops:
  0.0 1.5 %shard_map.64 = (bf16[12,256,256]{2,1,0:T(8,128)(2,1)S(1)}, bf16[2,256,256]{2,1,0:T(8,128)(2,1)S(1)}, bf16[256,256]{1,0:T(8,128)(2,1)S(1)}, bf16[256,256]{1,0:T(8,128)(2,1)S(1)}) custom-call(s32[2,24]{1,0:T(2,128)} %block_map.3, s32[2,24]{1,0:T(2,128)} %valid_rows.3, bf16[12,256,256]{2,1,0:T(8,128)(2,1)} %generators.1, bf16[2,256,256]{2,1,0:T(8,128)(2,1)} %coupling.1), custom_call_target="tpu_custom_call" | custom-call | flops 4000000000 | bytes 1048576 | tf_op jit(solution)/shard_map/pallas_call | solution.py:353
  1.5 0.0 slice-start
  1.5 2.3 %shard_map.65 = (bf16[8,256,256]{2,1,0:T(8,128)(2,1)S(1)}, bf16[4,256,256]{2,1,0:T(8,128)(2,1)S(1)}, bf16[256,256]{1,0:T(8,128)(2,1)S(1)}, bf16[2,256,256]{2,1,0:T(8,128)(2,1)S(1)}) custom-call(s32[2,24]{1,0:T(2,128)} %block_map.3, s32[2,24]{1,0:T(2,128)} %valid_rows.3, bf16[12,256,256]{2,1,0:T(8,128)(2,1)S(1)} %get-tuple-element.17.every, ...), custom_call_target="tpu_custom_call" | custom-call | flops 4000000000 | bytes 1048576 | tf_op jit(solution)/shard_map/pallas_call | solution.py:353
  3.8 0.6 %collective-permute-start = (bf16[8,256,256]{2,1,0:T(8,128)(2,1)S(1)}, bf16[8,256,256]{2,1,0:T(8,128)(2,1)S(1)}, u32[]{:S(2)}, u32[]{:S(2)}) collective-permute-start(bf16[8,256,256]{2,1,0:T(8,128)(2,1)S(1)} %get-tuple-element.20.mine), channel_id=1, source_target_pairs={{0,8},{1,9},{2,10},{3,11},{4,12},{5,13},{6,14},{7,15},{8,0},{9,1},... | collective-permute-start | bytes 3145736 | tf_op jit(solution)/shard_map/ppermute | solution.py:375
  4.4 2.6 %collective-permute-start.2 = (bf16[256,256]{1,0:T(8,128)(2,1)S(1)}, bf16[256,256]{1,0:T(8,128)(2,1)S(1)}, u32[]{:S(2)}, u32[]{:S(2)}) collective-permute-start(bf16[256,256]{1,0:T(8,128)(2,1)S(1)} %get-tuple-element.22), channel_id=1, source_target_pairs={{0,16},{1,17},{2,18},{3,19},{4,20},{5,21},{6,22},{7,23},{8,24},{9,... | collective-permute-start | bytes 393224 | tf_op jit(solution)/shard_map/ppermute | solution.py:375
  6.9 0.0 collective-permute-start.4
  7.0 0.0 slice-start.1
  7.0 1.7 %collective-permute-start.1 = (bf16[2,256,256]{2,1,0:T(8,128)(2,1)S(1)}, bf16[2,256,256]{2,1,0:T(8,128)(2,1)S(1)}, u32[]{:S(2)}, u32[]{:S(2)}) collective-permute-start(bf16[2,256,256]{2,1,0:T(8,128)(2,1)S(1)} %get-tuple-element.21), channel_id=1, source_target_pairs={{0,16},{1,17},{2,18},{3,19},{4,20},{5,21},{6,22},{7,23},{8,24},{9,... | collective-permute-start | bytes 786440 | tf_op jit(solution)/shard_map/ppermute | solution.py:375
  8.7 2.6 %collective-permute-done.2.refs_1_ = bf16[256,256]{1,0:T(8,128)(2,1)S(1)} collective-permute-done((bf16[256,256]{1,0:T(8,128)(2,1)S(1)}, bf16[256,256]{1,0:T(8,128)(2,1)S(1)}, u32[]{:S(2)}, u32[]{:S(2)}) %collective-permute-start.2) | collective-permute-done | bytes 131104 | tf_op jit(solution)/shard_map/ppermute | solution.py:375
  11.3 2.0 %collective-permute-start.3 = (bf16[256,256]{1,0:T(8,128)(2,1)S(1)}, bf16[256,256]{1,0:T(8,128)(2,1)S(1)}, u32[]{:S(2)}, u32[]{:S(2)}) collective-permute-start(bf16[256,256]{1,0:T(8,128)(2,1)S(1)} %collective-permute-done.2.refs_1_), channel_id=1, source_target_pairs={{0,1},{1,0},{2,3},{3,2},{4,5},{5,4},{6,7},{7,6},{8,9},{9,8},{10,11... | collective-permute-start | bytes 393224 | tf_op jit(solution)/shard_map/ppermute | solution.py:375
  13.3 0.4 %collective-permute-done.4.refs_3_ = bf16[256,256]{1,0:T(8,128)(2,1)S(1)} collective-permute-done((bf16[256,256]{1,0:T(8,128)(2,1)S(1)}, bf16[256,256]{1,0:T(8,128)(2,1)S(1)}, u32[]{:S(2)}, u32[]{:S(2)}) %collective-permute-start.4) | collective-permute-done | bytes 131104 | tf_op jit(solution)/shard_map/ppermute | solution.py:375
  13.6 1.5 %collective-permute-start.5 = (bf16[256,256]{1,0:T(8,128)(2,1)S(1)}, bf16[256,256]{1,0:T(8,128)(2,1)S(1)}, u32[]{:S(2)}, u32[]{:S(2)}) collective-permute-start(bf16[256,256]{1,0:T(8,128)(2,1)S(1)} %collective-permute-done.4.refs_3_), channel_id=1, source_target_pairs={{0,1},{1,0},{2,3},{3,2},{4,5},{5,4},{6,7},{7,6},{8,9},{9,8},{10,11... | collective-permute-start | bytes 393224 | tf_op jit(solution)/shard_map/ppermute | solution.py:375
  15.1 1.6 %collective-permute-start.10 = (bf16[256,256]{1,0:T(8,128)(2,1)S(1)}, bf16[256,256]{1,0:T(8,128)(2,1)S(1)}, u32[]{:S(2)}, u32[]{:S(2)}) collective-permute-start(bf16[256,256]{1,0:T(8,128)(2,1)S(1)} %get-tuple-element.27), channel_id=1, source_target_pairs={{0,24},{1,25},{2,26},{3,27},{4,28},{5,29},{6,30},{7,31},{8,16},{9,... | collective-permute-start | bytes 393224 | tf_op jit(solution)/shard_map/ppermute | solution.py:375
  16.8 0.0 collective-permute-done.3.refs_2_
  16.8 1.6 %collective-permute-start.7 = (bf16[256,256]{1,0:T(8,128)(2,1)S(1)}, bf16[256,256]{1,0:T(8,128)(2,1)S(1)}, u32[]{:S(2)}, u32[]{:S(2)}) collective-permute-start(bf16[256,256]{1,0:T(8,128)(2,1)S(1)} %collective-permute-done.2.refs_1_), channel_id=1, source_target_pairs={{0,2},{1,3},{2,0},{3,1},{4,6},{5,7},{6,4},{7,5},{8,10},{9,11},{10,... | collective-permute-start | bytes 393224 | tf_op jit(solution)/shard_map/ppermute | solution.py:375
  18.3 1.2 %collective-permute-done.5.refs_4_ = bf16[256,256]{1,0:T(8,128)(2,1)S(1)} collective-permute-done((bf16[256,256]{1,0:T(8,128)(2,1)S(1)}, bf16[256,256]{1,0:T(8,128)(2,1)S(1)}, u32[]{:S(2)}, u32[]{:S(2)}) %collective-permute-start.5) | collective-permute-done | bytes 131104 | tf_op jit(solution)/shard_map/ppermute | solution.py:375
  19.6 1.8 %collective-permute-start.9 = (bf16[256,256]{1,0:T(8,128)(2,1)S(1)}, bf16[256,256]{1,0:T(8,128)(2,1)S(1)}, u32[]{:S(2)}, u32[]{:S(2)}) collective-permute-start(bf16[256,256]{1,0:T(8,128)(2,1)S(1)} %collective-permute-done.4.refs_3_), channel_id=1, source_target_pairs={{0,2},{1,3},{2,0},{3,1},{4,6},{5,7},{6,4},{7,5},{8,10},{9,11},{10,... | collective-permute-start | bytes 393224 | tf_op jit(solution)/shard_map/ppermute | solution.py:375
  21.4 0.0 collective-permute-done.1.refs_0_
  21.4 0.4 %shard_map.66 = (bf16[1,2,2,256,256]{4,3,2,1,0:T(8,128)(2,1)S(1)}, bf16[1,2,2,256,256]{4,3,2,1,0:T(8,128)(2,1)S(1)}, bf16[2,512,256]{2,1,0:T(8,128)(2,1)S(1)}) custom-call(bf16[2,256,256]{2,1,0:T(8,128)(2,1)S(1)} %get-tuple-element.18.mixers.coupling, bf16[2,256,256]{2,1,0:T(8,128)(2,1)S(1)} %collective-permute-done.1.refs_0_, ...), custom_call_target="tpu_custom_call" | custom-call | flops 4000000000 | bytes 1048576 | tf_op jit(solution)/shard_map/pallas_call | solution.py:353
  21.8 0.1 collective-permute-start.6
  21.9 0.2 collective-permute-done.7.refs_2_
  22.1 1.2 %collective-permute-start.8 = (bf16[256,256]{1,0:T(8,128)(2,1)S(1)}, bf16[256,256]{1,0:T(8,128)(2,1)S(1)}, u32[]{:S(2)}, u32[]{:S(2)}) collective-permute-start(bf16[256,256]{1,0:T(8,128)(2,1)S(1)} %collective-permute-done.7.refs_2_), channel_id=1, source_target_pairs={{0,1},{1,0},{2,3},{3,2},{4,5},{5,4},{6,7},{7,6},{8,9},{9,8},{10,11... | collective-permute-start | bytes 393224 | tf_op jit(solution)/shard_map/ppermute | solution.py:375
  23.2 0.0 collective-permute-done.theirs
  23.2 0.0 slice-done
  23.2 0.0 slice-done.1
  23.2 0.6 %shard_map.68.refs_8_ = f32[2,2048,128]{2,1,0:T(8,128)S(1)} custom-call(bf16[8,256,256]{2,1,0:T(8,128)(2,1)S(1)} %get-tuple-element.20.mine, bf16[8,256,256]{2,1,0:T(8,128)(2,1)S(1)} %collective-permute-done.theirs, bf16[2,512,256]{2,1,0:T(8,128)(2,1)S(1)} %get-tuple-element.26.refs_0_.refs_1_, f32[8,2048,128]{2,1,0:T(8,128)S(1)} %bitcast.12), custom_call_target="tpu_custom_call" | custom-call | flops 4000000000 | bytes 1048576 | tf_op jit(solution)/shard_map/pallas_call | solution.py:353
  23.9 1.2 %shard_map.67.refs_7_ = f32[4,2048,128]{2,1,0:T(8,128)S(1)} custom-call(bf16[4,256,256]{2,1,0:T(8,128)(2,1)S(1)} %get-tuple-element.19.own, bf16[8,256,256]{2,1,0:T(8,128)(2,1)S(1)} %get-tuple-element.20.mine, bf16[8,256,256]{2,1,0:T(8,128)(2,1)S(1)} %collective-permute-done.theirs, f32[8,2048,128]{2,1,0:T(8,128)S(1)} %bitcast.13), custom_call_target="tpu_custom_call" | custom-call | flops 4000000000 | bytes 1048576 | tf_op jit(solution)/shard_map/pallas_call | solution.py:353
  25.1 0.0 collective-permute-done.10.refs_5_
  25.1 0.0 collective-permute-done.9.refs_4_
  25.1 2.7 %collective-permute-done.8.refs_3_ = bf16[256,256]{1,0:T(8,128)(2,1)S(1)} collective-permute-done((bf16[256,256]{1,0:T(8,128)(2,1)S(1)}, bf16[256,256]{1,0:T(8,128)(2,1)S(1)}, u32[]{:S(2)}, u32[]{:S(2)}) %collective-permute-start.8) | collective-permute-done | bytes 131104 | tf_op jit(solution)/shard_map/ppermute | solution.py:375
  27.8 0.0 collective-permute-done.6.swapped
  27.8 3.8 %shard_map.69 = (f32[8,2048,128]{2,1,0:T(8,128)}, f32[4,2048,128]{2,1,0:T(8,128)S(1)}, f32[2,2048,128]{2,1,0:T(8,128)S(1)}) custom-call(bf16[4,256,256]{2,1,0:T(8,128)(2,1)S(1)} %get-tuple-element.19.own, bf16[8,256,256]{2,1,0:T(8,128)(2,1)S(1)} %get-tuple-element.20.mine, ...), custom_call_target="tpu_custom_call", output_to_operand_aliasing={{1}: (12, {}), {2}: (13, {})} | custom-call | flops 4000000000 | bytes 1048576 | tf_op jit(solution)/shard_map/pallas_call | solution.py:353
  (1 shorter events, 0.0 us)
Async XLA Ops:
  1.5 21.7 %slice-start = ((s8[8388608]{0:T(1024)(128)(4,1)}), s8[4194304]{0:T(1024)(128)(4,1)S(1)}, s32[]{:S(2)}) async-start(s8[8388608]{0:T(1024)(128)(4,1)} %bitcast.10), calls=%async_computation | async-start | bytes 8388608
  3.8 19.4 %collective-permute-start = (bf16[8,256,256]{2,1,0:T(8,128)(2,1)S(1)}, bf16[8,256,256]{2,1,0:T(8,128)(2,1)S(1)}, u32[]{:S(2)}, u32[]{:S(2)}) collective-permute-start(bf16[8,256,256]{2,1,0:T(8,128)(2,1)S(1)} %get-tuple-element.20.mine), channel_id=1, source_target_pairs={{0,8},{1,9},{2,10},{3,11},{4,12},{5,13},{6,14},{7,15},{8,0},{9,1},... | collective-permute-start | bytes 3145736 | tf_op jit(solution)/shard_map/ppermute | solution.py:375
  4.4 6.9 %collective-permute-start.2 = (bf16[256,256]{1,0:T(8,128)(2,1)S(1)}, bf16[256,256]{1,0:T(8,128)(2,1)S(1)}, u32[]{:S(2)}, u32[]{:S(2)}) collective-permute-start(bf16[256,256]{1,0:T(8,128)(2,1)S(1)} %get-tuple-element.22), channel_id=1, source_target_pairs={{0,16},{1,17},{2,18},{3,19},{4,20},{5,21},{6,22},{7,23},{8,24},{9,... | collective-permute-start | bytes 393224 | tf_op jit(solution)/shard_map/ppermute | solution.py:375
  6.9 6.7 %collective-permute-start.4 = (bf16[256,256]{1,0:T(8,128)(2,1)S(1)}, bf16[256,256]{1,0:T(8,128)(2,1)S(1)}, u32[]{:S(2)}, u32[]{:S(2)}) collective-permute-start(bf16[256,256]{1,0:T(8,128)(2,1)S(1)} %get-tuple-element.23), channel_id=1, source_target_pairs={{0,24},{1,25},{2,26},{3,27},{4,28},{5,29},{6,30},{7,31},{8,16},{9,... | collective-permute-start | bytes 393224 | tf_op jit(solution)/shard_map/ppermute | solution.py:375
  7.0 16.2 %slice-start.1 = ((s8[8388608]{0:T(1024)(128)(4,1)}), s8[4194304]{0:T(1024)(128)(4,1)S(1)}, s32[]{:S(2)}) async-start(s8[8388608]{0:T(1024)(128)(4,1)} %bitcast.10), calls=%async_computation.1 | async-start | bytes 8388608
  7.0 14.4 %collective-permute-start.1 = (bf16[2,256,256]{2,1,0:T(8,128)(2,1)S(1)}, bf16[2,256,256]{2,1,0:T(8,128)(2,1)S(1)}, u32[]{:S(2)}, u32[]{:S(2)}) collective-permute-start(bf16[2,256,256]{2,1,0:T(8,128)(2,1)S(1)} %get-tuple-element.21), channel_id=1, source_target_pairs={{0,16},{1,17},{2,18},{3,19},{4,20},{5,21},{6,22},{7,23},{8,24},{9,... | collective-permute-start | bytes 786440 | tf_op jit(solution)/shard_map/ppermute | solution.py:375
  11.3 5.5 %collective-permute-start.3 = (bf16[256,256]{1,0:T(8,128)(2,1)S(1)}, bf16[256,256]{1,0:T(8,128)(2,1)S(1)}, u32[]{:S(2)}, u32[]{:S(2)}) collective-permute-start(bf16[256,256]{1,0:T(8,128)(2,1)S(1)} %collective-permute-done.2.refs_1_), channel_id=1, source_target_pairs={{0,1},{1,0},{2,3},{3,2},{4,5},{5,4},{6,7},{7,6},{8,9},{9,8},{10,11... | collective-permute-start | bytes 393224 | tf_op jit(solution)/shard_map/ppermute | solution.py:375
  13.6 5.9 %collective-permute-start.5 = (bf16[256,256]{1,0:T(8,128)(2,1)S(1)}, bf16[256,256]{1,0:T(8,128)(2,1)S(1)}, u32[]{:S(2)}, u32[]{:S(2)}) collective-permute-start(bf16[256,256]{1,0:T(8,128)(2,1)S(1)} %collective-permute-done.4.refs_3_), channel_id=1, source_target_pairs={{0,1},{1,0},{2,3},{3,2},{4,5},{5,4},{6,7},{7,6},{8,9},{9,8},{10,11... | collective-permute-start | bytes 393224 | tf_op jit(solution)/shard_map/ppermute | solution.py:375
  15.1 9.9 %collective-permute-start.10 = (bf16[256,256]{1,0:T(8,128)(2,1)S(1)}, bf16[256,256]{1,0:T(8,128)(2,1)S(1)}, u32[]{:S(2)}, u32[]{:S(2)}) collective-permute-start(bf16[256,256]{1,0:T(8,128)(2,1)S(1)} %get-tuple-element.27), channel_id=1, source_target_pairs={{0,24},{1,25},{2,26},{3,27},{4,28},{5,29},{6,30},{7,31},{8,16},{9,... | collective-permute-start | bytes 393224 | tf_op jit(solution)/shard_map/ppermute | solution.py:375
  16.8 5.3 %collective-permute-start.7 = (bf16[256,256]{1,0:T(8,128)(2,1)S(1)}, bf16[256,256]{1,0:T(8,128)(2,1)S(1)}, u32[]{:S(2)}, u32[]{:S(2)}) collective-permute-start(bf16[256,256]{1,0:T(8,128)(2,1)S(1)} %collective-permute-done.2.refs_1_), channel_id=1, source_target_pairs={{0,2},{1,3},{2,0},{3,1},{4,6},{5,7},{6,4},{7,5},{8,10},{9,11},{10,... | collective-permute-start | bytes 393224 | tf_op jit(solution)/shard_map/ppermute | solution.py:375
  19.6 5.5 %collective-permute-start.9 = (bf16[256,256]{1,0:T(8,128)(2,1)S(1)}, bf16[256,256]{1,0:T(8,128)(2,1)S(1)}, u32[]{:S(2)}, u32[]{:S(2)}) collective-permute-start(bf16[256,256]{1,0:T(8,128)(2,1)S(1)} %collective-permute-done.4.refs_3_), channel_id=1, source_target_pairs={{0,2},{1,3},{2,0},{3,1},{4,6},{5,7},{6,4},{7,5},{8,10},{9,11},{10,... | collective-permute-start | bytes 393224 | tf_op jit(solution)/shard_map/ppermute | solution.py:375
  21.8 6.0 %collective-permute-start.6 = (bf16[1,2,2,256,256]{4,3,2,1,0:T(8,128)(2,1)S(1)}, bf16[1,2,2,256,256]{4,3,2,1,0:T(8,128)(2,1)S(1)}, u32[]{:S(2)}, u32[]{:S(2)}) collective-permute-start(bf16[1,2,2,256,256]{4,3,2,1,0:T(8,128)(2,1)S(1)} %get-tuple-element.25), channel_id=1, source_target_pairs={{0,8},{1,9},{2,10},{3,11},{4,12},{5,13},{6,14},{7,15},{8,0},{9,1},... | collective-permute-start | bytes 1572872 | tf_op jit(solution)/shard_map/ppermute | solution.py:375
  22.1 5.7 %collective-permute-start.8 = (bf16[256,256]{1,0:T(8,128)(2,1)S(1)}, bf16[256,256]{1,0:T(8,128)(2,1)S(1)}, u32[]{:S(2)}, u32[]{:S(2)}) collective-permute-start(bf16[256,256]{1,0:T(8,128)(2,1)S(1)} %collective-permute-done.7.refs_2_), channel_id=1, source_target_pairs={{0,1},{1,0},{2,3},{3,2},{4,5},{5,4},{6,7},{7,6},{8,9},{9,8},{10,11... | collective-permute-start | bytes 393224 | tf_op jit(solution)/shard_map/ppermute | solution.py:375
